TPU v7x, 32 devices: a whole 2x2x4 slice. The times are simulated.
32 devices in a mesh: wide: 16 (over z, x, core), narrow: 2 (over y).
Axes of the slice: x: 2, y: 2, z: 4, core: 2. Of those that a mesh axis runs over, the one named last changes fastest.
Arguments:
- design: float32 [192, 96, 384], P('wide', 'narrow'), may hold values from 0 to 1
- passive: int32 [192, 96, 384], P('wide', 'narrow'), may hold values 0 or 1
- displacement: float32 [3, 3, 64, 32, 128], P(None, None, 'wide', 'narrow'), may hold values from -6 to 6
- support: int32 [64, 32, 128], P('wide', 'narrow'), may hold values 0 or 1
- loading: int32 [64, 32, 128], P('wide', 'narrow'), may hold values 0 or 1
Outputs:
- residual: float32 [3, 3, 64, 32, 128], P(None, None, 'wide', 'narrow')
- compliance: float32 [3], replicated
- sensitivity: float32 [192, 96, 384], P('wide', 'narrow')
All inputs are finite; a program needn't handle non-finite values. No bound on the sum of `passive` or of `support` or of `loading` on one device may be relied on, other than what follows from the above.
Results may differ from a plain program's by a relative error of at most 0.0001.
Values sent between devices are 32-bit elements; how exact they have to be, the bound alone decides.
No kernel may reach another device: no remote copies, remote signals or barrier semaphores. Data moves between devices by JAX's collectives and lax.ppermute only.
A program may use at most 64 MiB of HBM per device.

v0:
```python
import math

import jax
import jax.numpy as jnp
import numpy as np
from jax import lax
from jax.sharding import PartitionSpec as P

RAD = 3


sharpness = 8.0
thresholds = (0.7, 0.5, 0.3)
stiff_floor = 0.001
load_force = 4.0
poisson = 0.3


def with_halo(shard, sides, width):
    for axis, dim in sides:
        count, length = (lax.axis_size(axis), shard.shape[dim])
        up = [(i, (i + 1) % count) for i in range(count - 1)]
        down = [(j, i) for i, j in up]
        last = lax.slice_in_dim(shard, length - width, length, axis=dim)
        initial = lax.slice_in_dim(shard, 0, width, axis=dim)
        before = lax.ppermute(last, axis, up)
        after = lax.ppermute(initial, axis, down)
        shard = jnp.concatenate([before, shard, after], axis=dim)
    return shard


def passed_along(block, axis, distance):
    devices = range(lax.axis_size(axis))
    route = [(i - distance, i) for i in devices if i - distance in devices]
    return lax.ppermute(block, axis, route)


def element_matrix():
    inv_root = 1.0 / np.sqrt(3.0)
    elastic_scale = 1.0 / ((1.0 + poisson) * (1.0 - 2.0 * poisson))
    elastic = np.zeros((6, 6))
    for row_i in range(3):
        for col_j in range(3):
            elastic[row_i, col_j] = poisson
        elastic[row_i, row_i] = 1.0 - poisson
    for row_i in range(3, 6):
        elastic[row_i, row_i] = 0.5 - poisson
    elastic = elastic * elastic_scale
    corner_signs = [
        (2 * (corner // 4) - 1, 2 * (corner // 2 % 2) - 1, 2 * (corner % 2) - 1)
        for corner in range(8)
    ]
    stiffness = np.zeros((24, 24))
    for gauss_a in (-inv_root, inv_root):
        for gauss_b in (-inv_root, inv_root):
            for gauss_c in (-inv_root, inv_root):
                gauss_point = (gauss_a, gauss_b, gauss_c)
                derivs = np.zeros((8, 3))
                for corner in range(8):
                    for along in range(3):
                        slope_value = corner_signs[corner][along] / 8.0
                        for second in range(3):
                            if second != along:
                                slope_value = slope_value * (
                                    1.0 + corner_signs[corner][second] * gauss_point[second]
                                )
                        derivs[corner, along] = 2.0 * slope_value
                strain = np.zeros((6, 24))
                for corner in range(8):
                    column = 3 * corner
                    strain[0, column] = derivs[corner, 0]
                    strain[1, column + 1] = derivs[corner, 1]
                    strain[2, column + 2] = derivs[corner, 2]
                    strain[3, column] = derivs[corner, 1]
                    strain[3, column + 1] = derivs[corner, 0]
                    strain[4, column + 1] = derivs[corner, 2]
                    strain[4, column + 2] = derivs[corner, 1]
                    strain[5, column] = derivs[corner, 2]
                    strain[5, column + 2] = derivs[corner, 0]
                stiffness = stiffness + strain.T @ elastic @ strain * 0.125
    return stiffness.astype(np.float32)


def blur_axis(padded, axis_dim, length):
    summed = float(1 - RAD + RAD) * lax.slice_in_dim(padded, 0, length, axis=axis_dim)
    for offset in range(1, 2 * RAD + 1):
        summed = summed + float(RAD + 1 - abs(offset - RAD)) * lax.slice_in_dim(
            padded, offset, offset + length, axis=axis_dim
        )
    return summed


def edge_weights(start_index, amount, extent):
    places = start_index + jnp.arange(amount, dtype=jnp.int32)
    summed = jnp.zeros((amount,), jnp.float32)
    for offset in range(-RAD, RAD + 1):
        inside = ((places + offset >= 0) & (places + offset < extent)).astype(jnp.float32)
        summed = summed + float(RAD + 1 - abs(offset)) * inside
    return summed


def smooth_field(source):
    rows_out, cols_out, depth_out = source.shape
    padded = with_halo(source, (("wide", 0),), RAD)
    rowwise = blur_axis(padded, 0, rows_out)
    padded_cols = with_halo(rowwise, (("narrow", 1),), RAD)
    colwise = blur_axis(padded_cols, 1, cols_out)
    deepened = jnp.pad(colwise, ((0, 0), (0, 0), (RAD, RAD)))
    return blur_axis(deepened, 2, depth_out)


def project(blurred, threshold):
    low_end = float(math.tanh(sharpness * threshold))
    denominator = low_end + float(math.tanh(sharpness * (1.0 - threshold)))
    steep_part = jnp.tanh(sharpness * (blurred - threshold))
    return (
        (low_end + steep_part) / denominator,
        sharpness * (1.0 - steep_part * steep_part) / denominator,
    )


def depth_averaging(fine_len, coarse_len):
    rows_index = jnp.arange(fine_len, dtype=jnp.int32)[:, None] // 3
    cols_index = jnp.arange(coarse_len, dtype=jnp.int32)[None, :]
    return (rows_index == cols_index).astype(jnp.float32)


def aggregate(fine_stiff, coarse_averaging, count_x, count_y):
    merged = jnp.dot(
        fine_stiff.reshape(-1, fine_stiff.shape[2]),
        coarse_averaging,
        precision=lax.Precision.HIGHEST,
    )
    merged = merged.reshape(count_x, 3, count_y, 3, coarse_averaging.shape[1])
    return jnp.sum(merged, axis=(1, 3)) / 27.0


def spread(coarse, coarse_averaging):
    count_x, count_y, count_z = coarse.shape
    deepened = jnp.dot(
        coarse.reshape(-1, count_z), coarse_averaging.T, precision=lax.Precision.HIGHEST
    )
    deepened = deepened.reshape(count_x, 1, count_y, 1, coarse_averaging.shape[0])
    return jnp.broadcast_to(deepened, (count_x, 3, count_y, 3, coarse_averaging.shape[0])).reshape(
        3 * count_x, 3 * count_y, coarse_averaging.shape[0]
    )


def element_contributions(nodal_values, moduli, count_x, count_y, count_z, operator_matrix):
    batch = nodal_values.shape[0]
    corners = []
    for corner in range(8):
        along_x, along_y, along_z = (corner // 4, corner // 2 % 2, corner % 2)
        corners.append(
            nodal_values[
                :,
                :,
                along_x : along_x + count_x,
                along_y : along_y + count_y,
                along_z : along_z + count_z,
            ]
        )
    stacked = jnp.stack(corners, axis=1).reshape(batch, 24, count_x, count_y, count_z)
    product = jnp.einsum(
        "ij,bjxyz->bixyz", operator_matrix, stacked, precision=lax.Precision.HIGHEST
    )
    strain_energy = jnp.sum(stacked * product, axis=1)
    return (strain_energy, moduli[:, None] * product)


def gather_global(external_loads, count_x, count_y, count_z):
    summed = jnp.zeros(
        (external_loads.shape[0], 3, count_x + 1, count_y + 1, count_z + 1), jnp.float32
    )
    for corner in range(8):
        along_x, along_y, along_z = (corner // 4, corner // 2 % 2, corner % 2)
        summed = summed.at[
            :,
            :,
            along_x : along_x + count_x,
            along_y : along_y + count_y,
            along_z : along_z + count_z,
        ].add(external_loads[:, 3 * corner : 3 * corner + 3])
    return summed


def local(design, passive, displacement, support, loading):
    rows_fine, cols_fine, depth_fine = design.shape
    count_x, count_y, count_z = support.shape
    solid_mask = 1.0 - passive.astype(jnp.float32)
    freedom = 1.0 - support.astype(jnp.float32)
    load_values = load_force * loading.astype(jnp.float32)
    start_x = lax.axis_index("wide") * rows_fine
    start_y = lax.axis_index("narrow") * cols_fine
    weights = (
        edge_weights(start_x, rows_fine, rows_fine * lax.axis_size("wide"))[:, None, None]
        * edge_weights(start_y, cols_fine, cols_fine * lax.axis_size("narrow"))[None, :, None]
        * edge_weights(0, depth_fine, depth_fine)[None, None, :]
    )
    blurred = smooth_field(design) / weights
    coarse_averaging = depth_averaging(depth_fine, count_z)
    densities = []
    slopes = []
    moduli = []
    for level_index in range(3):
        density, slope_term = project(blurred, thresholds[level_index])
        density = density * solid_mask
        densities.append(density)
        slopes.append(slope_term)
        moduli.append(
            aggregate(
                stiff_floor + (1.0 - stiff_floor) * density**3, coarse_averaging, count_x, count_y
            )
        )
    young_modulus = jnp.stack(moduli)
    masked_moves = displacement * freedom
    operator_matrix = jnp.asarray(element_matrix(), dtype=jnp.float32)
    flattened = masked_moves.reshape(9, count_x, count_y, count_z)
    upper_rows = passed_along(flattened[:, :1], "wide", -1)
    nodal_values = jnp.concatenate([flattened, upper_rows], axis=1)
    upper_cols = passed_along(nodal_values[:, :, :1], "narrow", -1)
    nodal_values = jnp.concatenate([nodal_values, upper_cols], axis=2)
    nodal_values = jnp.pad(nodal_values, ((0, 0), (0, 0), (0, 0), (0, 1))).reshape(
        3, 3, count_x + 1, count_y + 1, count_z + 1
    )
    strain_energy, external_loads = element_contributions(
        nodal_values, young_modulus, count_x, count_y, count_z, operator_matrix
    )
    summed = gather_global(external_loads, count_x, count_y, count_z)
    lower_cols = passed_along(summed[:, :, :, count_y : count_y + 1, :count_z], "narrow", 1)
    summed = summed[:, :, :, :count_y, :count_z].at[:, :, :, :1].add(lower_cols)
    lower_rows = passed_along(summed[:, :, count_x : count_x + 1], "wide", 1)
    global_gathered = summed[:, :, :count_x].at[:, :, :1].add(lower_rows)
    zeros_field = jnp.zeros_like(load_values)
    applied = jnp.stack([zeros_field, zeros_field, -load_values])
    residual = (applied[None] - global_gathered) * freedom
    partial_sums = jnp.sum(young_modulus * strain_energy, axis=(1, 2, 3))
    compliance = lax.psum(partial_sums, ("wide", "narrow"))
    gradient = jnp.zeros_like(design)
    for level_index in range(3):
        scaled = strain_energy[level_index] / compliance[level_index]
        gradient = (
            gradient
            - 3.0
            * (1.0 - stiff_floor)
            / 27.0
            * densities[level_index] ** 2
            * spread(scaled, coarse_averaging)
            * slopes[level_index]
            * solid_mask
        )
    sensitivity = smooth_field(gradient / weights)
    return (residual, compliance, sensitivity)


def solution(mesh):
    in_specs = (
        P("wide", "narrow", None),
        P("wide", "narrow", None),
        P(None, None, "wide", "narrow", None),
        P("wide", "narrow", None),
        P("wide", "narrow", None),
    )
    out_specs = (P(None, None, "wide", "narrow", None), P(), P("wide", "narrow", None))
    return jax.shard_map(local, mesh=mesh, in_specs=in_specs, out_specs=out_specs, check_vma=False)
```

profile of v0, /device:TPU:0, one launch (start us, length us, event | category | flops | bytes accessed | tf_op | source)
XLA Modules:
  0.0 189.8 jit_solution(4245754079001352607)
XLA Ops:
  0.6 1.1 fusion.164
  1.7 2.4 %collective-permute-start = (f32[3,48,384]{2,1,0:T(8,128)S(1)}, f32[3,48,384]{2,1,0:T(8,128)S(1)}, u32[]{:S(2)}, u32[]{:S(2)}) collective-permute-start(f32[3,48,384]{2,1,0:T(8,128)S(1)} %get-tuple-element.143), channel_id=1, source_target_pairs={{0,2},{2,4},{4,6},{6,8},{8,10},{10,12},{12,14},{14,16},{16,18},{18... | collective-permute-start | bytes 663560 | tf_op jit(solution)/shard_map/ppermute | solution.py:26
  4.1 1.3 collective-permute-start.1
  6.2 1.0 broadcast_multiply_fusion
  7.2 1.3 collective-permute-start.4
  8.7 4.4 %collective-permute-done.4 = f32[9,1,16,128]{3,2,1,0:T(8,128)S(1)} collective-permute-done((f32[9,1,16,128]{3,2,1,0:T(8,128)S(1)}, f32[9,1,16,128]{3,2,1,0:T(8,128)S(1)}, u32[]{:S(2)}, u32[]{:S(2)}) %collective-permute-start.4) | collective-permute-done | bytes 73760 | tf_op jit(solution)/shard_map/ppermute | solution.py:35
  13.1 1.3 collective-permute-start.5
  15.1 3.7 %collective-permute-done.5 = f32[9,5,1,128]{3,2,1,0:T(1,128)S(1)} collective-permute-done((f32[9,5,1,128]{3,2,1,0:T(1,128)S(1)}, f32[9,5,1,128]{3,2,1,0:T(1,128)S(1)}, u32[]{:S(2)}, u32[]{:S(2)}) %collective-permute-start.5) | collective-permute-done | bytes 23072 | tf_op jit(solution)/shard_map/ppermute | solution.py:35
  19.8 1.0 copy-done.4
  21.4 1.6 collective-permute-start.2
  23.0 1.3 collective-permute-start.3
  24.3 4.9 %fusion.1 = f32[3,4,16,128,24]{3,4,2,1,0:T(8,128)} fusion(f32[24,24,1,1,1]{1,0,4,3,2:T(8,128)S(1)} %copy-done.9, f32[3,24,4,16,128]{4,3,2,1,0:T(8,128)S(1)} %bitcast.78), kind=kOutput, calls=%fused_computation.3 | convolution fusion | flops 169869312 | bytes 4720896 | tf_op jit(solution)/shard_map/ij,bjxyz->bixyz/dot_general | solution.py:164
  30.4 2.4 %fusion.43 = (f32[12,48,384]{2,1,0:T(8,128)}, f32[12,48,384]{2,1,0:T(8,128)S(1)}) fusion(s32[12,48,384]{2,1,0:T(8,128)S(1)} %copy-done.2, f32[384]{0:T(512)S(1)} %convert_add_fusion, f32[12,48]{1,0:T(8,128)S(1)} %broadcast_multiply_fusion.1, f32[12,48,384]{2,1,0:T(8,128)S(1)} %fusion.19), kind=kLoop, calls=%fused_computation.95 | loop fusion | flops 5308416 | bytes 3542784 | tf_op jit(solution)/shard_map/add | solution.py:212
  32.8 1.9 fusion.51
  34.7 1.5 dot_general.31
  36.2 2.4 %dot_general.29 = f32[4,3,16,3,384]{4,3,2,1,0:T(4,128)} reshape(f32[12,48,384]{2,1,0:T(8,128)} %get-tuple-element.133) | data formatting | bytes 1769472 | tf_op jit(solution)/shard_map/dot_general | solution.py:129
  38.6 1.2 convolution_reduce_fusion
  39.8 2.5 %convolution_reduce_fusion.1 = f32[4,16,128]{2,1,0:T(8,128)} fusion(f32[4,3,16,3,384]{4,3,2,1,0:T(4,128)} %dot_general.29, s32[384]{0:T(512)S(1)} %add_select_fusion), kind=kOutput, calls=%fused_computation.42 | convolution fusion | flops 339853312 | bytes 919040 | tf_op jit(solution)/shard_map/dot_general | solution.py:129
  42.2 1.5 dot_general.27
  45.2 2.3 %fusion = (f32[3,4,16,128]{3,2,1,0:T(8,128)S(1)}, f32[3,24,4,16,128]{4,3,2,1,0:T(8,128)S(1)}) fusion(f32[3,24,4,16,128]{4,3,2,1,0:T(8,128)S(1)} %bitcast.79, f32[3,4,16,128,24]{3,4,2,1,0:T(8,128)} %fusion.1, f32[3,4,16,128]{3,2,1,0:T(8,128)S(1)} %pad_maximum_fusion.6), kind=kLoop, calls=%fused_computation.2 | loop fusion | flops 1744896 | bytes 7274496 | tf_op jit(solution)/shard_map/reduce_sum | solution.py:167
  47.6 1.3 copy-done
  49.9 43.2 %psum.7 = f32[3]{0:T(128)S(1)} all-reduce(f32[3]{0:T(128)S(1)} %multiply_reduce_fusion), channel_id=1, replica_groups=mesh['wide'=16,'narrow'=2] {'wide','narrow'}, use_global_device_ids=true, to_apply=%region_5.6 | all-reduce | flops 3 | bytes 24 | tf_op jit(solution)/shard_map/psum | solution.py:238
  93.7 1.0 fusion.106
  94.9 1.4 reshape.821
  96.3 1.0 fusion.108
  97.5 1.4 reshape.819
  98.9 0.9 fusion.110
  99.8 1.2 broadcast_in_dim.9
  101.1 2.5 %reshape.817 = f32[12,48,384]{2,1,0:T(8,128)} reshape(f32[4,3,16,3,384]{4,3,2,1,0:T(4,128)} %broadcast_in_dim.9) | data formatting | bytes 1769472 | tf_op jit(solution)/shard_map/reshape | solution.py:144
  103.5 12.1 %scatter-add.35 = f32[3,3,5,17,129]{4,3,2,1,0:T(8,128)S(1)} dynamic-update-slice(f32[3,3,5,17,129]{4,3,2,1,0:T(8,128)S(1)} %scatter-add.34, f32[3,3,4,16,128]{4,3,2,1,0:T(8,128)} %fusion.91, s32[]{:T(128)} %constant.422.clone.1, s32[]{:T(128)} %constant.422.clone.1, s32[]{:T(128)} %constant.422.clone.1, s32[]{:T(128)} %constant.422.clone.1, s32[]{:T(128)} %constant.426.clone.1) | dynamic-update-slice | bytes 589828 | tf_op jit(solution)/shard_map/scatter-add | solution.py:183
  116.5 2.5 %scatter-add.36 = f32[3,3,5,17,129]{4,3,2,1,0:T(8,128)S(1)} dynamic-update-slice(f32[3,3,5,17,129]{4,3,2,1,0:T(8,128)S(1)} %scatter-add.35, f32[3,3,4,16,128]{4,3,2,1,0:T(8,128)} %slice_add_fusion.6, s32[]{:T(128)} %constant.422.clone.1, s32[]{:T(128)} %constant.422.clone.1, s32[]{:T(128)} %constant.422.clone.1, s32[]{:T(128)} %constant.426.clone.1, s32[]{:T(128)} %constant.422.clone.1) | dynamic-update-slice | bytes 589828 | tf_op jit(solution)/shard_map/scatter-add | solution.py:183
  119.0 0.9 slice_add_fusion.5
  119.8 12.1 %scatter-add.39 = f32[3,3,5,17,129]{4,3,2,1,0:T(8,128)S(1)} dynamic-update-slice(f32[3,3,5,17,129]{4,3,2,1,0:T(8,128)S(1)} %scatter-add.36, f32[3,3,4,16,128]{4,3,2,1,0:T(8,128)} %slice_add_fusion.5, s32[]{:T(128)} %constant.422.clone.1, s32[]{:T(128)} %constant.422.clone.1, s32[]{:T(128)} %constant.422.clone.1, s32[]{:T(128)} %constant.426.clone.1, s32[]{:T(128)} %constant.426.clone.1) | dynamic-update-slice | bytes 589828 | tf_op jit(solution)/shard_map/scatter-add | solution.py:183
  132.0 0.9 slice_add_fusion.3
  132.9 12.1 %scatter-add.41 = f32[3,3,5,17,129]{4,3,2,1,0:T(8,128)S(1)} dynamic-update-slice(f32[3,3,5,17,129]{4,3,2,1,0:T(8,128)S(1)} %fusion.92, f32[3,3,4,16,128]{4,3,2,1,0:T(8,128)} %slice_add_fusion.3, s32[]{:T(128)} %constant.422.clone.1, s32[]{:T(128)} %constant.422.clone.1, s32[]{:T(128)} %constant.426.clone.1, s32[]{:T(128)} %constant.422.clone.1, s32[]{:T(128)} %constant.426.clone.1) | dynamic-update-slice | bytes 589828 | tf_op jit(solution)/shard_map/scatter-add | solution.py:183
  145.8 2.5 %scatter-add.44 = f32[3,3,5,17,129]{4,3,2,1,0:T(8,128)S(1)} dynamic-update-slice(f32[3,3,5,17,129]{4,3,2,1,0:T(8,128)S(1)} %scatter-add.41, f32[3,3,4,16,128]{4,3,2,1,0:T(8,128)} %slice_add_fusion.2, s32[]{:T(128)} %constant.422.clone.1, s32[]{:T(128)} %constant.422.clone.1, s32[]{:T(128)} %constant.426.clone.1, s32[]{:T(128)} %constant.426.clone.1, s32[]{:T(128)} %constant.422.clone.1) | dynamic-update-slice | bytes 589828 | tf_op jit(solution)/shard_map/scatter-add | solution.py:183
  148.3 0.9 slice_add_fusion.1
  149.2 12.1 %scatter-add.45 = f32[3,3,5,17,129]{4,3,2,1,0:T(8,128)S(1)} dynamic-update-slice(f32[3,3,5,17,129]{4,3,2,1,0:T(8,128)S(1)} %scatter-add.44, f32[3,3,4,16,128]{4,3,2,1,0:T(8,128)} %slice_add_fusion.1, s32[]{:T(128)} %constant.422.clone.1, s32[]{:T(128)} %constant.422.clone.1, s32[]{:T(128)} %constant.426.clone.1, s32[]{:T(128)} %constant.426.clone.1, s32[]{:T(128)} %constant.426.clone.1) | dynamic-update-slice | bytes 589828 | tf_op jit(solution)/shard_map/scatter-add | solution.py:183
  161.3 4.2 %collective-permute-start.6 = (f32[3,3,5,1,128]{4,3,2,1,0:T(1,128)S(1)}, f32[3,3,5,1,128]{4,3,2,1,0:T(1,128)S(1)}, u32[]{:S(2)}, u32[]{:S(2)}) collective-permute-start(f32[3,3,5,1,128]{4,3,2,1,0:T(1,128)S(1)} %slice.787), channel_id=1, source_target_pairs={{0,1},{2,3},{4,5},{6,7},{8,9},{10,11},{12,13},{14,15},{16,17},{18,... | collective-permute-start | bytes 69128 | tf_op jit(solution)/shard_map/ppermute | solution.py:35
  165.5 3.7 %multiply_divide_fusion = f32[12,48,384]{2,1,0:T(8,128)S(1)} fusion(f32[12,48,384]{2,1,0:T(8,128)} %reshape.817, f32[12,48,384]{2,1,0:T(8,128)} %reshape.819, f32[12,48,384]{2,1,0:T(8,128)} %reshape.821, f32[12,48,384]{2,1,0:T(8,128)} %copy-done.3, s32[12,48,384]{2,1,0:T(8,128)} %param.27, f32[384]{0:T(512)S(1)} %convert_add_fusion, ...), kind=kLoop, calls=%fused_computation.35 | loop fusion | flops 10174464 | bytes 5312256 | tf_op jit(solution)/shard_map/div | solution.py:252
  169.4 1.3 collective-permute-start.7
  170.7 4.0 %collective-permute-start.8 = (f32[3,48,384]{2,1,0:T(8,128)S(1)}, f32[3,48,384]{2,1,0:T(8,128)S(1)}, u32[]{:S(2)}, u32[]{:S(2)}) collective-permute-start(f32[3,48,384]{2,1,0:T(8,128)S(1)} %get-tuple-element.137), channel_id=1, source_target_pairs={{0,2},{2,4},{4,6},{6,8},{8,10},{10,12},{12,14},{14,16},{16,18},{18... | collective-permute-start | bytes 663560 | tf_op jit(solution)/shard_map/ppermute | solution.py:26
  174.8 1.3 collective-permute-start.9
  176.1 2.0 %collective-permute-done.9 = f32[3,48,384]{2,1,0:T(8,128)S(1)} collective-permute-done((f32[3,48,384]{2,1,0:T(8,128)S(1)}, f32[3,48,384]{2,1,0:T(8,128)S(1)}, u32[]{:S(2)}, u32[]{:S(2)}) %collective-permute-start.9) | collective-permute-done | bytes 221216 | tf_op jit(solution)/shard_map/ppermute | solution.py:27
  178.4 2.0 %collective-permute-start.10 = (f32[12,3,384]{2,1,0:T(4,128)S(1)}, f32[12,3,384]{2,1,0:T(4,128)S(1)}, u32[]{:S(2)}, u32[]{:S(2)}) collective-permute-start(f32[12,3,384]{2,1,0:T(4,128)S(1)} %get-tuple-element.135), channel_id=1, source_target_pairs={{0,1},{2,3},{4,5},{6,7},{8,9},{10,11},{12,13},{14,15},{16,17},{18,... | collective-permute-start | bytes 165896 | tf_op jit(solution)/shard_map/ppermute | solution.py:26
  180.4 1.3 collective-permute-start.11
  182.5 4.2 %collective-permute-done.11 = f32[12,3,384]{2,1,0:T(4,128)S(1)} collective-permute-done((f32[12,3,384]{2,1,0:T(4,128)S(1)}, f32[12,3,384]{2,1,0:T(4,128)S(1)}, u32[]{:S(2)}, u32[]{:S(2)}) %collective-permute-start.11) | collective-permute-done | bytes 55328 | tf_op jit(solution)/shard_map/ppermute | solution.py:27
  187.4 2.3 %fusion.75 = f32[12,48,384]{2,1,0:T(8,128)} fusion(f32[12,48,384]{2,1,0:T(8,128)S(1)} %fusion.6), kind=kLoop, calls=%fused_computation.127 | loop fusion | flops 2433024 | bytes 1769472 | tf_op jit(solution)/shard_map/add | solution.py:87
  (80 shorter events, 11.4 us)
Async XLA Ops:
  0.6 8.0 %copy-start.8 = (s32[4,16,128]{2,1,0:T(8,128)S(1)}, s32[4,16,128]{2,1,0:T(8,128)}, u32[]{:S(2)}) copy-start(s32[4,16,128]{2,1,0:T(8,128)} %param.30) | copy-start | bytes 98308
  1.7 18.1 %collective-permute-start = (f32[3,48,384]{2,1,0:T(8,128)S(1)}, f32[3,48,384]{2,1,0:T(8,128)S(1)}, u32[]{:S(2)}, u32[]{:S(2)}) collective-permute-start(f32[3,48,384]{2,1,0:T(8,128)S(1)} %get-tuple-element.143), channel_id=1, source_target_pairs={{0,2},{2,4},{4,6},{6,8},{8,10},{10,12},{12,14},{14,16},{16,18},{18... | collective-permute-start | bytes 663560 | tf_op jit(solution)/shard_map/ppermute | solution.py:26
  4.1 16.8 %collective-permute-start.1 = (f32[3,48,384]{2,1,0:T(8,128)S(1)}, f32[3,48,384]{2,1,0:T(8,128)S(1)}, u32[]{:S(2)}, u32[]{:S(2)}) collective-permute-start(f32[3,48,384]{2,1,0:T(8,128)S(1)} %get-tuple-element.144), channel_id=1, source_target_pairs={{2,0},{4,2},{6,4},{8,6},{10,8},{12,10},{14,12},{16,14},{18,16},{20... | collective-permute-start | bytes 663560 | tf_op jit(solution)/shard_map/ppermute | solution.py:27
  6.2 1.0 copy-start.6
  7.2 5.9 %collective-permute-start.4 = (f32[9,1,16,128]{3,2,1,0:T(8,128)S(1)}, f32[9,1,16,128]{3,2,1,0:T(8,128)S(1)}, u32[]{:S(2)}, u32[]{:S(2)}) collective-permute-start(f32[9,1,16,128]{3,2,1,0:T(8,128)S(1)} %slice.762), channel_id=1, source_target_pairs={{2,0},{4,2},{6,4},{8,6},{10,8},{12,10},{14,12},{16,14},{18,16},{20... | collective-permute-start | bytes 221192 | tf_op jit(solution)/shard_map/ppermute | solution.py:35
  13.1 5.7 %collective-permute-start.5 = (f32[9,5,1,128]{3,2,1,0:T(1,128)S(1)}, f32[9,5,1,128]{3,2,1,0:T(1,128)S(1)}, u32[]{:S(2)}, u32[]{:S(2)}) collective-permute-start(f32[9,5,1,128]{3,2,1,0:T(1,128)S(1)} %pad_maximum_fusion.7), channel_id=1, source_target_pairs={{1,0},{3,2},{5,4},{7,6},{9,8},{11,10},{13,12},{15,14},{17,16},{19,... | collective-permute-start | bytes 69128 | tf_op jit(solution)/shard_map/ppermute | solution.py:35
  19.6 1.2 copy-start.4
  21.0 3.3 %copy-start.9 = (f32[24,24,1,1,1]{1,0,4,3,2:T(8,128)S(1)}, f32[24,24,1,1,1]{1,0,4,3,2:T(8,128)}, u32[]{:S(2)}) copy-start(f32[24,24,1,1,1]{1,0,4,3,2:T(8,128)} %constant.464) | copy-start | bytes 6916
  21.4 7.8 %collective-permute-start.2 = (f32[12,3,384]{2,1,0:T(4,128)S(1)}, f32[12,3,384]{2,1,0:T(4,128)S(1)}, u32[]{:S(2)}, u32[]{:S(2)}) collective-permute-start(f32[12,3,384]{2,1,0:T(4,128)S(1)} %get-tuple-element.139), channel_id=1, source_target_pairs={{0,1},{2,3},{4,5},{6,7},{8,9},{10,11},{12,13},{14,15},{16,17},{18,... | collective-permute-start | bytes 165896 | tf_op jit(solution)/shard_map/ppermute | solution.py:26
  23.0 6.2 %collective-permute-start.3 = (f32[12,3,384]{2,1,0:T(4,128)S(1)}, f32[12,3,384]{2,1,0:T(4,128)S(1)}, u32[]{:S(2)}, u32[]{:S(2)}) collective-permute-start(f32[12,3,384]{2,1,0:T(4,128)S(1)} %get-tuple-element.140), channel_id=1, source_target_pairs={{1,0},{3,2},{5,4},{7,6},{9,8},{11,10},{13,12},{15,14},{17,16},{19,... | collective-permute-start | bytes 165896 | tf_op jit(solution)/shard_map/ppermute | solution.py:27
  29.2 1.2 copy-start.2
  32.8 1.9 copy-start.3
  47.5 1.4 copy-start
  93.0 3.2 %copy-start.10 = (f32[3]{0:T(128)}, f32[3]{0:T(128)S(1)}, u32[]{:S(2)}) copy-start(f32[3]{0:T(128)S(1)} %psum.7) | copy-start | bytes 40
  101.0 14.6 %copy-start.1 = (f32[3,24,4,16,128]{4,3,2,1,0:T(8,128)S(1)}, f32[3,24,4,16,128]{4,3,2,1,0:T(8,128)}, u32[]{:S(2)}) copy-start(f32[3,24,4,16,128]{4,3,2,1,0:T(8,128)} %copy-done) | copy-start | bytes 7077892
  161.3 7.9 %collective-permute-start.6 = (f32[3,3,5,1,128]{4,3,2,1,0:T(1,128)S(1)}, f32[3,3,5,1,128]{4,3,2,1,0:T(1,128)S(1)}, u32[]{:S(2)}, u32[]{:S(2)}) collective-permute-start(f32[3,3,5,1,128]{4,3,2,1,0:T(1,128)S(1)} %slice.787), channel_id=1, source_target_pairs={{0,1},{2,3},{4,5},{6,7},{8,9},{10,11},{12,13},{14,15},{16,17},{18,... | collective-permute-start | bytes 69128 | tf_op jit(solution)/shard_map/ppermute | solution.py:35
  169.4 6.7 %collective-permute-start.7 = (f32[3,3,1,16,128]{4,3,2,1,0:T(8,128)S(1)}, f32[3,3,1,16,128]{4,3,2,1,0:T(8,128)S(1)}, u32[]{:S(2)}, u32[]{:S(2)}) collective-permute-start(f32[3,3,1,16,128]{4,3,2,1,0:T(8,128)S(1)} %slice.790), channel_id=1, source_target_pairs={{0,2},{2,4},{4,6},{6,8},{8,10},{10,12},{12,14},{14,16},{16,18},{18... | collective-permute-start | bytes 221192 | tf_op jit(solution)/shard_map/ppermute | solution.py:35
  170.7 5.4 %collective-permute-start.8 = (f32[3,48,384]{2,1,0:T(8,128)S(1)}, f32[3,48,384]{2,1,0:T(8,128)S(1)}, u32[]{:S(2)}, u32[]{:S(2)}) collective-permute-start(f32[3,48,384]{2,1,0:T(8,128)S(1)} %get-tuple-element.137), channel_id=1, source_target_pairs={{0,2},{2,4},{4,6},{6,8},{8,10},{10,12},{12,14},{14,16},{16,18},{18... | collective-permute-start | bytes 663560 | tf_op jit(solution)/shard_map/ppermute | solution.py:26
  174.8 3.4 %collective-permute-start.9 = (f32[3,48,384]{2,1,0:T(8,128)S(1)}, f32[3,48,384]{2,1,0:T(8,128)S(1)}, u32[]{:S(2)}, u32[]{:S(2)}) collective-permute-start(f32[3,48,384]{2,1,0:T(8,128)S(1)} %get-tuple-element.138), channel_id=1, source_target_pairs={{2,0},{4,2},{6,4},{8,6},{10,8},{12,10},{14,12},{16,14},{18,16},{20... | collective-permute-start | bytes 663560 | tf_op jit(solution)/shard_map/ppermute | solution.py:27
  176.1 5.6 %copy-start.5 = (f32[3,4,16,128]{3,2,1,0:T(8,128)S(1)}, f32[3,4,16,128]{3,2,1,0:T(8,128)}, u32[]{:S(2)}) copy-start(f32[3,4,16,128]{3,2,1,0:T(8,128)} %stack.41) | copy-start | bytes 294916
  176.1 5.6 %copy-start.7 = (f32[4,16,128]{2,1,0:T(8,128)S(1)}, f32[4,16,128]{2,1,0:T(8,128)}, u32[]{:S(2)}) copy-start(f32[4,16,128]{2,1,0:T(8,128)} %copy-done.6) | copy-start | bytes 98308
  178.4 4.1 %collective-permute-start.10 = (f32[12,3,384]{2,1,0:T(4,128)S(1)}, f32[12,3,384]{2,1,0:T(4,128)S(1)}, u32[]{:S(2)}, u32[]{:S(2)}) collective-permute-start(f32[12,3,384]{2,1,0:T(4,128)S(1)} %get-tuple-element.135), channel_id=1, source_target_pairs={{0,1},{2,3},{4,5},{6,7},{8,9},{10,11},{12,13},{14,15},{16,17},{18,... | collective-permute-start | bytes 165896 | tf_op jit(solution)/shard_map/ppermute | solution.py:26
  180.4 6.2 %collective-permute-start.11 = (f32[12,3,384]{2,1,0:T(4,128)S(1)}, f32[12,3,384]{2,1,0:T(4,128)S(1)}, u32[]{:S(2)}, u32[]{:S(2)}) collective-permute-start(f32[12,3,384]{2,1,0:T(4,128)S(1)} %get-tuple-element.136), channel_id=1, source_target_pairs={{1,0},{3,2},{5,4},{7,6},{9,8},{11,10},{13,12},{15,14},{17,16},{19,... | collective-permute-start | bytes 165896 | tf_op jit(solution)/shard_map/ppermute | solution.py:27
where the time goes:
time: 193 us; the launch traced here: 190 us
  local copies, waits for them, and re-layouts  72.1 us (37%)
  blocking collectives  43.2 us (22%)
  other arithmetic  23.6 us (12%)
  starting transfers between devices  23.3 us (12%)
  waiting for transfers between devices  14.4 us (7%)
  matrix products  12 us (6%)
    scatter-add x7, local copies, waits for them, and re-layouts, gather_global(): summed = summed.at[:, :, along_x:along_x + count_x, along_y:along_y + cou...  53.5 us
    psum x1, blocking collectives, local(): compliance = lax.psum(partial_sums, ('wide', 'narrow'))  43.2 us
    ppermute x4, starting transfers between devices, with_halo(): before = lax.ppermute(last, axis, up)  10 us
    ppermute x4, waiting for transfers between devices, passed_along(): return lax.ppermute(block, axis, route)  8.16 us
    ppermute x4, starting transfers between devices, passed_along(): return lax.ppermute(block, axis, route)  8.05 us
    ppermute x4, waiting for transfers between devices, with_halo(): after = lax.ppermute(initial, axis, down)  6.22 us
    dot_general x3, local copies, waits for them, and re-layouts, aggregate(): jnp.dot(fine_stiff.reshape(-1, fine_stiff.shape[2]), coarse_averaging, pr...  5.39 us
    reshape x3, local copies, waits for them, and re-layouts, spread(): jnp.broadcast_to(deepened, (count_x, 3, count_y, 3, coarse_averaging.shap...  5.24 us
  transfers between devices with their start and end apart: 12, of which 5 were waited for; matrix products, arithmetic and copies ran while one was open for 7% of the time, Pallas kernels for 0%

commit v1 on v0

v1 whole, which is shorter than its diff:
```python
import functools
import math

import jax
import jax.numpy as jnp
import numpy as np
from jax import lax
from jax.experimental import pallas as pl
from jax.experimental.pallas import tpu as pltpu
from jax.sharding import PartitionSpec as P

RAD = 3
sharpness = 8.0
thresholds = (0.7, 0.5, 0.3)
stiff_floor = 0.001
load_force = 4.0
poisson = 0.3
LANES = 128
REACH = 2 * RAD


def element_matrix():
    inv_root = 1.0 / np.sqrt(3.0)
    elastic_scale = 1.0 / ((1.0 + poisson) * (1.0 - 2.0 * poisson))
    elastic = np.zeros((6, 6))
    for row_i in range(3):
        for col_j in range(3):
            elastic[row_i, col_j] = poisson
        elastic[row_i, row_i] = 1.0 - poisson
    for row_i in range(3, 6):
        elastic[row_i, row_i] = 0.5 - poisson
    elastic = elastic * elastic_scale
    corner_signs = [
        (2 * (corner // 4) - 1, 2 * (corner // 2 % 2) - 1, 2 * (corner % 2) - 1)
        for corner in range(8)
    ]
    stiffness = np.zeros((24, 24))
    for gauss_a in (-inv_root, inv_root):
        for gauss_b in (-inv_root, inv_root):
            for gauss_c in (-inv_root, inv_root):
                gauss_point = (gauss_a, gauss_b, gauss_c)
                derivs = np.zeros((8, 3))
                for corner in range(8):
                    for along in range(3):
                        slope_value = corner_signs[corner][along] / 8.0
                        for second in range(3):
                            if second != along:
                                slope_value = slope_value * (
                                    1.0 + corner_signs[corner][second] * gauss_point[second]
                                )
                        derivs[corner, along] = 2.0 * slope_value
                strain = np.zeros((6, 24))
                for corner in range(8):
                    column = 3 * corner
                    strain[0, column] = derivs[corner, 0]
                    strain[1, column + 1] = derivs[corner, 1]
                    strain[2, column + 2] = derivs[corner, 2]
                    strain[3, column] = derivs[corner, 1]
                    strain[3, column + 1] = derivs[corner, 0]
                    strain[4, column + 1] = derivs[corner, 2]
                    strain[4, column + 2] = derivs[corner, 1]
                    strain[5, column] = derivs[corner, 2]
                    strain[5, column + 2] = derivs[corner, 0]
                stiffness = stiffness + strain.T @ elastic @ strain * 0.125
    return stiffness


def parity_operator():
    signs = np.ones((8, 8))
    for mode in range(8):
        for corner in range(8):
            for bit in range(3):
                if (mode >> bit) & 1:
                    signs[mode, corner] *= 2 * ((corner >> bit) & 1) - 1
    full = np.kron(signs, np.eye(3))
    coupled = full @ element_matrix() @ full.T / 64.0
    coupled[np.abs(coupled) < 1e-9] = 0.0
    return coupled


COUPLED = parity_operator()
LOW_END = tuple(math.tanh(sharpness * eta) for eta in thresholds)
DENOM = tuple(
    math.tanh(sharpness * eta) + math.tanh(sharpness * (1.0 - eta)) for eta in thresholds
)


def tent_rows(rows):
    for step in (1, 2, 1, 2):
        rows = [rows[i] + rows[i + step] for i in range(len(rows) - step)]
    return rows


def tent_sublanes(block, amount):
    size = block.shape[0]
    for step in (1, 2, 1, 2):
        block = block + pltpu.roll(block, size - step, 0)
    return block[:amount]


def lanes_up(parts, step, lane):
    rolled = [pltpu.roll(part, LANES - step, 1) for part in parts]
    rolled.append(jnp.zeros_like(parts[0]))
    return [
        jnp.where(lane < LANES - step, rolled[g], rolled[g + 1]) for g in range(len(parts))
    ]


def lanes_down(parts, step, lane):
    rolled = [jnp.zeros_like(parts[0])] + [pltpu.roll(part, step, 1) for part in parts]
    return [jnp.where(lane >= step, rolled[g + 1], rolled[g]) for g in range(len(parts))]


def tent_lanes(parts):
    lane = lax.broadcasted_iota(jnp.int32, parts[0].shape, 1)
    total = [4.0 * part for part in parts]
    for step in range(1, RAD + 1):
        ups, downs = lanes_up(parts, step, lane), lanes_down(parts, step, lane)
        if step == RAD:
            total = [t + (u + d) for t, u, d in zip(total, ups, downs)]
        else:
            total = [
                t + float(RAD + 1 - step) * (u + d) for t, u, d in zip(total, ups, downs)
            ]
    return total


def tent_weight(place, extent):
    total = jnp.zeros(place.shape, jnp.float32)
    for offset in range(-RAD, RAD + 1):
        inside = (place + offset >= 0) & (place + offset < extent)
        total = total + jnp.where(inside, float(RAD + 1 - abs(offset)), 0.0)
    return total


def halves(block):
    high = block.astype(jnp.bfloat16)
    low = (block - high.astype(jnp.float32)).astype(jnp.bfloat16)
    return jnp.concatenate([high, low], axis=1)


def lane_groups(depth):
    return [slice(g * LANES, (g + 1) * LANES) for g in range(depth // LANES)]


def modes_of(nodes, row, lane):
    fields = [[[None] * 3 for _ in range(2)] for _ in range(2)]
    for comp in range(3):
        value = nodes(comp, row)
        size = value.shape[0]
        ahead = jnp.where(lane < LANES - 1, pltpu.roll(value, LANES - 1, 1), 0.0)
        for mz, part in enumerate((value + ahead, ahead - value)):
            beside = pltpu.roll(part, size - 1, 0)
            fields[0][mz][comp] = part + beside
            fields[1][mz][comp] = beside - part
    return fields


def element_modes(low, high):
    modes = []
    for mx in range(2):
        for my in range(2):
            for mz in range(2):
                modes.append([
                    (h + l) if mx == 0 else (h - l)
                    for l, h in zip(low[my][mz], high[my][mz])
                ])
    return modes


def coupled_forces(modes):
    forces = [[None] * 3 for _ in range(8)]
    for mode in range(8):
        for comp in range(3):
            row = COUPLED[3 * mode + comp]
            groups = {}
            for place in np.nonzero(row)[0]:
                groups.setdefault(round(float(row[place]), 12), []).append(int(place))
            total = None
            for factor, places in groups.items():
                summed = modes[places[0] // 3][places[0] % 3]
                for place in places[1:]:
                    summed = summed + modes[place // 3][place % 3]
                term = factor * summed
                total = term if total is None else total + term
            forces[mode][comp] = total
    return forces


def pack_kernel(merged, n_narrow, design, passive, disp, support, up_ref, down_ref, *sides):
    rows, cols, depth = design.shape
    cx, cy, cz = support.shape
    groups = lane_groups(3 * cz)
    n = lax.axis_index("narrow")
    moved = lambda r, c, x: disp[r, c, x] * (1.0 - support[x].astype(jnp.float32))
    for k in range(RAD):
        up_ref[pl.ds(k * cols, cols), :] = design[rows - RAD + k]
        down_ref[pl.ds(k * cols, cols), :] = design[k]
    for r in range(3):
        for c in range(3):
            down_ref[pl.ds(RAD * cols + r * cy, cy), groups[c]] = moved(r, c, 0)

    def edge(high, low, kind):
        if kind == "merged":
            return jnp.where(n == 0, high, low)
        return high if kind == "high" else low

    kinds = ("merged",) if merged else ("high", "low")
    for index, kind in enumerate(kinds):
        side, side_up, side_down = sides[3 * index : 3 * index + 3]
        for k in range(rows):
            piece = edge(design[k, cols - REACH :, :], design[k, :REACH, :], kind)
            side[pl.ds(k * REACH, REACH), :] = piece
            if k < RAD:
                side_down[pl.ds(k * REACH, REACH), :] = piece
            if k >= rows - RAD:
                side_up[pl.ds((k - rows + RAD) * REACH, REACH), :] = piece
            mask = edge(passive[k, cols - RAD :, :], passive[k, :RAD, :], kind)
            side[pl.ds(rows * REACH + k * RAD, RAD), :] = 1.0 - mask.astype(jnp.float32)
        base = rows * (REACH + RAD)
        for r in range(3):
            for c in range(3):
                for x in range(cx):
                    value = moved(r, c, x)
                    piece = edge(value[cy - 2 :], value[:2], kind)
                    side[pl.ds(base + (r * cx + x) * 2, 2), groups[c]] = piece
                    if x == 0:
                        side_down[pl.ds(RAD * REACH + 2 * r, 2), groups[c]] = piece
        used = base + 6 * cx
        if side.shape[0] > used:
            side[used:, :] = jnp.zeros((side.shape[0] - used, depth), jnp.float32)
        used = RAD * REACH
        if side_up.shape[0] > used:
            side_up[used:, :] = jnp.zeros((side_up.shape[0] - used, depth), jnp.float32)
        used = RAD * REACH + 6
        if side_down.shape[0] > used:
            side_down[used:, :] = jnp.zeros((side_down.shape[0] - used, depth), jnp.float32)


def project_kernel(
    n_wide, n_narrow, design, passive, disp, support, from_low, from_high,
    side_b, side_a, up_b, up_a, down_b, down_a,
    gg_ref, nodes_ref, energy_ref, moduli_ref, part_ref,
    blurred, mask_ref, cubes, packed, agg,
):
    rows, cols, depth = design.shape
    cx, cy, cz = support.shape
    groups = lane_groups(depth)
    n = lax.axis_index("narrow")
    w = lax.axis_index("wide")
    valid_b = jnp.where(n > 0, 1.0, 0.0)
    valid_a = jnp.where(n < n_narrow - 1, 1.0, 0.0)
    ext = mask_ref.shape[1]

    nodes_ref[...] = jnp.zeros_like(nodes_ref)
    base = rows * (REACH + RAD)
    for r in range(3):
        for c in range(3):
            lanes = groups[c]
            for x in range(cx):
                free = 1.0 - support[x].astype(jnp.float32)
                nodes_ref[r, c, x, 1 : cy + 1, :] = disp[r, c, x] * free
                at = base + (r * cx + x) * 2
                nodes_ref[r, c, x, 0:1, :] = side_b[at + 1 : at + 2, lanes] * valid_b
                nodes_ref[r, c, x, cy + 1 : cy + 3, :] = side_a[at : at + 2, lanes] * valid_a
            at = RAD * cols + r * cy
            nodes_ref[r, c, cx, 1 : cy + 1, :] = from_high[at : at + cy, lanes]
            at = RAD * REACH + 2 * r
            nodes_ref[r, c, cx, 0:1, :] = down_b[at + 1 : at + 2, lanes] * valid_b
            nodes_ref[r, c, cx, cy + 1 : cy + 3, :] = down_a[at : at + 2, lanes] * valid_a

    lane = lax.broadcasted_iota(jnp.int32, nodes_ref.shape[3:], 1)
    for r in range(3):
        low = modes_of(lambda c, x: nodes_ref[r, c, x], 0, lane)
        for x in range(cx):
            high = modes_of(lambda c, x: nodes_ref[r, c, x], x + 1, lane)
            modes = element_modes(low, high)
            forces = coupled_forces(modes)
            total = None
            for mode in range(8):
                for comp in range(3):
                    if forces[mode][comp] is not None:
                        term = modes[mode][comp] * forces[mode][comp]
                        total = term if total is None else total + term
            energy_ref[r * cx + x] = total
            low = high

    for start in range(0, cols, 8):
        for lanes in groups:
            column = [from_low[k * cols + start : k * cols + start + 8, lanes] for k in range(RAD)]
            column += [design[k, start : start + 8, lanes] for k in range(rows)]
            column += [from_high[k * cols + start : k * cols + start + 8, lanes] for k in range(RAD)]
            for k, value in enumerate(tent_rows(column)):
                blurred[k, REACH + start : REACH + start + 8, lanes] = value
    for at, side, up, down, valid in (
        (0, side_b, up_b, down_b, valid_b),
        (REACH + cols, side_a, up_a, down_a, valid_a),
    ):
        for lanes in groups:
            pick = lambda ref, k: ref[k * REACH : (k + 1) * REACH, lanes] * valid
            column = [pick(up, k) for k in range(RAD)]
            column += [pick(side, k) for k in range(rows)]
            column += [pick(down, k) for k in range(RAD)]
            for k, value in enumerate(tent_rows(column)):
                blurred[k, at : at + REACH, lanes] = value
    tail = blurred.shape[1] - cols - 2 * REACH
    if tail:
        blurred[:, cols + 2 * REACH :, :] = jnp.zeros((rows, tail, depth), jnp.float32)

    for k in range(rows):
        mask_ref[k, RAD : RAD + cols, :] = 1.0 - passive[k].astype(jnp.float32)
        at = rows * REACH + k * RAD
        mask_ref[k, 0:RAD, :] = side_b[at : at + RAD, :]
        mask_ref[k, RAD + cols : 2 * RAD + cols, :] = side_a[at : at + RAD, :]
        mask_ref[k, 2 * RAD + cols :, :] = jnp.zeros((ext - 2 * RAD - cols, depth), jnp.float32)

    place_y = n * cols - RAD + lax.broadcasted_iota(jnp.int32, (ext, LANES), 0)
    extent_y = n_narrow * cols
    inside = (place_y >= 0) & (place_y < extent_y)
    weight_y = tent_weight(place_y, extent_y)
    recip_y = jnp.where(inside, 1.0 / jnp.maximum(weight_y, 1.0), 0.0)
    recip_z = []
    for g in range(len(groups)):
        place_z = g * LANES + lax.broadcasted_iota(jnp.int32, (ext, LANES), 1)
        recip_z.append(1.0 / tent_weight(place_z, depth))

    def coarse_row(x, carry):
        for sub in range(3):
            k = 3 * x + sub
            parts = [tent_sublanes(blurred[k, :, lanes], ext) for lanes in groups]
            parts = tent_lanes(parts)
            place_x = w * rows + k + jnp.zeros((8, LANES), jnp.int32)
            recip_x = (1.0 / tent_weight(place_x, n_wide * rows))[0:1]
            recip_xy = recip_y * recip_x
            for g, lanes in enumerate(groups):
                recip = recip_xy * recip_z[g]
                scaled = (sharpness * recip) * parts[g]
                mask = mask_ref[k, :, lanes]
                for r in range(3):
                    steep = jnp.tanh(scaled - sharpness * thresholds[r])
                    dense = (steep + LOW_END[r]) * mask
                    square = dense * dense
                    cube = square * dense
                    gg_ref[r, k, :, lanes] = square * (1.0 - steep * steep) * recip
                    at = r * cx + x
                    if sub == 0:
                        cubes[at, g] = cube
                    else:
                        cubes[at, g] = cubes[at, g] + cube
        return carry

    lax.fori_loop(0, cx, coarse_row, 0)

    padded = moduli_ref.shape[1]
    reach = cy + 2
    row_id = lax.broadcasted_iota(jnp.int32, (LANES, LANES), 0)
    col_id = lax.broadcasted_iota(jnp.int32, (LANES, LANES), 1)
    total = None
    packed[...] = jnp.zeros_like(packed)
    for g in range(len(groups)):
        for at in range(3 * cx):
            summed = cubes[at, g, pl.ds(0, reach, stride=3), :]
            summed = summed + cubes[at, g, pl.ds(1, reach, stride=3), :]
            summed = summed + cubes[at, g, pl.ds(2, reach, stride=3), :]
            packed[at * padded : at * padded + reach, :] = summed
        gather = ((g * LANES + row_id) // 3 == col_id).astype(jnp.float32).astype(jnp.bfloat16)
        term = jnp.dot(
            halves(packed[...]),
            jnp.concatenate([gather, gather], axis=0),
            preferred_element_type=jnp.float32,
        )
        total = term if total is None else total + term
    agg[...] = total
    sub_id = lax.broadcasted_iota(jnp.int32, (padded, LANES), 0)
    outside = jnp.where(n > 0, -1, 0)
    own = ((sub_id >= 1) & (sub_id <= cy)).astype(jnp.float32)
    part_ref[...] = jnp.zeros_like(part_ref)
    for r in range(3):
        partial = None
        for x in range(cx):
            at = r * cx + x
            value = agg[at * padded : (at + 1) * padded, :]
            value = stiff_floor + ((1.0 - stiff_floor) / 27.0 / DENOM[r] ** 3) * value
            value = jnp.where((sub_id > outside) & (sub_id < reach), value, 0.0)
            moduli_ref[at] = value
            term = value * energy_ref[at]
            partial = term if partial is None else partial + term
        part_ref[r : r + 1, :] = jnp.sum(partial * own, axis=0, keepdims=True)


def force_kernel(
    gg, nodes_ref, energy, moduli, support, loading,
    h_ref, up_ref, down_ref, residual_ref, spread_ref, packed,
):
    _, rows, ext, depth = gg.shape
    cx, cy, cz = support.shape
    padded = moduli.shape[1]
    reach = cy + 2
    groups = lane_groups(depth)

    row_id = lax.broadcasted_iota(jnp.int32, (LANES, LANES), 0)
    col_id = lax.broadcasted_iota(jnp.int32, (LANES, LANES), 1)
    for at in range(3 * cx):
        packed[at * padded : (at + 1) * padded, :] = energy[at]
    split = halves(packed[...])
    for g in range(len(groups)):
        copies = (row_id == (g * LANES + col_id) // 3).astype(jnp.float32).astype(jnp.bfloat16)
        fine = jnp.dot(
            split, jnp.concatenate([copies, copies], axis=0), preferred_element_type=jnp.float32
        )
        for at in range(3 * cx):
            value = fine[at * padded : at * padded + reach]
            for sub in range(3):
                spread_ref[at, g, pl.ds(sub, reach, stride=3), :] = value
            if 3 * reach < ext:
                spread_ref[at, g, 3 * reach :, :] = jnp.zeros((ext - 3 * reach, LANES), jnp.float32)

    for r in range(3):
        def fine_rows(x, carry):
            for sub in range(3):
                for g, lanes in enumerate(groups):
                    k = 3 * x + sub
                    h_ref[r, k, :, lanes] = gg[r, k, :, lanes] * spread_ref[r * cx + x, g]
            return carry

        lax.fori_loop(0, cx, fine_rows, 0)
        for k in range(RAD):
            at = (r * RAD + k) * ext
            up_ref[at : at + ext, :] = h_ref[r, rows - RAD + k]
            down_ref[at : at + ext, :] = h_ref[r, k]

    lane = lax.broadcasted_iota(jnp.int32, nodes_ref.shape[3:], 1)
    for r in range(3):
        nodes = lambda c, x: nodes_ref[r, c, x]
        low = modes_of(nodes, 0, lane)
        above = None
        for x in range(cx + 1):
            sums = [[[None] * 3 for _ in range(2)] for _ in range(2)]
            below, above_next = above, None
            if x < cx:
                high = modes_of(nodes, x + 1, lane)
                forces = coupled_forces(element_modes(low, high))
                low = high
                modulus = moduli[r * cx + x]
                scaled = [
                    [None if f is None else modulus * f for f in mode] for mode in forces
                ]
                above_next = [[[None] * 3 for _ in range(2)] for _ in range(2)]
                for my in range(2):
                    for mz in range(2):
                        for comp in range(3):
                            even = scaled[2 * my + mz][comp]
                            odd = scaled[4 + 2 * my + mz][comp]
                            if even is None:
                                sums[my][mz][comp] = -odd
                                above_next[my][mz][comp] = odd
                            else:
                                sums[my][mz][comp] = even - odd
                                above_next[my][mz][comp] = even + odd
            for comp in range(3):
                along = [None, None]
                for mz in range(2):
                    pair = []
                    for my in range(2):
                        value = sums[my][mz][comp]
                        if below is not None:
                            other = below[my][mz][comp]
                            value = other if value is None else value + other
                        pair.append(value)
                    along[mz] = (pair[0] - pair[1]) + pltpu.roll(pair[0] + pair[1], 1, 0)
                total = (along[0] - along[1]) + jnp.where(
                    lane >= 1, pltpu.roll(along[0] + along[1], 1, 1), 0.0
                )
                total = total[1 : cy + 1]
                if x < cx:
                    free = 1.0 - support[x].astype(jnp.float32)
                    if comp == 2:
                        total = total + load_force * loading[x].astype(jnp.float32)
                    residual_ref[r, comp, x] = -total * free
                else:
                    at = 3 * RAD * ext + r * cy
                    up_ref[at : at + cy, groups[comp]] = total
            above = above_next


def blur_kernel(
    h_ref, low_ref, high_ref, residual_in, support, fields_ref, residual_ref, summed
):
    _, rows, ext, depth = h_ref.shape
    cx, cy, cz = support.shape
    cols = fields_ref.shape[2]
    groups = lane_groups(depth)
    residual_ref[...] = residual_in[...]
    free = 1.0 - support[0].astype(jnp.float32)
    for r in range(3):
        at = 3 * RAD * ext + r * cy
        for comp in range(3):
            residual_ref[r, comp, 0] = (
                residual_in[r, comp, 0] - low_ref[at : at + cy, groups[comp]] * free
            )
    for r in range(3):
        def first_dim(s, carry):
            start = pl.multiple_of(8 * s, 8)
            for lanes in groups:
                column = [
                    low_ref[pl.ds((r * RAD + k) * ext + start, 8), lanes] for k in range(RAD)
                ]
                column += [h_ref[r, k, pl.ds(start, 8), lanes] for k in range(rows)]
                column += [
                    high_ref[pl.ds((r * RAD + k) * ext + start, 8), lanes] for k in range(RAD)
                ]
                for k, value in enumerate(tent_rows(column)):
                    summed[k, pl.ds(start, 8), lanes] = value
            return carry

        lax.fori_loop(0, ext // 8, first_dim, 0)

        def other_dims(k, carry):
            parts = [tent_sublanes(summed[k, :, lanes], cols) for lanes in groups]
            for lanes, part in zip(groups, tent_lanes(parts)):
                fields_ref[r, k, :, lanes] = part
            return carry

        lax.fori_loop(0, rows, other_dims, 0)


def call(kernel, shapes, scratch, flops, args, name):
    vmem = pl.BlockSpec(memory_space=pltpu.VMEM)
    return pl.pallas_call(
        kernel,
        out_shape=[jax.ShapeDtypeStruct(s, jnp.float32) for s in shapes],
        in_specs=[vmem] * len(args),
        out_specs=[vmem] * len(shapes),
        scratch_shapes=[pltpu.VMEM(s, jnp.float32) for s in scratch],
        compiler_params=pltpu.CompilerParams(vmem_limit_bytes=48 * 1024 * 1024),
        cost_estimate=pl.CostEstimate(flops=flops, bytes_accessed=1000000, transcendentals=0),
        name=name,
    )(*args)


def ceil8(amount):
    return -(-amount // 8) * 8


def all_sum(value, n_wide, n_narrow):
    total = n_wide * n_narrow
    axes = ("wide", "narrow")
    if total & (total - 1):
        return lax.psum(value, axes)
    step = 1
    while step < total:
        value = value + lax.ppermute(value, axes, [(i, i ^ step) for i in range(total)])
        step *= 2
    return value


def local(n_wide, n_narrow, design, passive, displacement, support, loading):
    rows, cols, depth = design.shape
    cx, cy, cz = support.shape
    merged = n_narrow == 2
    axes = ("wide", "narrow")
    ext = ceil8(cols + 2 * RAD)
    padded = ceil8(cy + 3)

    def route(dx, dy):
        pairs = []
        for i in range(n_wide):
            for j in range(n_narrow):
                if 0 <= i + dx < n_wide and 0 <= j + dy < n_narrow:
                    pairs.append((i * n_narrow + j, (i + dx) * n_narrow + j + dy))
        return pairs

    def side_route(dx, index):
        if merged:
            return route(dx, 1) + route(dx, -1)
        return route(dx, 1 if index == 0 else -1)

    sides = 1 if merged else 2
    side_shapes = [
        (ceil8(rows * (REACH + RAD) + 6 * cx), depth),
        (ceil8(RAD * REACH), depth),
        (ceil8(RAD * REACH + 6), depth),
    ]
    packs = call(
        functools.partial(pack_kernel, merged, n_narrow),
        [(RAD * cols, depth), (RAD * cols + 3 * cy, depth)] + side_shapes * sides,
        [], 200000, (design, passive, displacement, support), "pack",
    )
    send = lambda block, pairs: lax.ppermute(block, axes, pairs)
    from_low = send(packs[0], route(1, 0))
    from_high = send(packs[1], route(-1, 0))
    got = []
    for index in range(sides):
        side, side_up, side_down = packs[2 + 3 * index : 5 + 3 * index]
        got.append((
            send(side, side_route(0, index)),
            send(side_up, side_route(1, index)),
            send(side_down, side_route(-1, index)),
        ))
    before, after = got[0], got[-1]
    gg, nodes, energy, moduli, part = call(
        functools.partial(project_kernel, n_wide, n_narrow),
        [
            (3, rows, ext, depth), (3, 3, cx + 1, padded, cz), (3 * cx, padded, cz),
            (3 * cx, padded, cz), (8, LANES),
        ],
        [
            (rows, ceil8(cols + 2 * REACH), depth), (rows, ext, depth),
            (3 * cx, depth // LANES, ext, LANES), (3 * cx * padded, LANES),
            (3 * cx * padded, LANES),
        ],
        20000000,
        (
            design, passive, displacement, support, from_low, from_high,
            before[0], after[0], before[1], after[1], before[2], after[2],
        ),
        "project",
    )
    summed = all_sum(part, n_wide, n_narrow)
    h, up, down, residual = call(
        force_kernel,
        [
            (3, rows, ext, depth), (3 * RAD * ext + 3 * cy, depth), (3 * RAD * ext, depth),
            displacement.shape,
        ],
        [(3 * cx, depth // LANES, ext, LANES), (3 * cx * padded, LANES)],
        10000000, (gg, nodes, energy, moduli, support, loading), "force",
    )
    low = send(up, route(1, 0))
    high = send(down, route(-1, 0))
    fields, residual = call(
        blur_kernel,
        [(3, rows, cols, depth), displacement.shape],
        [(rows, ext, depth)],
        10000000, (h, low, high, residual, support), "blur",
    )
    compliance = jnp.sum(summed[:3], axis=1)
    sensitivity = None
    for r in range(3):
        factor = 3.0 * (1.0 - stiff_floor) / 27.0 * sharpness / DENOM[r] ** 3
        term = (-factor / compliance[r]) * fields[r]
        sensitivity = term if sensitivity is None else sensitivity + term
    return residual, compliance, sensitivity


def solution(mesh):
    in_specs = (
        P("wide", "narrow", None),
        P("wide", "narrow", None),
        P(None, None, "wide", "narrow", None),
        P("wide", "narrow", None),
        P("wide", "narrow", None),
    )
    out_specs = (P(None, None, "wide", "narrow", None), P(), P("wide", "narrow", None))
    body = functools.partial(local, mesh.shape["wide"], mesh.shape["narrow"])
    return jax.shard_map(body, mesh=mesh, in_specs=in_specs, out_specs=out_specs, check_vma=False)
```

time: 193 us -> 79.1 us (0.41); the launches traced: 190 us -> 78.5 us
  local copies, waits for them, and re-layouts: 72.1 us -> 6.28 us
  blocking collectives: 43.2 us -> 0 us
  other arithmetic: 23.6 us -> 1.19 us
  Pallas kernels: 0 us -> 20.6 us
  matrix products: 12 us -> 0 us
  starting transfers between devices: 23.3 us -> 32.2 us
    scatter-add x8 -> x0, local copies, waits for them, and re-layouts: 53.6 us -> none  [the longest x7 53.5 us: gather_global(): summed = summed.at[:, :, along_x:along_x + count_x, along_y:along_y + cou...]
    psum x1 -> x0, blocking collectives: 43.2 us -> none  [local(): compliance = lax.psum(partial_sums, ('wide', 'narrow'))]
    pallas_call x0 -> x4, Pallas kernels: none -> 20.6 us  [call(): pl.pallas_call(kernel, out_shape=[jax.ShapeDtypeStruct(s, jnp.float32) fo...]
    add x17 -> x6, other arithmetic: 13.9 us -> 1.07 us  [the longest x1 1.06 us: local(): sensitivity = term if sensitivity is None else sensitivity + term]
    dot_general x7 -> x0, matrix products: 12 us -> none  [the longest x1 4.87 us: element_contributions(): jnp.einsum('ij,bjxyz->bixyz', operator_matrix, stacked, precision=lax.Pre...]
    ppermute x12, starting transfers between devices: 23.3 us -> 32.2 us  [the longest x7 16.4 us: local(): send = lambda block, pairs: lax.ppermute(block, axes, pairs)]
    dot_general x3 -> x0, local copies, waits for them, and re-layouts: 5.39 us -> none  [aggregate(): jnp.dot(fine_stiff.reshape(-1, fine_stiff.shape[2]), coarse_averaging, pr...]
    reshape x3 -> x0, local copies, waits for them, and re-layouts: 5.24 us -> none  [spread(): jnp.broadcast_to(deepened, (count_x, 3, count_y, 3, coarse_averaging.shap...]
  transfers between devices with their start and end apart: 12 -> 12, of which waited for: 5 -> 7; matrix products, arithmetic and copies ran while one was open for 7% -> 1% of each run, Pallas kernels for 0% -> 0%
where the time goes in v1:
time: 79.1 us; the launch traced here: 78.5 us
  starting transfers between devices  32.2 us (41%)
  Pallas kernels  20.6 us (26%)
  waiting for transfers between devices  15.4 us (19%)
  local copies, waits for them, and re-layouts  6.28 us (8%)
  between operations  2.78 us (4%)
  other arithmetic  1.19 us (2%)
    pallas_call x4, Pallas kernels, call(): pl.pallas_call(kernel, out_shape=[jax.ShapeDtypeStruct(s, jnp.float32) fo...  20.6 us
    ppermute x7, starting transfers between devices, local(): send = lambda block, pairs: lax.ppermute(block, axes, pairs)  16.4 us
    ppermute x5, starting transfers between devices, all_sum(): lax.ppermute(value, axes, [(i, i ^ step) for i in range(total)])  15.8 us
    ppermute x5, waiting for transfers between devices, all_sum(): lax.ppermute(value, axes, [(i, i ^ step) for i in range(total)])  11.4 us
    unnamed x16, local copies, waits for them, and re-layouts  5.68 us
    ppermute x7, waiting for transfers between devices, local(): send = lambda block, pairs: lax.ppermute(block, axes, pairs)  3.99 us
  transfers between devices with their start and end apart: 12, of which 7 were waited for; matrix products, arithmetic and copies ran while one was open for 1% of the time, Pallas kernels for 0%

profile of v1, /device:TPU:0, one launch (start us, length us, event | category | flops | bytes accessed | tf_op | source)
XLA Modules:
  0.0 78.5 jit_solution(4464465740338771538)
XLA Ops:
  0.6 0.0 copy-start
  0.6 1.2 %copy-done = f32[12,48,384]{2,1,0:T(8,128)S(1)} copy-done((f32[12,48,384]{2,1,0:T(8,128)S(1)}, f32[12,48,384]{2,1,0:T(8,128)}, u32[]{:S(2)}) %copy-start) | copy-done | bytes 884760
  1.8 0.0 copy-start.1
  1.8 1.2 %copy-done.1 = s32[12,48,384]{2,1,0:T(8,128)S(1)} copy-done((s32[12,48,384]{2,1,0:T(8,128)S(1)}, s32[12,48,384]{2,1,0:T(8,128)}, u32[]{:S(2)}) %copy-start.1) | copy-done | bytes 884760
  3.0 0.0 copy-start.3
  3.0 1.0 %copy-done.3 = f32[3,3,4,16,128]{4,3,2,1,0:T(8,128)S(1)} copy-done((f32[3,3,4,16,128]{4,3,2,1,0:T(8,128)S(1)}, f32[3,3,4,16,128]{4,3,2,1,0:T(8,128)}, u32[]{:S(2)}) %copy-start.3) | copy-done | bytes 294936
  3.9 0.0 copy-start.4
  3.9 0.8 copy-done.4
  4.7 0.0 copy-start.5
  4.7 0.0 copy-start.6
  4.7 0.1 pack.1
  4.8 1.3 %collective-permute-start.1 = (f32[192,384]{1,0:T(8,128)S(1)}, f32[192,384]{1,0:T(8,128)S(1)}, u32[]{:S(2)}, u32[]{:S(2)}) collective-permute-start(f32[192,384]{1,0:T(8,128)S(1)} %get-tuple-element.20), channel_id=1, source_target_pairs={{2,0},{3,1},{4,2},{5,3},{6,4},{7,5},{8,6},{9,7},{10,8},{11,9},{12,... | collective-permute-start | bytes 884744 | tf_op jit(solution)/shard_map/ppermute | solution.py:589
  6.1 3.0 %collective-permute-start = (f32[144,384]{1,0:T(8,128)S(1)}, f32[144,384]{1,0:T(8,128)S(1)}, u32[]{:S(2)}, u32[]{:S(2)}) collective-permute-start(f32[144,384]{1,0:T(8,128)S(1)} %get-tuple-element.19), channel_id=1, source_target_pairs={{0,2},{1,3},{2,4},{3,5},{4,6},{5,7},{6,8},{7,9},{8,10},{9,11},{10,... | collective-permute-start | bytes 663560 | tf_op jit(solution)/shard_map/ppermute | solution.py:589
  9.2 3.1 %collective-permute-start.2 = (f32[136,384]{1,0:T(8,128)S(1)}, f32[136,384]{1,0:T(8,128)S(1)}, u32[]{:S(2)}, u32[]{:S(2)}) collective-permute-start(f32[136,384]{1,0:T(8,128)S(1)} %get-tuple-element.21), channel_id=1, source_target_pairs={{0,1},{2,3},{4,5},{6,7},{8,9},{10,11},{12,13},{14,15},{16,17},{18,... | collective-permute-start | bytes 626696 | tf_op jit(solution)/shard_map/ppermute | solution.py:589
  12.2 2.8 %collective-permute-start.3 = (f32[24,384]{1,0:T(8,128)S(1)}, f32[24,384]{1,0:T(8,128)S(1)}, u32[]{:S(2)}, u32[]{:S(2)}) collective-permute-start(f32[24,384]{1,0:T(8,128)S(1)} %get-tuple-element.22), channel_id=1, source_target_pairs={{0,3},{2,5},{4,7},{6,9},{8,11},{10,13},{12,15},{14,17},{16,19},{18... | collective-permute-start | bytes 110600 | tf_op jit(solution)/shard_map/ppermute | solution.py:589
  15.1 1.3 %collective-permute-start.4 = (f32[24,384]{1,0:T(8,128)S(1)}, f32[24,384]{1,0:T(8,128)S(1)}, u32[]{:S(2)}, u32[]{:S(2)}) collective-permute-start(f32[24,384]{1,0:T(8,128)S(1)} %get-tuple-element.23), channel_id=1, source_target_pairs={{2,1},{4,3},{6,5},{8,7},{10,9},{12,11},{14,13},{16,15},{18,17},{20... | collective-permute-start | bytes 110600 | tf_op jit(solution)/shard_map/ppermute | solution.py:589
  16.4 1.8 %collective-permute-done.3.up_b.up_a = f32[24,384]{1,0:T(8,128)S(1)} collective-permute-done((f32[24,384]{1,0:T(8,128)S(1)}, f32[24,384]{1,0:T(8,128)S(1)}, u32[]{:S(2)}, u32[]{:S(2)}) %collective-permute-start.3) | collective-permute-done | bytes 36896 | tf_op jit(solution)/shard_map/ppermute | solution.py:589
  18.2 2.2 %collective-permute-done.4.down_b.down_a = f32[24,384]{1,0:T(8,128)S(1)} collective-permute-done((f32[24,384]{1,0:T(8,128)S(1)}, f32[24,384]{1,0:T(8,128)S(1)}, u32[]{:S(2)}, u32[]{:S(2)}) %collective-permute-start.4) | collective-permute-done | bytes 36896 | tf_op jit(solution)/shard_map/ppermute | solution.py:589
  20.3 0.0 collective-permute-done.2.side_b.side_a
  20.3 0.0 collective-permute-done.from_low
  20.3 0.0 collective-permute-done.1.from_high
  20.4 5.9 %project.1 = (f32[3,12,56,384]{3,2,1,0:T(8,128)}, f32[3,3,5,24,128]{4,3,2,1,0:T(8,128)S(1)}, f32[12,24,128]{2,1,0:T(8,128)S(1)}, f32[12,24,128]{2,1,0:T(8,128)S(1)}, f32[8,128]{1,0:T(8,128)S(1)}) custom-call(f32[12,48,384]{2,1,0:T(8,128)S(1)} %copy-done, s32[12,48,384]{2,1,0:T(8,128)S(1)} %copy-done.1, f32[3,3,4,16,128]{4,3,2,1,0:T(8,128)S(1)} %copy-done.3, ...), custom_call_target="tpu_custom_call" | custom-call | flops 20000000 | bytes 1000000 | tf_op jit(solution)/shard_map/project/pallas_call | solution.py:529
  26.3 0.0 copy-done.5
  26.3 0.0 copy-done.6
  26.3 4.1 %force.1 = (f32[3,12,56,384]{3,2,1,0:T(8,128)S(1)}, f32[552,384]{1,0:T(8,128)S(1)}, f32[504,384]{1,0:T(8,128)S(1)}, f32[3,3,4,16,128]{4,3,2,1,0:T(8,128)S(1)}) custom-call(f32[3,12,56,384]{3,2,1,0:T(8,128)} %get-tuple-element.24.gg, f32[3,3,5,24,128]{4,3,2,1,0:T(8,128)S(1)} %get-tuple-element.25.nodes_ref, f32[12,24,128]{2,1,0:T(8,128)S(1)} %get-tuple-element.26.energy, ...), custom_call_target="tpu_custom_call" | custom-call | flops 10000000 | bytes 1000000 | tf_op jit(solution)/shard_map/force/pallas_call | solution.py:529
  30.4 0.0 copy-start.2
  30.4 1.6 %copy-done.2 = f32[3,12,56,384]{3,2,1,0:T(8,128)} copy-done((f32[3,12,56,384]{3,2,1,0:T(8,128)}, f32[3,12,56,384]{3,2,1,0:T(8,128)S(1)}, u32[]{:S(2)}) %copy-start.2) | copy-done | bytes 3096600
  32.0 3.6 %collective-permute-start.5 = (f32[552,384]{1,0:T(8,128)S(1)}, f32[552,384]{1,0:T(8,128)S(1)}, u32[]{:S(2)}, u32[]{:S(2)}) collective-permute-start(f32[552,384]{1,0:T(8,128)S(1)} %get-tuple-element.29), channel_id=1, source_target_pairs={{0,2},{1,3},{2,4},{3,5},{4,6},{5,7},{6,8},{7,9},{8,10},{9,11},{10,... | collective-permute-start | bytes 2543624 | tf_op jit(solution)/shard_map/ppermute | solution.py:589
  35.6 1.3 %collective-permute-start.6 = (f32[504,384]{1,0:T(8,128)S(1)}, f32[504,384]{1,0:T(8,128)S(1)}, u32[]{:S(2)}, u32[]{:S(2)}) collective-permute-start(f32[504,384]{1,0:T(8,128)S(1)} %get-tuple-element.30), channel_id=1, source_target_pairs={{2,0},{3,1},{4,2},{5,3},{6,4},{7,5},{8,6},{9,7},{10,8},{11,9},{12,... | collective-permute-start | bytes 2322440 | tf_op jit(solution)/shard_map/ppermute | solution.py:589
  36.9 1.4 %collective-permute-start.7 = (f32[8,128]{1,0:T(8,128)S(1)}, f32[8,128]{1,0:T(8,128)S(1)}, u32[]{:S(2)}, u32[]{:S(2)}) collective-permute-start(f32[8,128]{1,0:T(8,128)S(1)} %get-tuple-element.33), channel_id=1, source_target_pairs={{0,1},{1,0},{2,3},{3,2},{4,5},{5,4},{6,7},{7,6},{8,9},{9,8},{10,11... | collective-permute-start | bytes 12296 | tf_op jit(solution)/shard_map/ppermute | solution.py:552
  38.3 2.3 %collective-permute-done.7 = f32[8,128]{1,0:T(8,128)S(1)} collective-permute-done((f32[8,128]{1,0:T(8,128)S(1)}, f32[8,128]{1,0:T(8,128)S(1)}, u32[]{:S(2)}, u32[]{:S(2)}) %collective-permute-start.7) | collective-permute-done | bytes 4128 | tf_op jit(solution)/shard_map/ppermute | solution.py:552
  40.6 0.2 collective-permute-start.8
  40.8 1.0 %collective-permute-done.8 = f32[8,128]{1,0:T(8,128)S(1)} collective-permute-done((f32[8,128]{1,0:T(8,128)S(1)}, f32[8,128]{1,0:T(8,128)S(1)}, u32[]{:S(2)}, u32[]{:S(2)}) %collective-permute-start.8) | collective-permute-done | bytes 4128 | tf_op jit(solution)/shard_map/ppermute | solution.py:552
  41.8 3.2 %collective-permute-start.9 = (f32[8,128]{1,0:T(8,128)S(1)}, f32[8,128]{1,0:T(8,128)S(1)}, u32[]{:S(2)}, u32[]{:S(2)}) collective-permute-start(f32[8,128]{1,0:T(8,128)S(1)} %add.26), channel_id=1, source_target_pairs={{0,4},{1,5},{2,6},{3,7},{4,0},{5,1},{6,2},{7,3},{8,12},{9,13},{10,... | collective-permute-start | bytes 12296 | tf_op jit(solution)/shard_map/ppermute | solution.py:552
  44.9 5.0 %collective-permute-done.9 = f32[8,128]{1,0:T(8,128)S(1)} collective-permute-done((f32[8,128]{1,0:T(8,128)S(1)}, f32[8,128]{1,0:T(8,128)S(1)}, u32[]{:S(2)}, u32[]{:S(2)}) %collective-permute-start.9) | collective-permute-done | bytes 4128 | tf_op jit(solution)/shard_map/ppermute | solution.py:552
  50.0 8.0 %collective-permute-start.10 = (f32[8,128]{1,0:T(8,128)S(1)}, f32[8,128]{1,0:T(8,128)S(1)}, u32[]{:S(2)}, u32[]{:S(2)}) collective-permute-start(f32[8,128]{1,0:T(8,128)S(1)} %add.27), channel_id=1, source_target_pairs={{0,8},{1,9},{2,10},{3,11},{4,12},{5,13},{6,14},{7,15},{8,0},{9,1},... | collective-permute-start | bytes 12296 | tf_op jit(solution)/shard_map/ppermute | solution.py:552
  58.0 1.6 %collective-permute-done.10 = f32[8,128]{1,0:T(8,128)S(1)} collective-permute-done((f32[8,128]{1,0:T(8,128)S(1)}, f32[8,128]{1,0:T(8,128)S(1)}, u32[]{:S(2)}, u32[]{:S(2)}) %collective-permute-start.10) | collective-permute-done | bytes 4128 | tf_op jit(solution)/shard_map/ppermute | solution.py:552
  59.6 3.0 %collective-permute-start.11 = (f32[8,128]{1,0:T(8,128)S(1)}, f32[8,128]{1,0:T(8,128)S(1)}, u32[]{:S(2)}, u32[]{:S(2)}) collective-permute-start(f32[8,128]{1,0:T(8,128)S(1)} %add.28), channel_id=1, source_target_pairs={{0,16},{1,17},{2,18},{3,19},{4,20},{5,21},{6,22},{7,23},{8,24},{9,... | collective-permute-start | bytes 12296 | tf_op jit(solution)/shard_map/ppermute | solution.py:552
  62.6 1.6 %collective-permute-done.11 = f32[8,128]{1,0:T(8,128)S(1)} collective-permute-done((f32[8,128]{1,0:T(8,128)S(1)}, f32[8,128]{1,0:T(8,128)S(1)}, u32[]{:S(2)}, u32[]{:S(2)}) %collective-permute-start.11) | collective-permute-done | bytes 4128 | tf_op jit(solution)/shard_map/ppermute | solution.py:552
  64.2 0.1 slice_reduce_fusion
  64.3 0.0 copy-start.7
  64.3 0.6 fusion
  67.0 0.0 collective-permute-done.6.high_ref
  67.0 0.0 collective-permute-done.5.low_ref
  67.0 10.5 %blur.1 = (f32[3,12,48,384]{3,2,1,0:T(8,128)S(1)}, f32[3,3,4,16,128]{4,3,2,1,0:T(8,128)}) custom-call(f32[3,12,56,384]{3,2,1,0:T(8,128)} %copy-done.2, f32[552,384]{1,0:T(8,128)S(1)} %collective-permute-done.5.low_ref, f32[504,384]{1,0:T(8,128)S(1)} %collective-permute-done.6.high_ref, f32[3,3,4,16,128]{4,3,2,1,0:T(8,128)S(1)} %get-tuple-element.31.residual_in, ...), custom_call_target="tpu_custom_call" | custom-call | flops 10000000 | bytes 1000000 | tf_op jit(solution)/shard_map/blur/pallas_call | solution.py:529
  77.4 1.1 %add_bitcast_fusion = f32[12,48,384]{2,1,0:T(8,128)} fusion(f32[3,12,48,384]{3,2,1,0:T(8,128)S(1)} %get-tuple-element.34, f32[]{:T(128)} %bitcast.2, f32[]{:T(128)} %bitcast.1, f32[]{:T(128)} %bitcast), kind=kLoop, calls=%fused_computation | loop fusion | flops 1105920 | bytes 3538956 | tf_op jit(solution)/shard_map/add | solution.py:642
  78.5 0.0 copy-done.7
  (5 shorter events, 0.0 us)
Async XLA Ops:
  0.6 1.2 %copy-start = (f32[12,48,384]{2,1,0:T(8,128)S(1)}, f32[12,48,384]{2,1,0:T(8,128)}, u32[]{:S(2)}) copy-start(f32[12,48,384]{2,1,0:T(8,128)} %design.3) | copy-start | bytes 2654212
  1.8 1.2 %copy-start.1 = (s32[12,48,384]{2,1,0:T(8,128)S(1)}, s32[12,48,384]{2,1,0:T(8,128)}, u32[]{:S(2)}) copy-start(s32[12,48,384]{2,1,0:T(8,128)} %passive.3) | copy-start | bytes 2654212
  3.0 1.0 %copy-start.3 = (f32[3,3,4,16,128]{4,3,2,1,0:T(8,128)S(1)}, f32[3,3,4,16,128]{4,3,2,1,0:T(8,128)}, u32[]{:S(2)}) copy-start(f32[3,3,4,16,128]{4,3,2,1,0:T(8,128)} %disp.3) | copy-start | bytes 884740
  3.9 0.8 copy-start.4
  4.7 21.6 %copy-start.5 = (s32[4,16,128]{2,1,0:T(8,128)S(1)}, s32[4,16,128]{2,1,0:T(8,128)}, u32[]{:S(2)}) copy-start(s32[4,16,128]{2,1,0:T(8,128)} %support.7) | copy-start | bytes 98308
  4.7 21.6 %copy-start.6 = (s32[4,16,128]{2,1,0:T(8,128)S(1)}, s32[4,16,128]{2,1,0:T(8,128)}, u32[]{:S(2)}) copy-start(s32[4,16,128]{2,1,0:T(8,128)} %loading.1) | copy-start | bytes 98308
  4.8 15.5 %collective-permute-start.1 = (f32[192,384]{1,0:T(8,128)S(1)}, f32[192,384]{1,0:T(8,128)S(1)}, u32[]{:S(2)}, u32[]{:S(2)}) collective-permute-start(f32[192,384]{1,0:T(8,128)S(1)} %get-tuple-element.20), channel_id=1, source_target_pairs={{2,0},{3,1},{4,2},{5,3},{6,4},{7,5},{8,6},{9,7},{10,8},{11,9},{12,... | collective-permute-start | bytes 884744 | tf_op jit(solution)/shard_map/ppermute | solution.py:589
  6.1 14.2 %collective-permute-start = (f32[144,384]{1,0:T(8,128)S(1)}, f32[144,384]{1,0:T(8,128)S(1)}, u32[]{:S(2)}, u32[]{:S(2)}) collective-permute-start(f32[144,384]{1,0:T(8,128)S(1)} %get-tuple-element.19), channel_id=1, source_target_pairs={{0,2},{1,3},{2,4},{3,5},{4,6},{5,7},{6,8},{7,9},{8,10},{9,11},{10,... | collective-permute-start | bytes 663560 | tf_op jit(solution)/shard_map/ppermute | solution.py:589
  9.2 11.2 %collective-permute-start.2 = (f32[136,384]{1,0:T(8,128)S(1)}, f32[136,384]{1,0:T(8,128)S(1)}, u32[]{:S(2)}, u32[]{:S(2)}) collective-permute-start(f32[136,384]{1,0:T(8,128)S(1)} %get-tuple-element.21), channel_id=1, source_target_pairs={{0,1},{2,3},{4,5},{6,7},{8,9},{10,11},{12,13},{14,15},{16,17},{18,... | collective-permute-start | bytes 626696 | tf_op jit(solution)/shard_map/ppermute | solution.py:589
  12.2 6.0 %collective-permute-start.3 = (f32[24,384]{1,0:T(8,128)S(1)}, f32[24,384]{1,0:T(8,128)S(1)}, u32[]{:S(2)}, u32[]{:S(2)}) collective-permute-start(f32[24,384]{1,0:T(8,128)S(1)} %get-tuple-element.22), channel_id=1, source_target_pairs={{0,3},{2,5},{4,7},{6,9},{8,11},{10,13},{12,15},{14,17},{16,19},{18... | collective-permute-start | bytes 110600 | tf_op jit(solution)/shard_map/ppermute | solution.py:589
  15.1 5.3 %collective-permute-start.4 = (f32[24,384]{1,0:T(8,128)S(1)}, f32[24,384]{1,0:T(8,128)S(1)}, u32[]{:S(2)}, u32[]{:S(2)}) collective-permute-start(f32[24,384]{1,0:T(8,128)S(1)} %get-tuple-element.23), channel_id=1, source_target_pairs={{2,1},{4,3},{6,5},{8,7},{10,9},{12,11},{14,13},{16,15},{18,17},{20... | collective-permute-start | bytes 110600 | tf_op jit(solution)/shard_map/ppermute | solution.py:589
  30.4 1.6 %copy-start.2 = (f32[3,12,56,384]{3,2,1,0:T(8,128)}, f32[3,12,56,384]{3,2,1,0:T(8,128)S(1)}, u32[]{:S(2)}) copy-start(f32[3,12,56,384]{3,2,1,0:T(8,128)S(1)} %get-tuple-element.28.h_ref) | copy-start | bytes 9289732
  32.0 35.0 %collective-permute-start.5 = (f32[552,384]{1,0:T(8,128)S(1)}, f32[552,384]{1,0:T(8,128)S(1)}, u32[]{:S(2)}, u32[]{:S(2)}) collective-permute-start(f32[552,384]{1,0:T(8,128)S(1)} %get-tuple-element.29), channel_id=1, source_target_pairs={{0,2},{1,3},{2,4},{3,5},{4,6},{5,7},{6,8},{7,9},{8,10},{9,11},{10,... | collective-permute-start | bytes 2543624 | tf_op jit(solution)/shard_map/ppermute | solution.py:589
  35.6 31.3 %collective-permute-start.6 = (f32[504,384]{1,0:T(8,128)S(1)}, f32[504,384]{1,0:T(8,128)S(1)}, u32[]{:S(2)}, u32[]{:S(2)}) collective-permute-start(f32[504,384]{1,0:T(8,128)S(1)} %get-tuple-element.30), channel_id=1, source_target_pairs={{2,0},{3,1},{4,2},{5,3},{6,4},{7,5},{8,6},{9,7},{10,8},{11,9},{12,... | collective-permute-start | bytes 2322440 | tf_op jit(solution)/shard_map/ppermute | solution.py:589
  36.9 3.7 %collective-permute-start.7 = (f32[8,128]{1,0:T(8,128)S(1)}, f32[8,128]{1,0:T(8,128)S(1)}, u32[]{:S(2)}, u32[]{:S(2)}) collective-permute-start(f32[8,128]{1,0:T(8,128)S(1)} %get-tuple-element.33), channel_id=1, source_target_pairs={{0,1},{1,0},{2,3},{3,2},{4,5},{5,4},{6,7},{7,6},{8,9},{9,8},{10,11... | collective-permute-start | bytes 12296 | tf_op jit(solution)/shard_map/ppermute | solution.py:552
  40.6 1.2 %collective-permute-start.8 = (f32[8,128]{1,0:T(8,128)S(1)}, f32[8,128]{1,0:T(8,128)S(1)}, u32[]{:S(2)}, u32[]{:S(2)}) collective-permute-start(f32[8,128]{1,0:T(8,128)S(1)} %add.25), channel_id=1, source_target_pairs={{0,2},{1,3},{2,0},{3,1},{4,6},{5,7},{6,4},{7,5},{8,10},{9,11},{10,... | collective-permute-start | bytes 12296 | tf_op jit(solution)/shard_map/ppermute | solution.py:552
  41.8 8.2 %collective-permute-start.9 = (f32[8,128]{1,0:T(8,128)S(1)}, f32[8,128]{1,0:T(8,128)S(1)}, u32[]{:S(2)}, u32[]{:S(2)}) collective-permute-start(f32[8,128]{1,0:T(8,128)S(1)} %add.26), channel_id=1, source_target_pairs={{0,4},{1,5},{2,6},{3,7},{4,0},{5,1},{6,2},{7,3},{8,12},{9,13},{10,... | collective-permute-start | bytes 12296 | tf_op jit(solution)/shard_map/ppermute | solution.py:552
  50.0 9.6 %collective-permute-start.10 = (f32[8,128]{1,0:T(8,128)S(1)}, f32[8,128]{1,0:T(8,128)S(1)}, u32[]{:S(2)}, u32[]{:S(2)}) collective-permute-start(f32[8,128]{1,0:T(8,128)S(1)} %add.27), channel_id=1, source_target_pairs={{0,8},{1,9},{2,10},{3,11},{4,12},{5,13},{6,14},{7,15},{8,0},{9,1},... | collective-permute-start | bytes 12296 | tf_op jit(solution)/shard_map/ppermute | solution.py:552
  59.6 4.6 %collective-permute-start.11 = (f32[8,128]{1,0:T(8,128)S(1)}, f32[8,128]{1,0:T(8,128)S(1)}, u32[]{:S(2)}, u32[]{:S(2)}) collective-permute-start(f32[8,128]{1,0:T(8,128)S(1)} %add.28), channel_id=1, source_target_pairs={{0,16},{1,17},{2,18},{3,19},{4,20},{5,21},{6,22},{7,23},{8,24},{9,... | collective-permute-start | bytes 12296 | tf_op jit(solution)/shard_map/ppermute | solution.py:552
  64.3 14.2 %copy-start.7 = (f32[3]{0:T(128)}, f32[3]{0:T(128)S(1)}, u32[]{:S(2)}) copy-start(f32[3]{0:T(128)S(1)} %slice_reduce_fusion) | copy-start | bytes 40

commit v2 on v1

v2 whole, which is shorter than its diff:
```python
import functools
import math

import jax
import jax.numpy as jnp
import numpy as np
from jax import lax
from jax.experimental import pallas as pl
from jax.experimental.pallas import tpu as pltpu
from jax.sharding import PartitionSpec as P


RAD = 3
sharpness = 8.0
thresholds = (0.7, 0.5, 0.3)
stiff_floor = 0.001
load_force = 4.0
poisson = 0.3
LANES = 128
REACH = 2 * RAD


def element_matrix():
    inv_root = 1.0 / np.sqrt(3.0)
    elastic_scale = 1.0 / ((1.0 + poisson) * (1.0 - 2.0 * poisson))
    elastic = np.zeros((6, 6))
    for row_i in range(3):
        for col_j in range(3):
            elastic[row_i, col_j] = poisson
        elastic[row_i, row_i] = 1.0 - poisson
    for row_i in range(3, 6):
        elastic[row_i, row_i] = 0.5 - poisson
    elastic = elastic * elastic_scale
    corner_signs = [
        (2 * (corner // 4) - 1, 2 * (corner // 2 % 2) - 1, 2 * (corner % 2) - 1)
        for corner in range(8)
    ]
    stiffness = np.zeros((24, 24))
    for gauss_a in (-inv_root, inv_root):
        for gauss_b in (-inv_root, inv_root):
            for gauss_c in (-inv_root, inv_root):
                gauss_point = (gauss_a, gauss_b, gauss_c)
                derivs = np.zeros((8, 3))
                for corner in range(8):
                    for along in range(3):
                        slope_value = corner_signs[corner][along] / 8.0
                        for second in range(3):
                            if second != along:
                                slope_value = slope_value * (
                                    1.0 + corner_signs[corner][second] * gauss_point[second]
                                )
                        derivs[corner, along] = 2.0 * slope_value
                strain = np.zeros((6, 24))
                for corner in range(8):
                    column = 3 * corner
                    strain[0, column] = derivs[corner, 0]
                    strain[1, column + 1] = derivs[corner, 1]
                    strain[2, column + 2] = derivs[corner, 2]
                    strain[3, column] = derivs[corner, 1]
                    strain[3, column + 1] = derivs[corner, 0]
                    strain[4, column + 1] = derivs[corner, 2]
                    strain[4, column + 2] = derivs[corner, 1]
                    strain[5, column] = derivs[corner, 2]
                    strain[5, column + 2] = derivs[corner, 0]
                stiffness = stiffness + strain.T @ elastic @ strain * 0.125
    return stiffness


def parity_operator():
    signs = np.ones((8, 8))
    for mode in range(8):
        for corner in range(8):
            for bit in range(3):
                if (mode >> bit) & 1:
                    signs[mode, corner] *= 2 * ((corner >> bit) & 1) - 1
    full = np.kron(signs, np.eye(3))
    coupled = full @ element_matrix() @ full.T / 64.0
    coupled[np.abs(coupled) < 1e-9] = 0.0
    return coupled


COUPLED = parity_operator()
LOW_END = tuple(math.tanh(sharpness * eta) for eta in thresholds)
DENOM = tuple(
    math.tanh(sharpness * eta) + math.tanh(sharpness * (1.0 - eta)) for eta in thresholds
)


def tent_rows(rows):
    for step in (1, 2, 1, 2):
        rows = [rows[i] + rows[i + step] for i in range(len(rows) - step)]
    return rows


def tent_sublanes(block, amount):
    size = block.shape[0]
    for step in (1, 2, 1, 2):
        block = block + pltpu.roll(block, size - step, 0)
    return block[:amount]


def lanes_up(parts, step, lane):
    rolled = [pltpu.roll(part, LANES - step, 1) for part in parts]
    rolled.append(jnp.zeros_like(parts[0]))
    return [
        jnp.where(lane < LANES - step, rolled[g], rolled[g + 1]) for g in range(len(parts))
    ]


def lanes_down(parts, step, lane):
    rolled = [jnp.zeros_like(parts[0])] + [pltpu.roll(part, step, 1) for part in parts]
    return [jnp.where(lane >= step, rolled[g + 1], rolled[g]) for g in range(len(parts))]


def tent_lanes(parts):
    lane = lax.broadcasted_iota(jnp.int32, parts[0].shape, 1)
    total = [4.0 * part for part in parts]
    for step in range(1, RAD + 1):
        ups, downs = lanes_up(parts, step, lane), lanes_down(parts, step, lane)
        if step == RAD:
            total = [t + (u + d) for t, u, d in zip(total, ups, downs)]
        else:
            total = [
                t + float(RAD + 1 - step) * (u + d) for t, u, d in zip(total, ups, downs)
            ]
    return total


def tent_weight(place, extent):
    total = jnp.zeros(place.shape, jnp.float32)
    for offset in range(-RAD, RAD + 1):
        inside = (place + offset >= 0) & (place + offset < extent)
        total = total + jnp.where(inside, float(RAD + 1 - abs(offset)), 0.0)
    return total


def halves(block):
    high = block.astype(jnp.bfloat16)
    low = (block - high.astype(jnp.float32)).astype(jnp.bfloat16)
    return jnp.concatenate([high, low], axis=1)


def lane_groups(depth):
    return [slice(g * LANES, (g + 1) * LANES) for g in range(depth // LANES)]


def modes_of(nodes, row, lane):
    fields = [[[None] * 3 for _ in range(2)] for _ in range(2)]
    for comp in range(3):
        value = nodes(comp, row)
        size = value.shape[0]
        ahead = jnp.where(lane < LANES - 1, pltpu.roll(value, LANES - 1, 1), 0.0)
        for mz, part in enumerate((value + ahead, ahead - value)):
            beside = pltpu.roll(part, size - 1, 0)
            fields[0][mz][comp] = part + beside
            fields[1][mz][comp] = beside - part
    return fields


def element_modes(low, high):
    modes = []
    for mx in range(2):
        for my in range(2):
            for mz in range(2):
                modes.append([
                    (h + l) if mx == 0 else (h - l)
                    for l, h in zip(low[my][mz], high[my][mz])
                ])
    return modes


def coupled_forces(modes):
    forces = [[None] * 3 for _ in range(8)]
    for mode in range(8):
        for comp in range(3):
            row = COUPLED[3 * mode + comp]
            groups = {}
            for place in np.nonzero(row)[0]:
                groups.setdefault(round(float(row[place]), 12), []).append(int(place))
            total = None
            for factor, places in groups.items():
                summed = modes[places[0] // 3][places[0] % 3]
                for place in places[1:]:
                    summed = summed + modes[place // 3][place % 3]
                term = factor * summed
                total = term if total is None else total + term
            forces[mode][comp] = total
    return forces


def pick(n, high, low, kind):
    if kind == "merged":
        return jnp.where(n == 0, high, low)
    return high if kind == "high" else low


def column_start(n, cols, kind):
    if kind == "merged":
        return pl.multiple_of(jnp.where(n == 0, cols - 8, 0), 8)
    return cols - 8 if kind == "high" else 0


def fill_tail(ref, used):
    if ref.shape[0] > used:
        ref[used:, :] = jnp.zeros((ref.shape[0] - used, ref.shape[1]), jnp.float32)


def pack_kernel(
    kinds, design, passive, disp, support, near_ref, far_ref, row_ref, nodes_ref, *rest
):
    rows, cols, depth = design.shape
    cx, cy, _ = support.shape
    sides, (edges, masks, moves, frees, sems) = rest[: 3 * len(kinds)], rest[3 * len(kinds) :]
    groups = lane_groups(depth)
    n = lax.axis_index("narrow")
    even = lax.rem(lax.axis_index("wide"), 2) == 0
    near_start = jnp.where(even, rows - RAD, 0)
    far_start = jnp.where(even, 0, rows - RAD)
    copies = [
        pltpu.make_async_copy(disp, moves, sems.at[0]),
        pltpu.make_async_copy(support, frees, sems.at[1]),
    ]
    for index, kind in enumerate(kinds):
        start = column_start(n, cols, kind)
        copies.append(
            pltpu.make_async_copy(
                design.at[:, pl.ds(start, 8), :], edges.at[index], sems.at[2 + 2 * index]
            )
        )
        copies.append(
            pltpu.make_async_copy(
                passive.at[:, pl.ds(start, 8), :], masks.at[index], sems.at[3 + 2 * index]
            )
        )
    last = 2 + 2 * len(kinds)
    for at, start, ref in ((last, near_start, near_ref), (last + 1, far_start, far_ref)):
        copies.append(
            pltpu.make_async_copy(design.at[pl.ds(start, RAD)], ref.at[:RAD], sems.at[at])
        )
    for copy in copies:
        copy.start()
    nodes_ref[...] = jnp.zeros_like(nodes_ref)
    for copy in copies[:2]:
        copy.wait()
    for x in range(cx):
        free = 1.0 - frees[x].astype(jnp.float32)
        for r in range(3):
            for c in range(3):
                value = moves[r, c, x] * free
                nodes_ref[r, c, x, 1 : cy + 1, :] = value
                if x == 0:
                    near_ref[RAD, r * cy : (r + 1) * cy, groups[c]] = value
                    row_ref[r * cy : (r + 1) * cy, groups[c]] = value
    for copy in copies[2:last]:
        copy.wait()

    for index, kind in enumerate(kinds):
        side, side_near, side_far = sides[3 * index : 3 * index + 3]
        for k in range(rows):
            value = edges[index, k]
            piece = pick(n, value[8 - REACH :], value[:REACH], kind)
            side[pl.ds(k * REACH, REACH), :] = piece
            value = 1.0 - masks[index, k].astype(jnp.float32)
            side[pl.ds(rows * REACH + k * RAD, RAD), :] = pick(n, value[8 - RAD :], value[:RAD], kind)
        for k in range(RAD):
            for ref, start in ((side_near, near_start), (side_far, far_start)):
                value = edges[index, start + k]
                piece = pick(n, value[8 - REACH :], value[:REACH], kind)
                ref[pl.ds(k * REACH, REACH), :] = piece
        base = rows * (REACH + RAD)
        for r in range(3):
            for c in range(3):
                for x in range(cx):
                    value = nodes_ref[r, c, x]
                    piece = pick(n, value[cy - 1 : cy + 1], value[1:3], kind)
                    side[pl.ds(base + (r * cx + x) * 2, 2), groups[c]] = piece
                    if x == 0:
                        side_near[pl.ds(RAD * REACH + 2 * r, 2), groups[c]] = piece
                        side_far[pl.ds(RAD * REACH + 2 * r, 2), groups[c]] = piece
        fill_tail(side, base + 6 * cx)
        fill_tail(side_near, RAD * REACH + 6)
        fill_tail(side_far, RAD * REACH + 6)
    for copy in copies[last:]:
        copy.wait()


def element_energy(low, high):
    modes = element_modes(low, high)
    forces = coupled_forces(modes)
    total = None
    for mode in range(8):
        for comp in range(3):
            if forces[mode][comp] is not None:
                term = modes[mode][comp] * forces[mode][comp]
                total = term if total is None else total + term
    return total


def reciprocal_weight(place, extent):
    inside = (place >= 0) & (place < extent)
    return jnp.where(inside, 1.0 / jnp.maximum(tent_weight(place, extent), 1.0), 0.0)


def plane_reciprocals(n, n_narrow, cols, ext, depth):
    place_y = n * cols - RAD + lax.broadcasted_iota(jnp.int32, (ext, LANES), 0)
    recip_y = reciprocal_weight(place_y, n_narrow * cols)
    recip_z = []
    for g in range(depth // LANES):
        place_z = g * LANES + lax.broadcasted_iota(jnp.int32, (ext, LANES), 1)
        recip_z.append(1.0 / tent_weight(place_z, depth))
    return recip_y, recip_z


def low_ends():
    return [jnp.tanh(jnp.full((1, LANES), sharpness * eta, jnp.float32)) for eta in thresholds]


def project_row(row, recip_x, recips, lows, emit, groups):
    recip_y, recip_z = recips
    recip_xy = recip_y * recip_x
    for g, lanes in enumerate(groups):
        recip = recip_xy * recip_z[g]
        scaled = sharpness * row(lanes)
        for r in range(3):
            steep = jnp.tanh(scaled - sharpness * thresholds[r])
            dense = steep + lows[r]
            square = dense * dense
            emit(r, g, lanes, square * (1.0 - steep * steep) * recip, square * dense)


def element_sums(cubes, amount, packed, reach, padded):
    row_id = lax.broadcasted_iota(jnp.int32, (LANES, LANES), 0)
    col_id = lax.broadcasted_iota(jnp.int32, (LANES, LANES), 1)
    total = None
    packed[...] = jnp.zeros_like(packed)
    for g in range(cubes.shape[1]):
        for at in range(amount):
            summed = cubes[at, g, pl.ds(0, reach, stride=3), :]
            summed = summed + cubes[at, g, pl.ds(1, reach, stride=3), :]
            summed = summed + cubes[at, g, pl.ds(2, reach, stride=3), :]
            packed[at * padded : at * padded + reach, :] = summed
        gather = ((g * LANES + row_id) // 3 == col_id).astype(jnp.float32).astype(jnp.bfloat16)
        term = jnp.dot(
            halves(packed[...]),
            jnp.concatenate([gather, gather], axis=0),
            preferred_element_type=jnp.float32,
        )
        total = term if total is None else total + term
    return total


def modulus_of(value, r, keep):
    value = stiff_floor + ((1.0 - stiff_floor) / 27.0 / DENOM[r] ** 3) * value
    return jnp.where(keep, value, 0.0)


def load_kernel(design_hbm, passive_hbm, design, mask_ref, passive, sems):
    rows, cols, depth = design.shape
    copies = [
        pltpu.make_async_copy(passive_hbm, passive, sems.at[0]),
        pltpu.make_async_copy(design_hbm, design, sems.at[1]),
    ]
    for copy in copies:
        copy.start()
    copies[0].wait()
    for k in range(rows):
        mask_ref[k, RAD : RAD + cols, :] = 1.0 - passive[k].astype(jnp.float32)
        mask_ref[k, :RAD, :] = jnp.zeros((RAD, depth), jnp.float32)
        tail = mask_ref.shape[1] - RAD - cols
        mask_ref[k, RAD + cols :, :] = jnp.zeros((tail, depth), jnp.float32)
    copies[1].wait()


def blur_kernel(
    n_wide, n_narrow, design, mask_in, nodes_in, near, far,
    side_b, side_a, near_b, near_a, far_b, far_a,
    v_ref, nodes_ref, near_ref, far_ref, ends, corners, blurred, edge_mask,
):
    rows, cols, depth = design.shape
    cx = nodes_ref.shape[2]
    cy = cols // 3
    groups = lane_groups(depth)
    n = lax.axis_index("narrow")
    w = lax.axis_index("wide")
    valid_b = jnp.where(n > 0, 1.0, 0.0)
    valid_a = jnp.where(n < n_narrow - 1, 1.0, 0.0)
    ext = v_ref.shape[1]

    above = 1 - lax.rem(w, 2)
    for index, ref in ((above, near), (1 - above, far)):
        for k in range(RAD):
            ends[index, k] = ref[k]
    for index, pair in ((above, (near_b, near_a)), (1 - above, (far_b, far_a))):
        for which, ref in enumerate(pair):
            corners[which, index] = ref[...] * (valid_b, valid_a)[which]

    base = rows * (REACH + RAD)
    for r in range(3):
        for c in range(3):
            lanes = groups[c]
            for x in range(cx):
                nodes_ref[r, c, x] = nodes_in[r, c, x]
                at = base + (r * cx + x) * 2
                nodes_ref[r, c, x, 0:1, :] = side_b[at + 1 : at + 2, lanes] * valid_b
                nodes_ref[r, c, x, cy + 1 : cy + 3, :] = side_a[at : at + 2, lanes] * valid_a

    for start in range(0, cols, 8):
        place = slice(start, start + 8)
        for lanes in groups:
            column = [ends[0, k, place, lanes] for k in range(RAD)]
            column += [design[k, place, lanes] for k in range(rows)]
            column += [ends[1, k, place, lanes] for k in range(RAD)]
            for k, value in enumerate(tent_rows(column)):
                blurred[k, REACH + start : REACH + start + 8, lanes] = value
    span = lambda k: slice(k * REACH, (k + 1) * REACH)
    for which, at, side, valid in ((0, 0, side_b, valid_b), (1, REACH + cols, side_a, valid_a)):
        for lanes in groups:
            column = [corners[which, 0, span(k), lanes] for k in range(RAD)]
            column += [side[span(k), lanes] * valid for k in range(rows)]
            column += [corners[which, 1, span(k), lanes] for k in range(RAD)]
            for k, value in enumerate(tent_rows(column)):
                blurred[k, at : at + REACH, lanes] = value
    tail = blurred.shape[1] - cols - 2 * REACH
    if tail:
        blurred[:, cols + 2 * REACH :, :] = jnp.zeros((rows, tail, depth), jnp.float32)

    edge_mask[...] = mask_in[...]
    for k in range(rows):
        at = rows * REACH + k * RAD
        edge_mask[k, 0:RAD, :] = side_b[at : at + RAD, :]
        edge_mask[k, RAD + cols : 2 * RAD + cols, :] = side_a[at : at + RAD, :]

    recip_y, recip_z = plane_reciprocals(n, n_narrow, cols, ext, depth)

    def fine_row(x, carry):
        for sub in range(3):
            k = 3 * x + sub
            parts = tent_lanes([tent_sublanes(blurred[k, :, lanes], ext) for lanes in groups])
            place_x = w * rows + k + jnp.zeros((8, LANES), jnp.int32)
            recip_x = reciprocal_weight(place_x, n_wide * rows)[0:1]
            recip_xy = recip_y * recip_x
            for g, lanes in enumerate(groups):
                v_ref[k, :, lanes] = (recip_xy * recip_z[g]) * parts[g] * edge_mask[k, :, lanes]
        return carry

    for x in range(cx):
        fine_row(x, 0)

    near_first, near_x = above * (rows - RAD), 1 + above * (cx - 2)
    for ref, first, x in (
        (near_ref, near_first, near_x), (far_ref, rows - RAD - near_first, cx - near_x)
    ):
        for k in range(RAD):
            ref[k * ext : (k + 1) * ext, :] = v_ref[first + k]
        for r in range(3):
            at = RAD * ext + r * nodes_ref.shape[3]
            for c in range(3):
                ref[at : at + nodes_ref.shape[3], groups[c]] = nodes_ref[r, c, x]


def project_kernel(
    n_wide, n_narrow, v_ref, nodes_in, near, row, near_b, near_a, far_b, far_a,
    gg_ref, moduli_ref, part_ref, nodes_ref, energy, cubes, packed, agg, corners,
):
    rows, ext, depth = v_ref.shape
    cx = rows // 3
    padded = energy.shape[1]
    groups = lane_groups(depth)
    n = lax.axis_index("narrow")
    w = lax.axis_index("wide")
    cy = (ext - 2 * RAD) // 3
    cols = 3 * cy
    reach = cy + 2

    even = lax.rem(w, 2) == 0
    valid = (jnp.where(n > 0, 1.0, 0.0), jnp.where(n < n_narrow - 1, 1.0, 0.0))
    for which, (one, other) in enumerate(((near_b, far_b), (near_a, far_a))):
        corners[which] = jnp.where(even, one[...], other[...]) * valid[which]
    for r in range(3):
        span = slice(r * cy, (r + 1) * cy)
        at = RAD * REACH + 2 * r
        for c in range(3):
            lanes = groups[c]
            for x in range(cx):
                nodes_ref[r, c, x] = nodes_in[r, c, x]
            nodes_ref[r, c, cx] = jnp.zeros_like(nodes_ref[r, c, cx])
            nodes_ref[r, c, cx, 1 : cy + 1, :] = jnp.where(even, near[RAD, span, lanes], row[span, lanes])
            nodes_ref[r, c, cx, 0:1, :] = corners[0, at + 1 : at + 2, lanes]
            nodes_ref[r, c, cx, cy + 1 : cy + 3, :] = corners[1, at : at + 2, lanes]
    lane = lax.broadcasted_iota(jnp.int32, nodes_ref.shape[3:], 1)
    for r in range(3):
        nodes = lambda c, x: nodes_ref[r, c, x]
        low = modes_of(nodes, 0, lane)
        for x in range(cx):
            high = modes_of(nodes, x + 1, lane)
            energy[r * cx + x] = element_energy(low, high)
            low = high

    recips = plane_reciprocals(n, n_narrow, cols, ext, depth)
    lows = low_ends()

    def coarse_row(x, carry):
        for sub in range(3):
            k = 3 * x + sub
            place_x = w * rows + k + jnp.zeros((8, LANES), jnp.int32)
            recip_x = reciprocal_weight(place_x, n_wide * rows)[0:1]

            def emit(r, g, lanes, gradient, cube):
                gg_ref[r, k, :, lanes] = gradient
                at = r * cx + x
                cubes[at, g] = cube if sub == 0 else cubes[at, g] + cube

            project_row(lambda lanes: v_ref[k, :, lanes], recip_x, recips, lows, emit, groups)
        return carry

    lax.fori_loop(0, cx, coarse_row, 0)

    agg[...] = element_sums(cubes, 3 * cx, packed, reach, padded)
    sub_id = lax.broadcasted_iota(jnp.int32, (padded, LANES), 0)
    keep = (sub_id > jnp.where(n > 0, -1, 0)) & (sub_id < reach)
    own = ((sub_id >= 1) & (sub_id <= cy)).astype(jnp.float32)
    part_ref[...] = jnp.zeros_like(part_ref)
    for r in range(3):
        partial = None
        for x in range(cx):
            at = r * cx + x
            value = modulus_of(agg[at * padded : (at + 1) * padded, :], r, keep)
            moduli_ref[at] = value
            term = value * energy[at]
            partial = term if partial is None else partial + term
        part_ref[r : r + 1, :] = jnp.sum(partial * own, axis=0, keepdims=True)


def nodal_rows(nodes, moduli, cx, first, lane):
    low = modes_of(nodes, first, lane)
    below = None
    for x in range(first, cx + 1):
        sums, above = None, None
        if x < cx:
            high = modes_of(nodes, x + 1, lane)
            forces = coupled_forces(element_modes(low, high))
            low = high
            modulus = moduli(x)
            scaled = [[None if f is None else modulus * f for f in mode] for mode in forces]
            sums = [[[None] * 3 for _ in range(2)] for _ in range(2)]
            above = [[[None] * 3 for _ in range(2)] for _ in range(2)]
            for my in range(2):
                for mz in range(2):
                    for comp in range(3):
                        even = scaled[2 * my + mz][comp]
                        odd = scaled[4 + 2 * my + mz][comp]
                        sums[my][mz][comp] = -odd if even is None else even - odd
                        above[my][mz][comp] = odd if even is None else even + odd
        yield x, sums, below
        below = above


def nodal_total(sums, below, comp, lane):
    along = []
    for mz in range(2):
        pair = []
        for my in range(2):
            terms = [part[my][mz][comp] for part in (sums, below) if part is not None]
            pair.append(terms[0] if len(terms) == 1 else terms[0] + terms[1])
        along.append((pair[0] - pair[1]) + pltpu.roll(pair[0] + pair[1], 1, 0))
    return (along[0] - along[1]) + jnp.where(
        lane >= 1, pltpu.roll(along[0] + along[1], 1, 1), 0.0
    )


def fields_kernel(
    n_wide, n_narrow, gg, energy, nodes_ref, near, far,
    summed_ref, extra_ref, moduli_ref, outer, spread_ref, packed, cubes, packed_outer,
):
    _, rows, ext, depth = gg.shape
    cx = rows // 3
    cols = 3 * ((ext - 2 * RAD) // 3)
    padded = energy.shape[1]
    reach = ext // 3
    groups = lane_groups(depth)
    n = lax.axis_index("narrow")
    w = lax.axis_index("wide")
    above = 1 - lax.rem(w, 2)
    row_id = lax.broadcasted_iota(jnp.int32, (LANES, LANES), 0)
    col_id = lax.broadcasted_iota(jnp.int32, (LANES, LANES), 1)
    coarse = cx + 2
    lane = lax.broadcasted_iota(jnp.int32, (padded, LANES), 1)
    for r in range(3):
        base = r * coarse
        for x in range(cx):
            packed[base + x + 1] = energy[r * cx + x]
        span = slice(RAD * ext + r * padded, RAD * ext + (r + 1) * padded)
        for c in range(3):
            extra_ref[r, c, above] = near[span, groups[c]]
            extra_ref[r, c, 1 - above] = far[span, groups[c]]
        first, last = (
            modes_of(lambda c, x: nodes_ref[r, c, x], x, lane) for x in (0, cx)
        )
        below, beyond = (
            modes_of(lambda c, x: extra_ref[r, c, x], x, lane) for x in (0, 1)
        )
        packed[base] = element_energy(below, first)
        packed[base + cx + 1] = element_energy(last, beyond)
    split = halves(packed[...].reshape(3 * coarse * padded, LANES))
    for g in range(len(groups)):
        copies = (row_id == (g * LANES + col_id) // 3).astype(jnp.float32).astype(jnp.bfloat16)
        fine = jnp.dot(
            split, jnp.concatenate([copies, copies], axis=0), preferred_element_type=jnp.float32
        )
        for at in range(3 * coarse):
            value = fine[at * padded : at * padded + reach]
            for sub in range(3):
                spread_ref[at, g, pl.ds(sub, reach, stride=3), :] = value
            if 3 * reach < ext:
                spread_ref[at, g, 3 * reach :, :] = jnp.zeros((ext - 3 * reach, LANES), jnp.float32)

    recips = plane_reciprocals(n, n_narrow, cols, ext, depth)
    lows = low_ends()

    def neighbour_row(k, carry):
        at = pl.multiple_of(k * ext, 8)
        for ref, side in ((near, above), (far, 1 - above)):
            first = w * rows + jnp.where(side == 0, -RAD, rows)
            place_x = first + k + jnp.zeros((8, LANES), jnp.int32)
            recip_x = reciprocal_weight(place_x, n_wide * rows)[0:1]

            def emit(r, g, lanes, gradient, cube):
                outer[r, side * RAD + k, :, lanes] = gradient
                cubes[k, side * 3 + r, g] = cube

            project_row(
                lambda lanes: ref[pl.ds(at, ext), lanes], recip_x, recips, lows, emit, groups
            )
        return carry

    lax.fori_loop(0, RAD, neighbour_row, 0)

    for r in range(3):
        for g in range(len(groups)):
            cubes[0, r, g] = cubes[0, r, g] + cubes[1, r, g] + cubes[2, r, g]
    sums = element_sums(cubes.at[0], 3, packed_outer, reach, padded)
    sub_id = lax.broadcasted_iota(jnp.int32, (padded, LANES), 0)
    last = jnp.where(w > 0, reach, 0)
    keep = (sub_id > jnp.where(n > 0, -1, 0)) & (sub_id < last)
    for r in range(3):
        moduli_ref[r] = modulus_of(sums[r * padded : (r + 1) * padded], r, keep)

    for r in range(3):
        def first_dim(s, carry):
            place = pl.ds(pl.multiple_of(8 * s, 8), 8)
            for g, lanes in enumerate(groups):
                column = []
                for x in range(coarse):
                    spread = spread_ref[r * coarse + x, g, place, :]
                    for sub in range(3):
                        if x == 0:
                            value = outer[r, sub, place, lanes]
                        elif x == coarse - 1:
                            value = outer[r, RAD + sub, place, lanes]
                        else:
                            value = gg[r, 3 * (x - 1) + sub, place, lanes]
                        column.append(value * spread)
                for k, value in enumerate(tent_rows(column)):
                    summed_ref[r, k, place, lanes] = value
            return carry

        lax.fori_loop(0, ext // 8, first_dim, 0)


def force_kernel(nodes_ref, extra, moduli, moduli_below, support, loading, residual_ref):
    cx, cy, _ = support.shape
    lane = lax.broadcasted_iota(jnp.int32, nodes_ref.shape[3:], 1)
    for r in range(3):
        nodes = lambda c, x: extra[r, c, 0] if x < 0 else nodes_ref[r, c, x]
        modulus = lambda x: moduli_below[r] if x < 0 else moduli[r * cx + x]
        for x, sums, below in nodal_rows(nodes, modulus, cx, -1, lane):
            if 0 <= x < cx:
                free = 1.0 - support[x].astype(jnp.float32)
                for comp in range(3):
                    total = nodal_total(sums, below, comp, lane)[1 : cy + 1]
                    if comp == 2:
                        total = total + load_force * loading[x].astype(jnp.float32)
                    residual_ref[r, comp, x] = -total * free


def realization_factors(part, shape):
    factors, totals = [], []
    for r in range(3):
        total = jnp.sum(part[r : r + 1, :], axis=1, keepdims=True)
        factor = 3.0 * (1.0 - stiff_floor) / 27.0 * sharpness / DENOM[r] ** 3
        factors.append(jnp.broadcast_to(-factor / total, shape))
        totals.append(total)
    return factors, totals


def final_kernel(part, summed, out_ref, compliance_ref):
    rows, cols, depth = out_ref.shape
    groups = lane_groups(depth)
    factors, totals = realization_factors(part, (1, LANES))
    for r in range(3):
        compliance_ref[r] = jnp.sum(totals[r])

    def other_dims(step, carry):
        for sub in range(3):
            k = 3 * step + sub
            parts = []
            for lanes in groups:
                total = None
                for r in range(3):
                    term = factors[r] * summed[r, k, :, lanes]
                    total = term if total is None else total + term
                parts.append(tent_sublanes(total, cols))
            for lanes, value in zip(groups, tent_lanes(parts)):
                out_ref[k, :, lanes] = value
        return carry

    for step in range(rows // 3):
        other_dims(step, 0)


def call(kernel, shapes, scratch, flops, args, hbm=0, scalars=(), limit=20):
    vmem = pl.BlockSpec(memory_space=pltpu.VMEM)
    smem = pl.BlockSpec(memory_space=pltpu.SMEM)
    scratch = [pltpu.VMEM(s, jnp.float32) if isinstance(s, tuple) else s for s in scratch]
    args = [
        pltpu.with_memory_space_constraint(arg, pltpu.HBM) if i < hbm else arg
        for i, arg in enumerate(args)
    ]
    return pl.pallas_call(
        kernel,
        out_shape=[jax.ShapeDtypeStruct(s, jnp.float32) for s in list(shapes) + list(scalars)],
        in_specs=[pl.BlockSpec(memory_space=pltpu.HBM)] * hbm + [vmem] * (len(args) - hbm),
        out_specs=[vmem] * len(shapes) + [smem] * len(scalars),
        scratch_shapes=scratch,
        compiler_params=pltpu.CompilerParams(vmem_limit_bytes=limit * 1024 * 1024),
        cost_estimate=pl.CostEstimate(flops=flops, bytes_accessed=1000000, transcendentals=0),
    )(*args)


def ceil8(amount):
    return -(-amount // 8) * 8


def exchange_sum(value, total, group):
    axes = ("wide", "narrow")
    parts = [lax.ppermute(value, axes, [(i, i ^ k) for i in range(total)]) for k in group]
    for part in parts:
        value = value + part
    return value


def local(n_wide, n_narrow, design, passive, displacement, support, loading):
    rows, cols, depth = design.shape
    cx, cy, cz = support.shape
    merged = n_narrow == 2
    axes = ("wide", "narrow")
    ext = ceil8(cols + 2 * RAD)
    padded = ceil8(cy + 3)

    def route(toward, dy):
        pairs = []
        for i in range(n_wide):
            if toward == "down" and i % 2:
                continue
            mate = {"near": i ^ 1, "far": i + 1 if i % 2 else i - 1, "self": i, "down": i - 1}[toward]
            for j in range(n_narrow):
                if 0 <= mate < n_wide and 0 <= j + dy < n_narrow:
                    pairs.append((i * n_narrow + j, mate * n_narrow + j + dy))
        return pairs

    def side_route(toward, index):
        if merged:
            return route(toward, 1) + route(toward, -1)
        return route(toward, 1 if index == 0 else -1)

    def send(block, pairs):
        return lax.ppermute(block, axes, pairs)

    kinds = ("merged",) if merged else ("high", "low")
    sides = len(kinds)
    corner = (ceil8(RAD * REACH + 6), depth)
    ends = (RAD, cols, depth)
    nodes_shape = (3, 3, cx, padded, cz)
    coarse_shape = (3 * cx, padded, cz)
    count = ceil8(cols + 2 * REACH)
    ints = lambda *shape: pltpu.VMEM(shape, jnp.int32)
    packs = call(
        functools.partial(pack_kernel, kinds),
        [(RAD + 1, cols, depth), ends, (3 * cy, depth), nodes_shape]
        + [(ceil8(rows * (REACH + RAD) + 6 * cx), depth), corner, corner] * sides,
        [
            (sides, rows, 8, depth), ints(sides, rows, 8, depth), displacement.shape,
            ints(*support.shape), pltpu.SemaphoreType.DMA((4 + 2 * sides,)),
        ],
        200000, (design, passive, displacement, support), hbm=4,
    )
    far = send(packs[1], route("far", 0))
    got = []
    for index in range(sides):
        side, side_near, side_far = packs[4 + 3 * index : 7 + 3 * index]
        got.append((
            send(side, side_route("self", index)),
            send(side_near, side_route("near", index)),
            send(side_far, side_route("far", index)),
        ))
    near = send(packs[0], route("near", 0))
    row = send(packs[2], route("down", 0))
    own_design, own_mask = call(
        load_kernel, [design.shape, (rows, ext, depth)],
        [ints(*passive.shape), pltpu.SemaphoreType.DMA((2,))],
        200000, (design, passive), hbm=2,
    )
    before, after = got[0], got[-1]
    corners = (before[1], after[1], before[2], after[2])
    outer = (RAD * ext + 3 * padded, depth)
    v, nodes, v_near, v_far = call(
        functools.partial(blur_kernel, n_wide, n_narrow),
        [(rows, ext, depth), nodes_shape, outer, outer],
        [(2,) + ends, (2, 2) + corner, (rows, count, depth), (rows, ext, depth)],
        10000000,
        (own_design, own_mask, packs[3], near, far, before[0], after[0]) + corners,
    )
    v_far = send(v_far, route("far", 0))
    v_near = send(v_near, route("near", 0))
    gg, moduli, part, nodes, energy = call(
        functools.partial(project_kernel, n_wide, n_narrow),
        [
            (3, rows, ext, depth), coarse_shape, (8, LANES), (3, 3, cx + 1, padded, cz),
            coarse_shape,
        ],
        [
            (3 * cx, depth // LANES, ext, LANES), (3 * cx * padded, LANES),
            (3 * cx * padded, LANES), (2,) + corner,
        ],
        10000000, (v, nodes, near, row) + corners,
    )
    total = n_wide * n_narrow
    steps = [1 << bit for bit in range(total.bit_length() - 1)]
    groups = [(s,) for s in steps[:-2]] + [(steps[-2], steps[-1], steps[-2] + steps[-1])]
    fields, extra, moduli_below = call(
        functools.partial(fields_kernel, n_wide, n_narrow),
        [(3, rows, ext, depth), (3, 3, 2, padded, cz), (3, padded, cz)],
        [
            (3, 2 * RAD, ext, depth), (3 * (cx + 2), depth // LANES, ext, LANES),
            (3 * (cx + 2), padded, LANES), (RAD, 6, depth // LANES, ext, LANES),
            (3 * padded, LANES),
        ],
        10000000, (gg, energy, nodes, v_near, v_far),
    )
    (residual,) = call(
        force_kernel, [displacement.shape], [], 10000000,
        (nodes, extra, moduli, moduli_below, support, loading),
    )
    summed = part
    for group in groups:
        summed = exchange_sum(summed, total, group)
    sensitivity, compliance = call(
        final_kernel, [design.shape], [], 10000000, (summed, fields), scalars=[(3,)],
    )
    return residual, compliance, sensitivity


def solution(mesh):
    in_specs = (
        P("wide", "narrow", None),
        P("wide", "narrow", None),
        P(None, None, "wide", "narrow", None),
        P("wide", "narrow", None),
        P("wide", "narrow", None),
    )
    out_specs = (P(None, None, "wide", "narrow", None), P(), P("wide", "narrow", None))

    def body(*args):
        return local(mesh.shape["wide"], mesh.shape["narrow"], *args)

    return jax.shard_map(body, mesh=mesh, in_specs=in_specs, out_specs=out_specs, check_vma=False)
```

time: 79.1 us -> 57.5 us (0.73)
  local copies, waits for them, and re-layouts: 6.28 us -> 0.01 us
  Pallas kernels: 20.6 us -> 15.1 us
  waiting for transfers between devices: 15.4 us -> 11.6 us
  starting transfers between devices: 32.2 us -> 29.8 us
  between operations: 2.78 us -> 0.78 us
  other arithmetic: 1.19 us -> 0.01 us
    unnamed x16 -> x4, local copies, waits for them, and re-layouts: 5.68 us -> 0.01 us
    pallas_call x4 -> x7, Pallas kernels: 20.6 us -> 15.1 us  [call(): pl.pallas_call(kernel, out_shape=[jax.ShapeDtypeStruct(s, jnp.float32) fo...]
    ppermute x12 -> x14, waiting for transfers between devices: 15.4 us -> 11.6 us  [the longest x6 9.45 us: exchange_sum(): lax.ppermute(value, axes, [(i, i ^ k) for i in range(total)])]
    ppermute x12 -> x14, starting transfers between devices: 32.2 us -> 29.8 us  [the longest x6 19.4 us: exchange_sum(): lax.ppermute(value, axes, [(i, i ^ k) for i in range(total)])]
    add x6 -> x4, other arithmetic: 1.07 us -> 0.01 us  [exchange_sum(): value = value + part]
  transfers between devices with their start and end apart: 12 -> 14, of which waited for: 7 -> 6; matrix products, arithmetic and copies ran while one was open for 1% -> 0% of each run, Pallas kernels for 0% -> 7%
where the time goes in v2:
time: 57.5 us; the launch traced here: 57.2 us
  starting transfers between devices  29.8 us (52%)
  Pallas kernels  15.1 us (26%)
  waiting for transfers between devices  11.6 us (20%)
  between operations  0.78 us (1%)
    ppermute x6, starting transfers between devices, exchange_sum(): lax.ppermute(value, axes, [(i, i ^ k) for i in range(total)])  19.4 us
    pallas_call x7, Pallas kernels, call(): pl.pallas_call(kernel, out_shape=[jax.ShapeDtypeStruct(s, jnp.float32) fo...  15.1 us
    ppermute x8, starting transfers between devices, send(): return lax.ppermute(block, axes, pairs)  10.4 us
    ppermute x6, waiting for transfers between devices, exchange_sum(): lax.ppermute(value, axes, [(i, i ^ k) for i in range(total)])  9.45 us
    ppermute x8, waiting for transfers between devices, send(): return lax.ppermute(block, axes, pairs)  2.17 us
  transfers between devices with their start and end apart: 14, of which 6 were waited for; matrix products, arithmetic and copies ran while one was open for 0% of the time, Pallas kernels for 7%

profile of v2, /device:TPU:0, one launch (start us, length us, event | category | flops | bytes accessed | tf_op | source)
XLA Modules:
  0.0 57.2 jit_solution(3661929129361836723)
XLA Ops:
  0.6 1.3 %shard_map.77 = (f32[4,48,384]{2,1,0:T(8,128)S(1)}, f32[3,48,384]{2,1,0:T(8,128)S(1)}, f32[48,384]{1,0:T(8,128)S(1)}, f32[3,3,4,24,128]{4,3,2,1,0:T(8,128)S(1)},...) custom-call(f32[12,48,384]{2,1,0:T(8,128)} %design.1, s32[12,48,384]{2,1,0:T(8,128)} %passive.1, ...), custom_call_target="tpu_custom_call" | custom-call | flops 200000 | bytes 1000000 | tf_op jit(solution)/shard_map/pallas_call | solution.py:729
  2.0 0.6 collective-permute-start
  2.5 0.7 %collective-permute-start.1 = (f32[3,48,384]{2,1,0:T(8,128)S(1)}, f32[3,48,384]{2,1,0:T(8,128)S(1)}, u32[]{:S(2)}, u32[]{:S(2)}) collective-permute-start(f32[3,48,384]{2,1,0:T(8,128)S(1)} %get-tuple-element.30), channel_id=1, source_target_pairs={{2,4},{3,5},{4,2},{5,3},{6,8},{7,9},{8,6},{9,7},{10,12},{11,13},{1... | collective-permute-start | bytes 663560 | tf_op jit(solution)/shard_map/ppermute | solution.py:777
  3.2 2.6 %collective-permute-start.2 = (f32[136,384]{1,0:T(8,128)S(1)}, f32[136,384]{1,0:T(8,128)S(1)}, u32[]{:S(2)}, u32[]{:S(2)}) collective-permute-start(f32[136,384]{1,0:T(8,128)S(1)} %get-tuple-element.31), channel_id=1, source_target_pairs={{0,1},{2,3},{4,5},{6,7},{8,9},{10,11},{12,13},{14,15},{16,17},{18,... | collective-permute-start | bytes 626696 | tf_op jit(solution)/shard_map/ppermute | solution.py:777
  5.8 2.7 %collective-permute-start.3 = (f32[24,384]{1,0:T(8,128)S(1)}, f32[24,384]{1,0:T(8,128)S(1)}, u32[]{:S(2)}, u32[]{:S(2)}) collective-permute-start(f32[24,384]{1,0:T(8,128)S(1)} %get-tuple-element.32), channel_id=1, source_target_pairs={{0,3},{2,1},{4,7},{6,5},{8,11},{10,9},{12,15},{14,13},{16,19},{18,... | collective-permute-start | bytes 110600 | tf_op jit(solution)/shard_map/ppermute | solution.py:777
  8.4 0.7 %collective-permute-start.4 = (f32[24,384]{1,0:T(8,128)S(1)}, f32[24,384]{1,0:T(8,128)S(1)}, u32[]{:S(2)}, u32[]{:S(2)}) collective-permute-start(f32[24,384]{1,0:T(8,128)S(1)} %get-tuple-element.33), channel_id=1, source_target_pairs={{2,5},{4,3},{6,9},{8,7},{10,13},{12,11},{14,17},{16,15},{18,21},{2... | collective-permute-start | bytes 110600 | tf_op jit(solution)/shard_map/ppermute | solution.py:777
  9.1 1.5 %shard_map.76 = (f32[12,48,384]{2,1,0:T(8,128)S(1)}, f32[12,56,384]{2,1,0:T(8,128)S(1)}) custom-call(f32[12,48,384]{2,1,0:T(8,128)} %design.1, s32[12,48,384]{2,1,0:T(8,128)} %passive.1), custom_call_target="tpu_custom_call" | custom-call | flops 200000 | bytes 1000000 | tf_op jit(solution)/shard_map/pallas_call | solution.py:729
  10.6 2.1 %collective-permute-done.3.near_b.near_a = f32[24,384]{1,0:T(8,128)S(1)} collective-permute-done((f32[24,384]{1,0:T(8,128)S(1)}, f32[24,384]{1,0:T(8,128)S(1)}, u32[]{:S(2)}, u32[]{:S(2)}) %collective-permute-start.3) | collective-permute-done | bytes 36896 | tf_op jit(solution)/shard_map/ppermute | solution.py:777
  12.7 0.0 collective-permute-done.4.far_b.far_a
  12.7 0.0 collective-permute-done.2.side_b.side_a
  12.7 0.0 collective-permute-done.1.far
  12.7 0.0 collective-permute-done.near
  12.7 2.3 %shard_map.78 = (f32[12,56,384]{2,1,0:T(8,128)S(1)}, f32[3,3,4,24,128]{4,3,2,1,0:T(8,128)S(1)}, f32[240,384]{1,0:T(8,128)S(1)}, f32[240,384]{1,0:T(8,128)S(1)}) custom-call(f32[12,48,384]{2,1,0:T(8,128)S(1)} %get-tuple-element.26.design, f32[12,56,384]{2,1,0:T(8,128)S(1)} %get-tuple-element.27.mask_in, f32[3,3,4,24,128]{4,3,2,1,0:T(8,128)S(1)} %get-tuple-element.28.nodes_in, ...), custom_call_target="tpu_custom_call" | custom-call | flops 10000000 | bytes 1000000 | tf_op jit(solution)/shard_map/pallas_call | solution.py:729
  15.0 1.9 %collective-permute-start.6 = (f32[240,384]{1,0:T(8,128)S(1)}, f32[240,384]{1,0:T(8,128)S(1)}, u32[]{:S(2)}, u32[]{:S(2)}) collective-permute-start(f32[240,384]{1,0:T(8,128)S(1)} %get-tuple-element.40), channel_id=1, source_target_pairs={{0,2},{1,3},{2,0},{3,1},{4,6},{5,7},{6,4},{7,5},{8,10},{9,11},{10,... | collective-permute-start | bytes 1105928 | tf_op jit(solution)/shard_map/ppermute | solution.py:777
  16.9 0.7 %collective-permute-start.7 = (f32[240,384]{1,0:T(8,128)S(1)}, f32[240,384]{1,0:T(8,128)S(1)}, u32[]{:S(2)}, u32[]{:S(2)}) collective-permute-start(f32[240,384]{1,0:T(8,128)S(1)} %get-tuple-element.41), channel_id=1, source_target_pairs={{2,4},{3,5},{4,2},{5,3},{6,8},{7,9},{8,6},{9,7},{10,12},{11,13},{1... | collective-permute-start | bytes 1105928 | tf_op jit(solution)/shard_map/ppermute | solution.py:777
  17.6 0.7 %collective-permute-start.5 = (f32[48,384]{1,0:T(8,128)S(1)}, f32[48,384]{1,0:T(8,128)S(1)}, u32[]{:S(2)}, u32[]{:S(2)}) collective-permute-start(f32[48,384]{1,0:T(8,128)S(1)} %get-tuple-element.36), channel_id=1, source_target_pairs={{4,2},{5,3},{8,6},{9,7},{12,10},{13,11},{16,14},{17,15},{20,18},{2... | collective-permute-start | bytes 221192 | tf_op jit(solution)/shard_map/ppermute | solution.py:777
  18.3 0.0 collective-permute-done.5.row
  18.3 2.4 %shard_map.79 = (f32[3,12,56,384]{3,2,1,0:T(8,128)S(1)}, f32[12,24,128]{2,1,0:T(8,128)S(1)}, f32[8,128]{1,0:T(8,128)S(1)}, f32[3,3,5,24,128]{4,3,2,1,0:T(8,128)S(1)}, f32[12,24,128]{2,1,0:T(8,128)S(1)}) custom-call(f32[12,56,384]{2,1,0:T(8,128)S(1)} %get-tuple-element.34.v_ref, f32[3,3,4,24,128]{4,3,2,1,0:T(8,128)S(1)} %get-tuple-element.35.nodes_in, ...), custom_call_target="tpu_custom_call" | custom-call | flops 10000000 | bytes 1000000 | tf_op jit(solution)/shard_map/pallas_call | solution.py:729
  20.7 0.6 collective-permute-start.8
  21.3 3.1 %collective-permute-done.8 = f32[8,128]{1,0:T(8,128)S(1)} collective-permute-done((f32[8,128]{1,0:T(8,128)S(1)}, f32[8,128]{1,0:T(8,128)S(1)}, u32[]{:S(2)}, u32[]{:S(2)}) %collective-permute-start.8) | collective-permute-done | bytes 4128 | tf_op jit(solution)/shard_map/ppermute | solution.py:746
  24.4 7.9 %collective-permute-start.9 = (f32[8,128]{1,0:T(8,128)S(1)}, f32[8,128]{1,0:T(8,128)S(1)}, u32[]{:S(2)}, u32[]{:S(2)}) collective-permute-start(f32[8,128]{1,0:T(8,128)S(1)} %add.18), channel_id=1, source_target_pairs={{0,2},{1,3},{2,0},{3,1},{4,6},{5,7},{6,4},{7,5},{8,10},{9,11},{10,... | collective-permute-start | bytes 12296 | tf_op jit(solution)/shard_map/ppermute | solution.py:746
  32.3 0.8 %collective-permute-done.9 = f32[8,128]{1,0:T(8,128)S(1)} collective-permute-done((f32[8,128]{1,0:T(8,128)S(1)}, f32[8,128]{1,0:T(8,128)S(1)}, u32[]{:S(2)}, u32[]{:S(2)}) %collective-permute-start.9) | collective-permute-done | bytes 4128 | tf_op jit(solution)/shard_map/ppermute | solution.py:746
  33.2 3.1 %collective-permute-start.10 = (f32[8,128]{1,0:T(8,128)S(1)}, f32[8,128]{1,0:T(8,128)S(1)}, u32[]{:S(2)}, u32[]{:S(2)}) collective-permute-start(f32[8,128]{1,0:T(8,128)S(1)} %add.19), channel_id=1, source_target_pairs={{0,4},{1,5},{2,6},{3,7},{4,0},{5,1},{6,2},{7,3},{8,12},{9,13},{10,... | collective-permute-start | bytes 12296 | tf_op jit(solution)/shard_map/ppermute | solution.py:746
  36.3 1.6 %collective-permute-done.10 = f32[8,128]{1,0:T(8,128)S(1)} collective-permute-done((f32[8,128]{1,0:T(8,128)S(1)}, f32[8,128]{1,0:T(8,128)S(1)}, u32[]{:S(2)}, u32[]{:S(2)}) %collective-permute-start.10) | collective-permute-done | bytes 4128 | tf_op jit(solution)/shard_map/ppermute | solution.py:746
  37.8 7.2 %collective-permute-start.13 = (f32[8,128]{1,0:T(8,128)S(1)}, f32[8,128]{1,0:T(8,128)S(1)}, u32[]{:S(2)}, u32[]{:S(2)}) collective-permute-start(f32[8,128]{1,0:T(8,128)S(1)} %add.20), channel_id=1, source_target_pairs={{0,24},{1,25},{2,26},{3,27},{4,28},{5,29},{6,30},{7,31},{8,16},{9,... | collective-permute-start | bytes 12296 | tf_op jit(solution)/shard_map/ppermute | solution.py:746
  45.0 0.0 collective-permute-start.12
  45.1 0.6 collective-permute-start.11
  45.6 1.0 %collective-permute-done.13 = f32[8,128]{1,0:T(8,128)S(1)} collective-permute-done((f32[8,128]{1,0:T(8,128)S(1)}, f32[8,128]{1,0:T(8,128)S(1)}, u32[]{:S(2)}, u32[]{:S(2)}) %collective-permute-start.13) | collective-permute-done | bytes 4128 | tf_op jit(solution)/shard_map/ppermute | solution.py:746
  46.6 2.9 %collective-permute-done.12 = f32[8,128]{1,0:T(8,128)S(1)} collective-permute-done((f32[8,128]{1,0:T(8,128)S(1)}, f32[8,128]{1,0:T(8,128)S(1)}, u32[]{:S(2)}, u32[]{:S(2)}) %collective-permute-start.12) | collective-permute-done | bytes 4128 | tf_op jit(solution)/shard_map/ppermute | solution.py:746
  49.6 0.0 collective-permute-done.11
  49.6 0.0 collective-permute-done.6.near
  49.6 0.0 collective-permute-done.7.far
  49.6 0.0 copy-start
  49.6 0.0 copy-start.1
  49.6 2.7 %shard_map.80 = (f32[3,12,56,384]{3,2,1,0:T(8,128)S(1)}, f32[3,3,2,24,128]{4,3,2,1,0:T(8,128)S(1)}, f32[3,24,128]{2,1,0:T(8,128)S(1)}) custom-call(f32[3,12,56,384]{3,2,1,0:T(8,128)S(1)} %get-tuple-element.38.gg, f32[12,24,128]{2,1,0:T(8,128)S(1)} %get-tuple-element.39.energy, f32[3,3,5,24,128]{4,3,2,1,0:T(8,128)S(1)} %get-tuple-element.37.nodes_ref, ...), custom_call_target="tpu_custom_call" | custom-call | flops 10000000 | bytes 1000000 | tf_op jit(solution)/shard_map/pallas_call | solution.py:729
  52.3 2.5 %shard_map.82 = (f32[12,48,384]{2,1,0:T(8,128)}, f32[3]{0:T(128)}) custom-call(f32[8,128]{1,0:T(8,128)S(1)} %add_add_fusion.part, f32[3,12,56,384]{3,2,1,0:T(8,128)S(1)} %get-tuple-element.46.summed), custom_call_target="tpu_custom_call" | custom-call | flops 10000000 | bytes 1000000 | tf_op jit(solution)/shard_map/pallas_call | solution.py:729
  54.8 0.0 copy-done
  54.8 0.0 copy-done.1
  54.8 2.4 %shard_map.81 = f32[3,3,4,16,128]{4,3,2,1,0:T(8,128)} custom-call(f32[3,3,5,24,128]{4,3,2,1,0:T(8,128)S(1)} %get-tuple-element.37.nodes_ref, f32[3,3,2,24,128]{4,3,2,1,0:T(8,128)S(1)} %get-tuple-element.42.extra, f32[12,24,128]{2,1,0:T(8,128)S(1)} %get-tuple-element.43.moduli, f32[3,24,128]{2,1,0:T(8,128)S(1)} %get-tuple-element.44.moduli_below, ...), custom_call_target="tpu_custom_call" | custom-call | flops 10000000 | bytes 1000000 | tf_op jit(solution)/shard_map/pallas_call | solution.py:729
  (4 shorter events, 0.0 us)
Async XLA Ops:
  2.0 10.8 %collective-permute-start = (f32[4,48,384]{2,1,0:T(8,128)S(1)}, f32[4,48,384]{2,1,0:T(8,128)S(1)}, u32[]{:S(2)}, u32[]{:S(2)}) collective-permute-start(f32[4,48,384]{2,1,0:T(8,128)S(1)} %get-tuple-element.29), channel_id=1, source_target_pairs={{0,2},{1,3},{2,0},{3,1},{4,6},{5,7},{6,4},{7,5},{8,10},{9,11},{10,... | collective-permute-start | bytes 884744 | tf_op jit(solution)/shard_map/ppermute | solution.py:777
  2.5 10.2 %collective-permute-start.1 = (f32[3,48,384]{2,1,0:T(8,128)S(1)}, f32[3,48,384]{2,1,0:T(8,128)S(1)}, u32[]{:S(2)}, u32[]{:S(2)}) collective-permute-start(f32[3,48,384]{2,1,0:T(8,128)S(1)} %get-tuple-element.30), channel_id=1, source_target_pairs={{2,4},{3,5},{4,2},{5,3},{6,8},{7,9},{8,6},{9,7},{10,12},{11,13},{1... | collective-permute-start | bytes 663560 | tf_op jit(solution)/shard_map/ppermute | solution.py:777
  3.2 9.5 %collective-permute-start.2 = (f32[136,384]{1,0:T(8,128)S(1)}, f32[136,384]{1,0:T(8,128)S(1)}, u32[]{:S(2)}, u32[]{:S(2)}) collective-permute-start(f32[136,384]{1,0:T(8,128)S(1)} %get-tuple-element.31), channel_id=1, source_target_pairs={{0,1},{2,3},{4,5},{6,7},{8,9},{10,11},{12,13},{14,15},{16,17},{18,... | collective-permute-start | bytes 626696 | tf_op jit(solution)/shard_map/ppermute | solution.py:777
  5.8 6.9 %collective-permute-start.3 = (f32[24,384]{1,0:T(8,128)S(1)}, f32[24,384]{1,0:T(8,128)S(1)}, u32[]{:S(2)}, u32[]{:S(2)}) collective-permute-start(f32[24,384]{1,0:T(8,128)S(1)} %get-tuple-element.32), channel_id=1, source_target_pairs={{0,3},{2,1},{4,7},{6,5},{8,11},{10,9},{12,15},{14,13},{16,19},{18,... | collective-permute-start | bytes 110600 | tf_op jit(solution)/shard_map/ppermute | solution.py:777
  8.4 4.3 %collective-permute-start.4 = (f32[24,384]{1,0:T(8,128)S(1)}, f32[24,384]{1,0:T(8,128)S(1)}, u32[]{:S(2)}, u32[]{:S(2)}) collective-permute-start(f32[24,384]{1,0:T(8,128)S(1)} %get-tuple-element.33), channel_id=1, source_target_pairs={{2,5},{4,3},{6,9},{8,7},{10,13},{12,11},{14,17},{16,15},{18,21},{2... | collective-permute-start | bytes 110600 | tf_op jit(solution)/shard_map/ppermute | solution.py:777
  15.0 34.6 %collective-permute-start.6 = (f32[240,384]{1,0:T(8,128)S(1)}, f32[240,384]{1,0:T(8,128)S(1)}, u32[]{:S(2)}, u32[]{:S(2)}) collective-permute-start(f32[240,384]{1,0:T(8,128)S(1)} %get-tuple-element.40), channel_id=1, source_target_pairs={{0,2},{1,3},{2,0},{3,1},{4,6},{5,7},{6,4},{7,5},{8,10},{9,11},{10,... | collective-permute-start | bytes 1105928 | tf_op jit(solution)/shard_map/ppermute | solution.py:777
  16.9 32.6 %collective-permute-start.7 = (f32[240,384]{1,0:T(8,128)S(1)}, f32[240,384]{1,0:T(8,128)S(1)}, u32[]{:S(2)}, u32[]{:S(2)}) collective-permute-start(f32[240,384]{1,0:T(8,128)S(1)} %get-tuple-element.41), channel_id=1, source_target_pairs={{2,4},{3,5},{4,2},{5,3},{6,8},{7,9},{8,6},{9,7},{10,12},{11,13},{1... | collective-permute-start | bytes 1105928 | tf_op jit(solution)/shard_map/ppermute | solution.py:777
  17.6 0.7 %collective-permute-start.5 = (f32[48,384]{1,0:T(8,128)S(1)}, f32[48,384]{1,0:T(8,128)S(1)}, u32[]{:S(2)}, u32[]{:S(2)}) collective-permute-start(f32[48,384]{1,0:T(8,128)S(1)} %get-tuple-element.36), channel_id=1, source_target_pairs={{4,2},{5,3},{8,6},{9,7},{12,10},{13,11},{16,14},{17,15},{20,18},{2... | collective-permute-start | bytes 221192 | tf_op jit(solution)/shard_map/ppermute | solution.py:777
  20.7 3.7 %collective-permute-start.8 = (f32[8,128]{1,0:T(8,128)S(1)}, f32[8,128]{1,0:T(8,128)S(1)}, u32[]{:S(2)}, u32[]{:S(2)}) collective-permute-start(f32[8,128]{1,0:T(8,128)S(1)} %get-tuple-element.45), channel_id=1, source_target_pairs={{0,1},{1,0},{2,3},{3,2},{4,5},{5,4},{6,7},{7,6},{8,9},{9,8},{10,11... | collective-permute-start | bytes 12296 | tf_op jit(solution)/shard_map/ppermute | solution.py:746
  24.4 8.8 %collective-permute-start.9 = (f32[8,128]{1,0:T(8,128)S(1)}, f32[8,128]{1,0:T(8,128)S(1)}, u32[]{:S(2)}, u32[]{:S(2)}) collective-permute-start(f32[8,128]{1,0:T(8,128)S(1)} %add.18), channel_id=1, source_target_pairs={{0,2},{1,3},{2,0},{3,1},{4,6},{5,7},{6,4},{7,5},{8,10},{9,11},{10,... | collective-permute-start | bytes 12296 | tf_op jit(solution)/shard_map/ppermute | solution.py:746
  33.2 4.7 %collective-permute-start.10 = (f32[8,128]{1,0:T(8,128)S(1)}, f32[8,128]{1,0:T(8,128)S(1)}, u32[]{:S(2)}, u32[]{:S(2)}) collective-permute-start(f32[8,128]{1,0:T(8,128)S(1)} %add.19), channel_id=1, source_target_pairs={{0,4},{1,5},{2,6},{3,7},{4,0},{5,1},{6,2},{7,3},{8,12},{9,13},{10,... | collective-permute-start | bytes 12296 | tf_op jit(solution)/shard_map/ppermute | solution.py:746
  37.8 8.8 %collective-permute-start.13 = (f32[8,128]{1,0:T(8,128)S(1)}, f32[8,128]{1,0:T(8,128)S(1)}, u32[]{:S(2)}, u32[]{:S(2)}) collective-permute-start(f32[8,128]{1,0:T(8,128)S(1)} %add.20), channel_id=1, source_target_pairs={{0,24},{1,25},{2,26},{3,27},{4,28},{5,29},{6,30},{7,31},{8,16},{9,... | collective-permute-start | bytes 12296 | tf_op jit(solution)/shard_map/ppermute | solution.py:746
  45.0 4.5 %collective-permute-start.12 = (f32[8,128]{1,0:T(8,128)S(1)}, f32[8,128]{1,0:T(8,128)S(1)}, u32[]{:S(2)}, u32[]{:S(2)}) collective-permute-start(f32[8,128]{1,0:T(8,128)S(1)} %add.20), channel_id=1, source_target_pairs={{0,16},{1,17},{2,18},{3,19},{4,20},{5,21},{6,22},{7,23},{8,24},{9,... | collective-permute-start | bytes 12296 | tf_op jit(solution)/shard_map/ppermute | solution.py:746
  45.1 4.5 %collective-permute-start.11 = (f32[8,128]{1,0:T(8,128)S(1)}, f32[8,128]{1,0:T(8,128)S(1)}, u32[]{:S(2)}, u32[]{:S(2)}) collective-permute-start(f32[8,128]{1,0:T(8,128)S(1)} %add.20), channel_id=1, source_target_pairs={{0,8},{1,9},{2,10},{3,11},{4,12},{5,13},{6,14},{7,15},{8,0},{9,1},... | collective-permute-start | bytes 12296 | tf_op jit(solution)/shard_map/ppermute | solution.py:746
  49.6 5.2 %copy-start = (s32[4,16,128]{2,1,0:T(8,128)S(1)}, s32[4,16,128]{2,1,0:T(8,128)}, u32[]{:S(2)}) copy-start(s32[4,16,128]{2,1,0:T(8,128)} %support.3) | copy-start | bytes 98308
  49.6 5.2 %copy-start.1 = (s32[4,16,128]{2,1,0:T(8,128)S(1)}, s32[4,16,128]{2,1,0:T(8,128)}, u32[]{:S(2)}) copy-start(s32[4,16,128]{2,1,0:T(8,128)} %loading.1) | copy-start | bytes 98308

commit v3 on v2

--- a/solution.py
+++ b/solution.py
@@ -210,7 +210,7 @@
 ):
     rows, cols, depth = design.shape
     cx, cy, _ = support.shape
-    sides, (edges, masks, moves, frees, sems) = rest[: 3 * len(kinds)], rest[3 * len(kinds) :]
+    sides, (edges, masks, moves, frees, sems) = rest[: 2 * len(kinds)], rest[2 * len(kinds) :]
     groups = lane_groups(depth)
     n = lax.axis_index("narrow")
     even = lax.rem(lax.axis_index("wide"), 2) == 0
@@ -255,7 +255,7 @@
         copy.wait()
 
     for index, kind in enumerate(kinds):
-        side, side_near, side_far = sides[3 * index : 3 * index + 3]
+        side, side_far = sides[2 * index : 2 * index + 2]
         for k in range(rows):
             value = edges[index, k]
             piece = pick(n, value[8 - REACH :], value[:REACH], kind)
@@ -263,10 +263,9 @@
             value = 1.0 - masks[index, k].astype(jnp.float32)
             side[pl.ds(rows * REACH + k * RAD, RAD), :] = pick(n, value[8 - RAD :], value[:RAD], kind)
         for k in range(RAD):
-            for ref, start in ((side_near, near_start), (side_far, far_start)):
-                value = edges[index, start + k]
-                piece = pick(n, value[8 - REACH :], value[:REACH], kind)
-                ref[pl.ds(k * REACH, REACH), :] = piece
+            value = edges[index, far_start + k]
+            piece = pick(n, value[8 - REACH :], value[:REACH], kind)
+            side_far[pl.ds(k * REACH, REACH), :] = piece
         base = rows * (REACH + RAD)
         for r in range(3):
             for c in range(3):
@@ -275,10 +274,8 @@
                     piece = pick(n, value[cy - 1 : cy + 1], value[1:3], kind)
                     side[pl.ds(base + (r * cx + x) * 2, 2), groups[c]] = piece
                     if x == 0:
-                        side_near[pl.ds(RAD * REACH + 2 * r, 2), groups[c]] = piece
                         side_far[pl.ds(RAD * REACH + 2 * r, 2), groups[c]] = piece
         fill_tail(side, base + 6 * cx)
-        fill_tail(side_near, RAD * REACH + 6)
         fill_tail(side_far, RAD * REACH + 6)
     for copy in copies[last:]:
         copy.wait()
@@ -390,9 +387,13 @@
     for index, ref in ((above, near), (1 - above, far)):
         for k in range(RAD):
             ends[index, k] = ref[k]
-    for index, pair in ((above, (near_b, near_a)), (1 - above, (far_b, far_a))):
-        for which, ref in enumerate(pair):
-            corners[which, index] = ref[...] * (valid_b, valid_a)[which]
+    reach = RAD * REACH
+    last = (rows - RAD) * REACH
+    for which, (one, other) in enumerate(((near_b, far_b), (near_a, far_a))):
+        valid = (valid_b, valid_a)[which]
+        piece = jnp.where(above == 1, one[:reach], one[last : last + reach])
+        corners[which, above, :reach] = piece * valid
+        corners[which, 1 - above, :reach] = other[:reach] * valid
 
     base = rows * (REACH + RAD)
     for r in range(3):
@@ -475,10 +476,14 @@
     even = lax.rem(w, 2) == 0
     valid = (jnp.where(n > 0, 1.0, 0.0), jnp.where(n < n_narrow - 1, 1.0, 0.0))
     for which, (one, other) in enumerate(((near_b, far_b), (near_a, far_a))):
-        corners[which] = jnp.where(even, one[...], other[...]) * valid[which]
+        for r in range(3):
+            here = rows * (REACH + RAD) + r * cx * 2
+            there = RAD * REACH + 2 * r
+            piece = jnp.where(even, one[here : here + 2], other[there : there + 2])
+            corners[which, 2 * r : 2 * r + 2] = piece * valid[which]
     for r in range(3):
         span = slice(r * cy, (r + 1) * cy)
-        at = RAD * REACH + 2 * r
+        at = 2 * r
         for c in range(3):
             lanes = groups[c]
             for x in range(cx):
@@ -528,7 +533,8 @@
             moduli_ref[at] = value
             term = value * energy[at]
             partial = term if partial is None else partial + term
-        part_ref[r : r + 1, :] = jnp.sum(partial * own, axis=0, keepdims=True)
+        summed = jnp.sum(jnp.sum(partial * own, axis=0, keepdims=True), axis=1, keepdims=True)
+        part_ref[r : r + 1, :] = jnp.broadcast_to(summed, (1, LANES))
 
 
 def nodal_rows(nodes, moduli, cx, first, lane):
@@ -568,12 +574,13 @@
     )
 
 
-def fields_kernel(
-    n_wide, n_narrow, gg, energy, nodes_ref, near, far,
-    summed_ref, extra_ref, moduli_ref, outer, spread_ref, packed, cubes, packed_outer,
+def outer_kernel(
+    n_wide, n_narrow, energy, nodes_ref, near, far,
+    outer, spread_ref, force_ref, extra_ref, packed, cubes, packed_outer,
 ):
-    _, rows, ext, depth = gg.shape
-    cx = rows // 3
+    _, _, ext, depth = outer.shape
+    cx = nodes_ref.shape[2] - 1
+    rows = 3 * cx
     cols = 3 * ((ext - 2 * RAD) // 3)
     padded = energy.shape[1]
     reach = ext // 3
@@ -642,9 +649,21 @@
     sub_id = lax.broadcasted_iota(jnp.int32, (padded, LANES), 0)
     last = jnp.where(w > 0, reach, 0)
     keep = (sub_id > jnp.where(n > 0, -1, 0)) & (sub_id < last)
-    for r in range(3):
-        moduli_ref[r] = modulus_of(sums[r * padded : (r + 1) * padded], r, keep)
-
+    cy = cols // 3
+    for r in range(3):
+        modulus = modulus_of(sums[r * padded : (r + 1) * padded], r, keep)
+        nodes = lambda c, x: extra_ref[r, c, 0] if x < 0 else nodes_ref[r, c, x]
+        for x, sums_at, below in nodal_rows(nodes, lambda x: modulus, 0, -1, lane):
+            if x == 0:
+                for comp in range(3):
+                    total = nodal_total(sums_at, below, comp, lane)
+                    force_ref[r, comp] = total[1 : cy + 1]
+
+
+def fields_kernel(gg, outer, spread_ref, summed_ref):
+    _, rows, ext, depth = gg.shape
+    coarse = rows // 3 + 2
+    groups = lane_groups(depth)
     for r in range(3):
         def first_dim(s, carry):
             place = pl.ds(pl.multiple_of(8 * s, 8), 8)
@@ -667,14 +686,13 @@
         lax.fori_loop(0, ext // 8, first_dim, 0)
 
 
-def force_kernel(nodes_ref, extra, moduli, moduli_below, support, loading, residual_ref):
+def force_kernel(nodes_ref, moduli, support, loading, residual_ref):
     cx, cy, _ = support.shape
     lane = lax.broadcasted_iota(jnp.int32, nodes_ref.shape[3:], 1)
     for r in range(3):
-        nodes = lambda c, x: extra[r, c, 0] if x < 0 else nodes_ref[r, c, x]
-        modulus = lambda x: moduli_below[r] if x < 0 else moduli[r * cx + x]
-        for x, sums, below in nodal_rows(nodes, modulus, cx, -1, lane):
-            if 0 <= x < cx:
+        nodes = lambda c, x: nodes_ref[r, c, x]
+        for x, sums, below in nodal_rows(nodes, lambda x: moduli[r * cx + x], cx, 0, lane):
+            if x < cx:
                 free = 1.0 - support[x].astype(jnp.float32)
                 for comp in range(3):
                     total = nodal_total(sums, below, comp, lane)[1 : cy + 1]
@@ -683,24 +701,27 @@
                     residual_ref[r, comp, x] = -total * free
 
 
-def realization_factors(part, shape):
-    factors, totals = [], []
-    for r in range(3):
-        total = jnp.sum(part[r : r + 1, :], axis=1, keepdims=True)
-        factor = 3.0 * (1.0 - stiff_floor) / 27.0 * sharpness / DENOM[r] ** 3
-        factors.append(jnp.broadcast_to(-factor / total, shape))
-        totals.append(total)
-    return factors, totals
-
-
-def final_kernel(part, summed, out_ref, compliance_ref):
+def final_kernel(
+    part, summed, residual, force, support, out_hbm, residual_hbm, compliance_ref, out_ref, row,
+    sems,
+):
     rows, cols, depth = out_ref.shape
     groups = lane_groups(depth)
-    factors, totals = realization_factors(part, (1, LANES))
-    for r in range(3):
-        compliance_ref[r] = jnp.sum(totals[r])
-
-    def other_dims(step, carry):
+    free = 1.0 - support[0].astype(jnp.float32)
+    for r in range(3):
+        for comp in range(3):
+            row[r, comp, 0] = residual[r, comp, 0] - force[r, comp] * free
+    copies = [
+        pltpu.make_async_copy(residual.at[:, :, 1:], residual_hbm.at[:, :, 1:], sems.at[0]),
+        pltpu.make_async_copy(row, residual_hbm.at[:, :, :1], sems.at[1]),
+    ]
+    for copy in copies:
+        copy.start()
+    factors = []
+    for r in range(3):
+        factor = 3.0 * (1.0 - stiff_floor) / 27.0 * sharpness / DENOM[r] ** 3
+        factors.append(-factor / part[r : r + 1, :])
+    for step in range(rows // 3):
         for sub in range(3):
             k = 3 * step + sub
             parts = []
@@ -712,13 +733,18 @@
                 parts.append(tent_sublanes(total, cols))
             for lanes, value in zip(groups, tent_lanes(parts)):
                 out_ref[k, :, lanes] = value
-        return carry
-
-    for step in range(rows // 3):
-        other_dims(step, 0)
-
-
-def call(kernel, shapes, scratch, flops, args, hbm=0, scalars=(), limit=20):
+        place = pl.ds(3 * step, 3)
+        copies.append(
+            pltpu.make_async_copy(out_ref.at[place], out_hbm.at[place], sems.at[2 + step])
+        )
+        copies[-1].start()
+    for r in range(3):
+        compliance_ref[r] = jnp.max(part[r : r + 1, :1])
+    for copy in copies:
+        copy.wait()
+
+
+def call(kernel, shapes, scratch, flops, args, hbm=0, scalars=(), limit=20, out_hbm=0):
     vmem = pl.BlockSpec(memory_space=pltpu.VMEM)
     smem = pl.BlockSpec(memory_space=pltpu.SMEM)
     scratch = [pltpu.VMEM(s, jnp.float32) if isinstance(s, tuple) else s for s in scratch]
@@ -730,7 +756,8 @@
         kernel,
         out_shape=[jax.ShapeDtypeStruct(s, jnp.float32) for s in list(shapes) + list(scalars)],
         in_specs=[pl.BlockSpec(memory_space=pltpu.HBM)] * hbm + [vmem] * (len(args) - hbm),
-        out_specs=[vmem] * len(shapes) + [smem] * len(scalars),
+        out_specs=[pl.BlockSpec(memory_space=pltpu.HBM)] * out_hbm
+        + [vmem] * (len(shapes) - out_hbm) + [smem] * len(scalars),
         scratch_shapes=scratch,
         compiler_params=pltpu.CompilerParams(vmem_limit_bytes=limit * 1024 * 1024),
         cost_estimate=pl.CostEstimate(flops=flops, bytes_accessed=1000000, transcendentals=0),
@@ -787,7 +814,7 @@
     packs = call(
         functools.partial(pack_kernel, kinds),
         [(RAD + 1, cols, depth), ends, (3 * cy, depth), nodes_shape]
-        + [(ceil8(rows * (REACH + RAD) + 6 * cx), depth), corner, corner] * sides,
+        + [(ceil8(rows * (REACH + RAD) + 6 * cx), depth), corner] * sides,
         [
             (sides, rows, 8, depth), ints(sides, rows, 8, depth), displacement.shape,
             ints(*support.shape), pltpu.SemaphoreType.DMA((4 + 2 * sides,)),
@@ -797,12 +824,9 @@
     far = send(packs[1], route("far", 0))
     got = []
     for index in range(sides):
-        side, side_near, side_far = packs[4 + 3 * index : 7 + 3 * index]
-        got.append((
-            send(side, side_route("self", index)),
-            send(side_near, side_route("near", index)),
-            send(side_far, side_route("far", index)),
-        ))
+        side, side_far = packs[4 + 2 * index : 6 + 2 * index]
+        side = send(side, side_route("self", index))
+        got.append((side, send(side, route("near", 0)), send(side_far, side_route("far", index))))
     near = send(packs[0], route("near", 0))
     row = send(packs[2], route("down", 0))
     own_design, own_mask = call(
@@ -837,25 +861,28 @@
     total = n_wide * n_narrow
     steps = [1 << bit for bit in range(total.bit_length() - 1)]
     groups = [(s,) for s in steps[:-2]] + [(steps[-2], steps[-1], steps[-2] + steps[-1])]
-    fields, extra, moduli_below = call(
-        functools.partial(fields_kernel, n_wide, n_narrow),
-        [(3, rows, ext, depth), (3, 3, 2, padded, cz), (3, padded, cz)],
-        [
-            (3, 2 * RAD, ext, depth), (3 * (cx + 2), depth // LANES, ext, LANES),
-            (3 * (cx + 2), padded, LANES), (RAD, 6, depth // LANES, ext, LANES),
-            (3 * padded, LANES),
-        ],
-        10000000, (gg, energy, nodes, v_near, v_far),
-    )
     (residual,) = call(
         force_kernel, [displacement.shape], [], 10000000,
-        (nodes, extra, moduli, moduli_below, support, loading),
+        (nodes, moduli, support, loading),
     )
+    spread_shape = (3 * (cx + 2), depth // LANES, ext, LANES)
+    outer_rows, spread, force = call(
+        functools.partial(outer_kernel, n_wide, n_narrow),
+        [(3, 2 * RAD, ext, depth), spread_shape, (3, 3, cy, cz)],
+        [
+            (3, 3, 2, padded, cz), (3 * (cx + 2), padded, LANES),
+            (RAD, 6, depth // LANES, ext, LANES), (3 * padded, LANES),
+        ],
+        10000000, (energy, nodes, v_near, v_far),
+    )
+    (fields,) = call(fields_kernel, [(3, rows, ext, depth)], [], 10000000, (gg, outer_rows, spread))
     summed = part
     for group in groups:
         summed = exchange_sum(summed, total, group)
-    sensitivity, compliance = call(
-        final_kernel, [design.shape], [], 10000000, (summed, fields), scalars=[(3,)],
+    sensitivity, residual, compliance = call(
+        final_kernel, [design.shape, displacement.shape],
+        [design.shape, (3, 3, 1, cy, cz), pltpu.SemaphoreType.DMA((2 + rows // 3,))], 10000000,
+        (summed, fields, residual, force, support), scalars=[(3,)], out_hbm=2,
     )
     return residual, compliance, sensitivity
 

time: 57.5 us -> 57.5 us (level)
  starting transfers between devices: 29.8 us -> 30.5 us
    ppermute x6, waiting for transfers between devices: 9.45 us -> 6.71 us  [exchange_sum(): lax.ppermute(value, axes, [(i, i ^ k) for i in range(total)])]
    ppermute x8, waiting for transfers between devices: 2.17 us -> 4.51 us  [send(): return lax.ppermute(block, axes, pairs)]
    ppermute x6, starting transfers between devices: 19.4 us -> 20.2 us  [exchange_sum(): lax.ppermute(value, axes, [(i, i ^ k) for i in range(total)])]
    pallas_call x7 -> x8, Pallas kernels: 15.1 us -> 14.8 us  [call(): pl.pallas_call(kernel, out_shape=[jax.ShapeDtypeStruct(s, jnp.float32) fo...]
  transfers between devices with their start and end apart: 14 -> 14, of which waited for: 6 -> 5; matrix products, arithmetic and copies ran while one was open for 0% -> 0% of each run, Pallas kernels for 7% -> 10%
where the time goes in v3:
time: 57.5 us; the launch traced here: 57.3 us
  starting transfers between devices  30.5 us (53%)
  Pallas kernels  14.8 us (26%)
  waiting for transfers between devices  11.2 us (19%)
  between operations  0.78 us (1%)
    ppermute x6, starting transfers between devices, exchange_sum(): lax.ppermute(value, axes, [(i, i ^ k) for i in range(total)])  20.2 us
    pallas_call x8, Pallas kernels, call(): pl.pallas_call(kernel, out_shape=[jax.ShapeDtypeStruct(s, jnp.float32) fo...  14.8 us
    ppermute x8, starting transfers between devices, send(): return lax.ppermute(block, axes, pairs)  10.3 us
    ppermute x6, waiting for transfers between devices, exchange_sum(): lax.ppermute(value, axes, [(i, i ^ k) for i in range(total)])  6.71 us
    ppermute x8, waiting for transfers between devices, send(): return lax.ppermute(block, axes, pairs)  4.51 us
  transfers between devices with their start and end apart: 14, of which 5 were waited for; matrix products, arithmetic and copies ran while one was open for 0% of the time, Pallas kernels for 10%

profile of v3, /device:TPU:0, one launch (start us, length us, event | category | flops | bytes accessed | tf_op | source)
XLA Modules:
  0.0 57.3 jit_solution(17234228479181289210)
XLA Ops:
  0.6 1.3 %shard_map.77 = (f32[4,48,384]{2,1,0:T(8,128)S(1)}, f32[3,48,384]{2,1,0:T(8,128)S(1)}, f32[48,384]{1,0:T(8,128)S(1)}, f32[3,3,4,24,128]{4,3,2,1,0:T(8,128)S(1)},...) custom-call(f32[12,48,384]{2,1,0:T(8,128)} %design.1, s32[12,48,384]{2,1,0:T(8,128)} %passive.1, ...), custom_call_target="tpu_custom_call" | custom-call | flops 200000 | bytes 1000000 | tf_op jit(solution)/shard_map/pallas_call | solution.py:755
  2.0 3.1 %collective-permute-start.2 = (f32[136,384]{1,0:T(8,128)S(1)}, f32[136,384]{1,0:T(8,128)S(1)}, u32[]{:S(2)}, u32[]{:S(2)}) collective-permute-start(f32[136,384]{1,0:T(8,128)S(1)} %get-tuple-element.31), channel_id=1, source_target_pairs={{0,1},{2,3},{4,5},{6,7},{8,9},{10,11},{12,13},{14,15},{16,17},{18,... | collective-permute-start | bytes 626696 | tf_op jit(solution)/shard_map/ppermute | solution.py:804
  5.0 0.0 collective-permute-start
  5.0 0.7 %collective-permute-start.1 = (f32[3,48,384]{2,1,0:T(8,128)S(1)}, f32[3,48,384]{2,1,0:T(8,128)S(1)}, u32[]{:S(2)}, u32[]{:S(2)}) collective-permute-start(f32[3,48,384]{2,1,0:T(8,128)S(1)} %get-tuple-element.30), channel_id=1, source_target_pairs={{2,4},{3,5},{4,2},{5,3},{6,8},{7,9},{8,6},{9,7},{10,12},{11,13},{1... | collective-permute-start | bytes 663560 | tf_op jit(solution)/shard_map/ppermute | solution.py:804
  5.7 4.5 %collective-permute-done.2.side_b.side_a = f32[136,384]{1,0:T(8,128)S(1)} collective-permute-done((f32[136,384]{1,0:T(8,128)S(1)}, f32[136,384]{1,0:T(8,128)S(1)}, u32[]{:S(2)}, u32[]{:S(2)}) %collective-permute-start.2) | collective-permute-done | bytes 208928 | tf_op jit(solution)/shard_map/ppermute | solution.py:804
  10.2 0.0 collective-permute-start.3
  10.2 0.7 %collective-permute-start.4 = (f32[24,384]{1,0:T(8,128)S(1)}, f32[24,384]{1,0:T(8,128)S(1)}, u32[]{:S(2)}, u32[]{:S(2)}) collective-permute-start(f32[24,384]{1,0:T(8,128)S(1)} %get-tuple-element.32), channel_id=1, source_target_pairs={{2,5},{4,3},{6,9},{8,7},{10,13},{12,11},{14,17},{16,15},{18,21},{2... | collective-permute-start | bytes 110600 | tf_op jit(solution)/shard_map/ppermute | solution.py:804
  10.8 1.5 %shard_map.76 = (f32[12,48,384]{2,1,0:T(8,128)S(1)}, f32[12,56,384]{2,1,0:T(8,128)S(1)}) custom-call(f32[12,48,384]{2,1,0:T(8,128)} %design.1, s32[12,48,384]{2,1,0:T(8,128)} %passive.1), custom_call_target="tpu_custom_call" | custom-call | flops 200000 | bytes 1000000 | tf_op jit(solution)/shard_map/pallas_call | solution.py:755
  12.3 0.0 copy-start
  12.3 0.0 copy-start.1
  12.3 0.0 collective-permute-done.4.far_b.far_a
  12.3 0.0 collective-permute-done.1.far
  12.4 0.0 collective-permute-done.near
  12.4 0.0 collective-permute-done.3.near_b.near_a
  12.4 2.3 %shard_map.78 = (f32[12,56,384]{2,1,0:T(8,128)S(1)}, f32[3,3,4,24,128]{4,3,2,1,0:T(8,128)S(1)}, f32[240,384]{1,0:T(8,128)S(1)}, f32[240,384]{1,0:T(8,128)S(1)}) custom-call(f32[12,48,384]{2,1,0:T(8,128)S(1)} %get-tuple-element.26.design, f32[12,56,384]{2,1,0:T(8,128)S(1)} %get-tuple-element.27.mask_in, f32[3,3,4,24,128]{4,3,2,1,0:T(8,128)S(1)} %get-tuple-element.28.nodes_in, ...), custom_call_target="tpu_custom_call" | custom-call | flops 10000000 | bytes 1000000 | tf_op jit(solution)/shard_map/pallas_call | solution.py:755
  14.7 4.6 %collective-permute-start.12 = (f32[240,384]{1,0:T(8,128)S(1)}, f32[240,384]{1,0:T(8,128)S(1)}, u32[]{:S(2)}, u32[]{:S(2)}) collective-permute-start(f32[240,384]{1,0:T(8,128)S(1)} %get-tuple-element.40), channel_id=1, source_target_pairs={{0,2},{1,3},{2,0},{3,1},{4,6},{5,7},{6,4},{7,5},{8,10},{9,11},{10,... | collective-permute-start | bytes 1105928 | tf_op jit(solution)/shard_map/ppermute | solution.py:804
  19.2 0.7 %collective-permute-start.13 = (f32[240,384]{1,0:T(8,128)S(1)}, f32[240,384]{1,0:T(8,128)S(1)}, u32[]{:S(2)}, u32[]{:S(2)}) collective-permute-start(f32[240,384]{1,0:T(8,128)S(1)} %get-tuple-element.41), channel_id=1, source_target_pairs={{2,4},{3,5},{4,2},{5,3},{6,8},{7,9},{8,6},{9,7},{10,12},{11,13},{1... | collective-permute-start | bytes 1105928 | tf_op jit(solution)/shard_map/ppermute | solution.py:804
  19.9 0.7 %collective-permute-start.5 = (f32[48,384]{1,0:T(8,128)S(1)}, f32[48,384]{1,0:T(8,128)S(1)}, u32[]{:S(2)}, u32[]{:S(2)}) collective-permute-start(f32[48,384]{1,0:T(8,128)S(1)} %get-tuple-element.35), channel_id=1, source_target_pairs={{4,2},{5,3},{8,6},{9,7},{12,10},{13,11},{16,14},{17,15},{20,18},{2... | collective-permute-start | bytes 221192 | tf_op jit(solution)/shard_map/ppermute | solution.py:804
  20.6 0.0 collective-permute-done.5.row
  20.6 2.5 %shard_map.79 = (f32[3,12,56,384]{3,2,1,0:T(8,128)S(1)}, f32[12,24,128]{2,1,0:T(8,128)S(1)}, f32[8,128]{1,0:T(8,128)S(1)}, f32[3,3,5,24,128]{4,3,2,1,0:T(8,128)S(1)}, f32[12,24,128]{2,1,0:T(8,128)S(1)}) custom-call(f32[12,56,384]{2,1,0:T(8,128)S(1)} %get-tuple-element.33.v_ref, f32[3,3,4,24,128]{4,3,2,1,0:T(8,128)S(1)} %get-tuple-element.34.nodes_in, ...), custom_call_target="tpu_custom_call" | custom-call | flops 10000000 | bytes 1000000 | tf_op jit(solution)/shard_map/pallas_call | solution.py:755
  23.1 1.7 %collective-permute-start.6 = (f32[8,128]{1,0:T(8,128)S(1)}, f32[8,128]{1,0:T(8,128)S(1)}, u32[]{:S(2)}, u32[]{:S(2)}) collective-permute-start(f32[8,128]{1,0:T(8,128)S(1)} %get-tuple-element.36), channel_id=1, source_target_pairs={{0,1},{1,0},{2,3},{3,2},{4,5},{5,4},{6,7},{7,6},{8,9},{9,8},{10,11... | collective-permute-start | bytes 12296 | tf_op jit(solution)/shard_map/ppermute | solution.py:773
  24.9 1.9 %collective-permute-done.6 = f32[8,128]{1,0:T(8,128)S(1)} collective-permute-done((f32[8,128]{1,0:T(8,128)S(1)}, f32[8,128]{1,0:T(8,128)S(1)}, u32[]{:S(2)}, u32[]{:S(2)}) %collective-permute-start.6) | collective-permute-done | bytes 4128 | tf_op jit(solution)/shard_map/ppermute | solution.py:773
  26.7 8.1 %collective-permute-start.7 = (f32[8,128]{1,0:T(8,128)S(1)}, f32[8,128]{1,0:T(8,128)S(1)}, u32[]{:S(2)}, u32[]{:S(2)}) collective-permute-start(f32[8,128]{1,0:T(8,128)S(1)} %add.18), channel_id=1, source_target_pairs={{0,2},{1,3},{2,0},{3,1},{4,6},{5,7},{6,4},{7,5},{8,10},{9,11},{10,... | collective-permute-start | bytes 12296 | tf_op jit(solution)/shard_map/ppermute | solution.py:773
  34.8 0.8 %collective-permute-done.7 = f32[8,128]{1,0:T(8,128)S(1)} collective-permute-done((f32[8,128]{1,0:T(8,128)S(1)}, f32[8,128]{1,0:T(8,128)S(1)}, u32[]{:S(2)}, u32[]{:S(2)}) %collective-permute-start.7) | collective-permute-done | bytes 4128 | tf_op jit(solution)/shard_map/ppermute | solution.py:773
  35.7 2.6 %collective-permute-start.8 = (f32[8,128]{1,0:T(8,128)S(1)}, f32[8,128]{1,0:T(8,128)S(1)}, u32[]{:S(2)}, u32[]{:S(2)}) collective-permute-start(f32[8,128]{1,0:T(8,128)S(1)} %add.19), channel_id=1, source_target_pairs={{0,4},{1,5},{2,6},{3,7},{4,0},{5,1},{6,2},{7,3},{8,12},{9,13},{10,... | collective-permute-start | bytes 12296 | tf_op jit(solution)/shard_map/ppermute | solution.py:773
  38.3 1.6 %collective-permute-done.8 = f32[8,128]{1,0:T(8,128)S(1)} collective-permute-done((f32[8,128]{1,0:T(8,128)S(1)}, f32[8,128]{1,0:T(8,128)S(1)}, u32[]{:S(2)}, u32[]{:S(2)}) %collective-permute-start.8) | collective-permute-done | bytes 4128 | tf_op jit(solution)/shard_map/ppermute | solution.py:773
  39.9 7.2 %collective-permute-start.11 = (f32[8,128]{1,0:T(8,128)S(1)}, f32[8,128]{1,0:T(8,128)S(1)}, u32[]{:S(2)}, u32[]{:S(2)}) collective-permute-start(f32[8,128]{1,0:T(8,128)S(1)} %add.20), channel_id=1, source_target_pairs={{0,24},{1,25},{2,26},{3,27},{4,28},{5,29},{6,30},{7,31},{8,16},{9,... | collective-permute-start | bytes 12296 | tf_op jit(solution)/shard_map/ppermute | solution.py:773
  47.0 0.0 collective-permute-start.10
  47.0 0.6 collective-permute-start.9
  47.6 0.0 copy-done
  47.6 0.0 copy-done.1
  47.6 1.5 %shard_map.82.residual = f32[3,3,4,16,128]{4,3,2,1,0:T(8,128)S(1)} custom-call(f32[3,3,5,24,128]{4,3,2,1,0:T(8,128)S(1)} %get-tuple-element.39.nodes_ref, f32[12,24,128]{2,1,0:T(8,128)S(1)} %get-tuple-element.44.moduli, s32[4,16,128]{2,1,0:T(8,128)S(1)} %copy-done, s32[4,16,128]{2,1,0:T(8,128)S(1)} %copy-done.1), custom_call_target="tpu_custom_call" | custom-call | flops 10000000 | bytes 1000000 | tf_op jit(solution)/shard_map/pallas_call | solution.py:755
  49.1 0.0 collective-permute-done.11
  49.1 2.4 %collective-permute-done.10 = f32[8,128]{1,0:T(8,128)S(1)} collective-permute-done((f32[8,128]{1,0:T(8,128)S(1)}, f32[8,128]{1,0:T(8,128)S(1)}, u32[]{:S(2)}, u32[]{:S(2)}) %collective-permute-start.10) | collective-permute-done | bytes 4128 | tf_op jit(solution)/shard_map/ppermute | solution.py:773
  51.6 0.0 collective-permute-done.9
  51.6 0.0 collective-permute-done.12.near
  51.6 0.0 collective-permute-done.13.far
  51.6 2.1 %shard_map.80 = (f32[3,6,56,384]{3,2,1,0:T(8,128)S(1)}, f32[18,3,56,128]{3,2,1,0:T(8,128)S(1)}, f32[3,3,16,128]{3,2,1,0:T(8,128)S(1)}) custom-call(f32[12,24,128]{2,1,0:T(8,128)S(1)} %get-tuple-element.38.energy, f32[3,3,5,24,128]{4,3,2,1,0:T(8,128)S(1)} %get-tuple-element.39.nodes_ref, f32[240,384]{1,0:T(8,128)S(1)} %collective-permute-done.12.near, ...), custom_call_target="tpu_custom_call" | custom-call | flops 10000000 | bytes 1000000 | tf_op jit(solution)/shard_map/pallas_call | solution.py:755
  53.7 0.8 %shard_map.81.summed = f32[3,12,56,384]{3,2,1,0:T(8,128)S(1)} custom-call(f32[3,12,56,384]{3,2,1,0:T(8,128)S(1)} %get-tuple-element.37.gg, f32[3,6,56,384]{3,2,1,0:T(8,128)S(1)} %get-tuple-element.42.outer, f32[18,3,56,128]{3,2,1,0:T(8,128)S(1)} %get-tuple-element.43.spread_ref), custom_call_target="tpu_custom_call" | custom-call | flops 10000000 | bytes 1000000 | tf_op jit(solution)/shard_map/pallas_call | solution.py:755
  54.5 2.8 %shard_map.83 = (f32[12,48,384]{2,1,0:T(8,128)}, f32[3,3,4,16,128]{4,3,2,1,0:T(8,128)}, f32[3]{0:T(128)}) custom-call(f32[8,128]{1,0:T(8,128)S(1)} %add_add_fusion.part, f32[3,12,56,384]{3,2,1,0:T(8,128)S(1)} %shard_map.81.summed, f32[3,3,4,16,128]{4,3,2,1,0:T(8,128)S(1)} %shard_map.82.residual, f32[3,3,16,128]{3,2,1,0:T(8,128)S(1)} %get-tuple-element.45.force, ...), custom_call_target="tpu_custom_call" | custom-call | flops 10000000 | bytes 1000000 | tf_op jit(solution)/shard_map/pallas_call | solution.py:755
  (4 shorter events, 0.0 us)
Async XLA Ops:
  2.0 8.2 %collective-permute-start.2 = (f32[136,384]{1,0:T(8,128)S(1)}, f32[136,384]{1,0:T(8,128)S(1)}, u32[]{:S(2)}, u32[]{:S(2)}) collective-permute-start(f32[136,384]{1,0:T(8,128)S(1)} %get-tuple-element.31), channel_id=1, source_target_pairs={{0,1},{2,3},{4,5},{6,7},{8,9},{10,11},{12,13},{14,15},{16,17},{18,... | collective-permute-start | bytes 626696 | tf_op jit(solution)/shard_map/ppermute | solution.py:804
  5.0 7.3 %collective-permute-start = (f32[4,48,384]{2,1,0:T(8,128)S(1)}, f32[4,48,384]{2,1,0:T(8,128)S(1)}, u32[]{:S(2)}, u32[]{:S(2)}) collective-permute-start(f32[4,48,384]{2,1,0:T(8,128)S(1)} %get-tuple-element.29), channel_id=1, source_target_pairs={{0,2},{1,3},{2,0},{3,1},{4,6},{5,7},{6,4},{7,5},{8,10},{9,11},{10,... | collective-permute-start | bytes 884744 | tf_op jit(solution)/shard_map/ppermute | solution.py:804
  5.0 7.3 %collective-permute-start.1 = (f32[3,48,384]{2,1,0:T(8,128)S(1)}, f32[3,48,384]{2,1,0:T(8,128)S(1)}, u32[]{:S(2)}, u32[]{:S(2)}) collective-permute-start(f32[3,48,384]{2,1,0:T(8,128)S(1)} %get-tuple-element.30), channel_id=1, source_target_pairs={{2,4},{3,5},{4,2},{5,3},{6,8},{7,9},{8,6},{9,7},{10,12},{11,13},{1... | collective-permute-start | bytes 663560 | tf_op jit(solution)/shard_map/ppermute | solution.py:804
  10.2 2.2 %collective-permute-start.3 = (f32[136,384]{1,0:T(8,128)S(1)}, f32[136,384]{1,0:T(8,128)S(1)}, u32[]{:S(2)}, u32[]{:S(2)}) collective-permute-start(f32[136,384]{1,0:T(8,128)S(1)} %collective-permute-done.2.side_b.side_a), channel_id=1, source_target_pairs={{0,2},{1,3},{2,0},{3,1},{4,6},{5,7},{6,4},{7,5},{8,10},{9,11},{10,... | collective-permute-start | bytes 626696 | tf_op jit(solution)/shard_map/ppermute | solution.py:804
  10.2 2.1 %collective-permute-start.4 = (f32[24,384]{1,0:T(8,128)S(1)}, f32[24,384]{1,0:T(8,128)S(1)}, u32[]{:S(2)}, u32[]{:S(2)}) collective-permute-start(f32[24,384]{1,0:T(8,128)S(1)} %get-tuple-element.32), channel_id=1, source_target_pairs={{2,5},{4,3},{6,9},{8,7},{10,13},{12,11},{14,17},{16,15},{18,21},{2... | collective-permute-start | bytes 110600 | tf_op jit(solution)/shard_map/ppermute | solution.py:804
  12.3 35.3 %copy-start = (s32[4,16,128]{2,1,0:T(8,128)S(1)}, s32[4,16,128]{2,1,0:T(8,128)}, u32[]{:S(2)}) copy-start(s32[4,16,128]{2,1,0:T(8,128)} %support.5) | copy-start | bytes 98308
  12.3 35.3 %copy-start.1 = (s32[4,16,128]{2,1,0:T(8,128)S(1)}, s32[4,16,128]{2,1,0:T(8,128)}, u32[]{:S(2)}) copy-start(s32[4,16,128]{2,1,0:T(8,128)} %loading.1) | copy-start | bytes 98308
  14.7 36.9 %collective-permute-start.12 = (f32[240,384]{1,0:T(8,128)S(1)}, f32[240,384]{1,0:T(8,128)S(1)}, u32[]{:S(2)}, u32[]{:S(2)}) collective-permute-start(f32[240,384]{1,0:T(8,128)S(1)} %get-tuple-element.40), channel_id=1, source_target_pairs={{0,2},{1,3},{2,0},{3,1},{4,6},{5,7},{6,4},{7,5},{8,10},{9,11},{10,... | collective-permute-start | bytes 1105928 | tf_op jit(solution)/shard_map/ppermute | solution.py:804
  19.2 32.3 %collective-permute-start.13 = (f32[240,384]{1,0:T(8,128)S(1)}, f32[240,384]{1,0:T(8,128)S(1)}, u32[]{:S(2)}, u32[]{:S(2)}) collective-permute-start(f32[240,384]{1,0:T(8,128)S(1)} %get-tuple-element.41), channel_id=1, source_target_pairs={{2,4},{3,5},{4,2},{5,3},{6,8},{7,9},{8,6},{9,7},{10,12},{11,13},{1... | collective-permute-start | bytes 1105928 | tf_op jit(solution)/shard_map/ppermute | solution.py:804
  19.9 0.7 %collective-permute-start.5 = (f32[48,384]{1,0:T(8,128)S(1)}, f32[48,384]{1,0:T(8,128)S(1)}, u32[]{:S(2)}, u32[]{:S(2)}) collective-permute-start(f32[48,384]{1,0:T(8,128)S(1)} %get-tuple-element.35), channel_id=1, source_target_pairs={{4,2},{5,3},{8,6},{9,7},{12,10},{13,11},{16,14},{17,15},{20,18},{2... | collective-permute-start | bytes 221192 | tf_op jit(solution)/shard_map/ppermute | solution.py:804
  23.1 3.6 %collective-permute-start.6 = (f32[8,128]{1,0:T(8,128)S(1)}, f32[8,128]{1,0:T(8,128)S(1)}, u32[]{:S(2)}, u32[]{:S(2)}) collective-permute-start(f32[8,128]{1,0:T(8,128)S(1)} %get-tuple-element.36), channel_id=1, source_target_pairs={{0,1},{1,0},{2,3},{3,2},{4,5},{5,4},{6,7},{7,6},{8,9},{9,8},{10,11... | collective-permute-start | bytes 12296 | tf_op jit(solution)/shard_map/ppermute | solution.py:773
  26.7 8.9 %collective-permute-start.7 = (f32[8,128]{1,0:T(8,128)S(1)}, f32[8,128]{1,0:T(8,128)S(1)}, u32[]{:S(2)}, u32[]{:S(2)}) collective-permute-start(f32[8,128]{1,0:T(8,128)S(1)} %add.18), channel_id=1, source_target_pairs={{0,2},{1,3},{2,0},{3,1},{4,6},{5,7},{6,4},{7,5},{8,10},{9,11},{10,... | collective-permute-start | bytes 12296 | tf_op jit(solution)/shard_map/ppermute | solution.py:773
  35.7 4.2 %collective-permute-start.8 = (f32[8,128]{1,0:T(8,128)S(1)}, f32[8,128]{1,0:T(8,128)S(1)}, u32[]{:S(2)}, u32[]{:S(2)}) collective-permute-start(f32[8,128]{1,0:T(8,128)S(1)} %add.19), channel_id=1, source_target_pairs={{0,4},{1,5},{2,6},{3,7},{4,0},{5,1},{6,2},{7,3},{8,12},{9,13},{10,... | collective-permute-start | bytes 12296 | tf_op jit(solution)/shard_map/ppermute | solution.py:773
  39.9 9.2 %collective-permute-start.11 = (f32[8,128]{1,0:T(8,128)S(1)}, f32[8,128]{1,0:T(8,128)S(1)}, u32[]{:S(2)}, u32[]{:S(2)}) collective-permute-start(f32[8,128]{1,0:T(8,128)S(1)} %add.20), channel_id=1, source_target_pairs={{0,24},{1,25},{2,26},{3,27},{4,28},{5,29},{6,30},{7,31},{8,16},{9,... | collective-permute-start | bytes 12296 | tf_op jit(solution)/shard_map/ppermute | solution.py:773
  47.0 4.5 %collective-permute-start.10 = (f32[8,128]{1,0:T(8,128)S(1)}, f32[8,128]{1,0:T(8,128)S(1)}, u32[]{:S(2)}, u32[]{:S(2)}) collective-permute-start(f32[8,128]{1,0:T(8,128)S(1)} %add.20), channel_id=1, source_target_pairs={{0,16},{1,17},{2,18},{3,19},{4,20},{5,21},{6,22},{7,23},{8,24},{9,... | collective-permute-start | bytes 12296 | tf_op jit(solution)/shard_map/ppermute | solution.py:773
  47.0 4.5 %collective-permute-start.9 = (f32[8,128]{1,0:T(8,128)S(1)}, f32[8,128]{1,0:T(8,128)S(1)}, u32[]{:S(2)}, u32[]{:S(2)}) collective-permute-start(f32[8,128]{1,0:T(8,128)S(1)} %add.20), channel_id=1, source_target_pairs={{0,8},{1,9},{2,10},{3,11},{4,12},{5,13},{6,14},{7,15},{8,0},{9,1},... | collective-permute-start | bytes 12296 | tf_op jit(solution)/shard_map/ppermute | solution.py:773

commit v4 on v3

--- a/solution.py
+++ b/solution.py
@@ -18,6 +18,7 @@
 poisson = 0.3
 LANES = 128
 REACH = 2 * RAD
+SCALE = 2.0**60
 
 
 def element_matrix():
@@ -595,7 +596,7 @@
     for r in range(3):
         base = r * coarse
         for x in range(cx):
-            packed[base + x + 1] = energy[r * cx + x]
+            packed[base + x + 1] = SCALE * energy[r * cx + x]
         span = slice(RAD * ext + r * padded, RAD * ext + (r + 1) * padded)
         for c in range(3):
             extra_ref[r, c, above] = near[span, groups[c]]
@@ -606,8 +607,8 @@
         below, beyond = (
             modes_of(lambda c, x: extra_ref[r, c, x], x, lane) for x in (0, 1)
         )
-        packed[base] = element_energy(below, first)
-        packed[base + cx + 1] = element_energy(last, beyond)
+        packed[base] = SCALE * element_energy(below, first)
+        packed[base + cx + 1] = SCALE * element_energy(last, beyond)
     split = halves(packed[...].reshape(3 * coarse * padded, LANES))
     for g in range(len(groups)):
         copies = (row_id == (g * LANES + col_id) // 3).astype(jnp.float32).astype(jnp.bfloat16)
@@ -660,7 +661,7 @@
                     force_ref[r, comp] = total[1 : cy + 1]
 
 
-def fields_kernel(gg, outer, spread_ref, summed_ref):
+def fields_kernel(gg, outer, spread_ref, summed_ref, rowwise):
     _, rows, ext, depth = gg.shape
     coarse = rows // 3 + 2
     groups = lane_groups(depth)
@@ -680,10 +681,19 @@
                             value = gg[r, 3 * (x - 1) + sub, place, lanes]
                         column.append(value * spread)
                 for k, value in enumerate(tent_rows(column)):
-                    summed_ref[r, k, place, lanes] = value
+                    rowwise[k, place, lanes] = value
             return carry
 
         lax.fori_loop(0, ext // 8, first_dim, 0)
+
+        def second_dim(x, carry):
+            for sub in range(3):
+                for lanes in groups:
+                    value = tent_sublanes(rowwise[3 * x + sub, :, lanes], summed_ref.shape[2])
+                    summed_ref[r, 3 * x + sub, :, lanes] = value
+            return carry
+
+        lax.fori_loop(0, rows // 3, second_dim, 0)
 
 
 def force_kernel(nodes_ref, moduli, support, loading, residual_ref):
@@ -705,7 +715,7 @@
     part, summed, residual, force, support, out_hbm, residual_hbm, compliance_ref, out_ref, row,
     sems,
 ):
-    rows, cols, depth = out_ref.shape
+    rows, _, depth = out_ref.shape
     groups = lane_groups(depth)
     free = 1.0 - support[0].astype(jnp.float32)
     for r in range(3):
@@ -720,7 +730,7 @@
     factors = []
     for r in range(3):
         factor = 3.0 * (1.0 - stiff_floor) / 27.0 * sharpness / DENOM[r] ** 3
-        factors.append(-factor / part[r : r + 1, :])
+        factors.append((-factor / SCALE) / part[r : r + 1, :])
     for step in range(rows // 3):
         for sub in range(3):
             k = 3 * step + sub
@@ -730,7 +740,7 @@
                 for r in range(3):
                     term = factors[r] * summed[r, k, :, lanes]
                     total = term if total is None else total + term
-                parts.append(tent_sublanes(total, cols))
+                parts.append(total)
             for lanes, value in zip(groups, tent_lanes(parts)):
                 out_ref[k, :, lanes] = value
         place = pl.ds(3 * step, 3)
@@ -875,7 +885,10 @@
         ],
         10000000, (energy, nodes, v_near, v_far),
     )
-    (fields,) = call(fields_kernel, [(3, rows, ext, depth)], [], 10000000, (gg, outer_rows, spread))
+    (fields,) = call(
+        fields_kernel, [(3, rows, cols, depth)], [(rows, ext, depth)], 10000000,
+        (gg, outer_rows, spread),
+    )
     summed = part
     for group in groups:
         summed = exchange_sum(summed, total, group)

time: 57.5 us -> 58.8 us (1.023)
  Pallas kernels: 14.8 us -> 16 us
    pallas_call x8, Pallas kernels: 14.8 us -> 16 us  [call(): pl.pallas_call(kernel, out_shape=[jax.ShapeDtypeStruct(s, jnp.float32) fo...]
  transfers between devices with their start and end apart: 14 -> 14, of which waited for: 5 -> 5; matrix products, arithmetic and copies ran while one was open for 0% -> 0% of each run, Pallas kernels for 10% -> 9%
where the time goes in v4:
time: 58.8 us; the launch traced here: 58.5 us
  starting transfers between devices  30.5 us (52%)
  Pallas kernels  16 us (27%)
  waiting for transfers between devices  11.2 us (19%)
  between operations  0.79 us (1%)
    ppermute x6, starting transfers between devices, exchange_sum(): lax.ppermute(value, axes, [(i, i ^ k) for i in range(total)])  20.2 us
    pallas_call x8, Pallas kernels, call(): pl.pallas_call(kernel, out_shape=[jax.ShapeDtypeStruct(s, jnp.float32) fo...  16 us
    ppermute x8, starting transfers between devices, send(): return lax.ppermute(block, axes, pairs)  10.3 us
    ppermute x6, waiting for transfers between devices, exchange_sum(): lax.ppermute(value, axes, [(i, i ^ k) for i in range(total)])  6.71 us
    ppermute x8, waiting for transfers between devices, send(): return lax.ppermute(block, axes, pairs)  4.51 us
  transfers between devices with their start and end apart: 14, of which 5 were waited for; matrix products, arithmetic and copies ran while one was open for 0% of the time, Pallas kernels for 9%

profile of v4, /device:TPU:0, one launch (start us, length us, event | category | flops | bytes accessed | tf_op | source)
XLA Modules:
  0.0 58.5 jit_solution(3052512630241517426)
XLA Ops:
  0.6 1.3 %shard_map.77 = (f32[4,48,384]{2,1,0:T(8,128)S(1)}, f32[3,48,384]{2,1,0:T(8,128)S(1)}, f32[48,384]{1,0:T(8,128)S(1)}, f32[3,3,4,24,128]{4,3,2,1,0:T(8,128)S(1)},...) custom-call(f32[12,48,384]{2,1,0:T(8,128)} %design.1, s32[12,48,384]{2,1,0:T(8,128)} %passive.1, ...), custom_call_target="tpu_custom_call" | custom-call | flops 200000 | bytes 1000000 | tf_op jit(solution)/shard_map/pallas_call | solution.py:765
  2.0 3.1 %collective-permute-start.2 = (f32[136,384]{1,0:T(8,128)S(1)}, f32[136,384]{1,0:T(8,128)S(1)}, u32[]{:S(2)}, u32[]{:S(2)}) collective-permute-start(f32[136,384]{1,0:T(8,128)S(1)} %get-tuple-element.31), channel_id=1, source_target_pairs={{0,1},{2,3},{4,5},{6,7},{8,9},{10,11},{12,13},{14,15},{16,17},{18,... | collective-permute-start | bytes 626696 | tf_op jit(solution)/shard_map/ppermute | solution.py:814
  5.0 0.0 collective-permute-start
  5.0 0.7 %collective-permute-start.1 = (f32[3,48,384]{2,1,0:T(8,128)S(1)}, f32[3,48,384]{2,1,0:T(8,128)S(1)}, u32[]{:S(2)}, u32[]{:S(2)}) collective-permute-start(f32[3,48,384]{2,1,0:T(8,128)S(1)} %get-tuple-element.30), channel_id=1, source_target_pairs={{2,4},{3,5},{4,2},{5,3},{6,8},{7,9},{8,6},{9,7},{10,12},{11,13},{1... | collective-permute-start | bytes 663560 | tf_op jit(solution)/shard_map/ppermute | solution.py:814
  5.7 4.5 %collective-permute-done.2.side_b.side_a = f32[136,384]{1,0:T(8,128)S(1)} collective-permute-done((f32[136,384]{1,0:T(8,128)S(1)}, f32[136,384]{1,0:T(8,128)S(1)}, u32[]{:S(2)}, u32[]{:S(2)}) %collective-permute-start.2) | collective-permute-done | bytes 208928 | tf_op jit(solution)/shard_map/ppermute | solution.py:814
  10.2 0.0 collective-permute-start.3
  10.2 0.7 %collective-permute-start.4 = (f32[24,384]{1,0:T(8,128)S(1)}, f32[24,384]{1,0:T(8,128)S(1)}, u32[]{:S(2)}, u32[]{:S(2)}) collective-permute-start(f32[24,384]{1,0:T(8,128)S(1)} %get-tuple-element.32), channel_id=1, source_target_pairs={{2,5},{4,3},{6,9},{8,7},{10,13},{12,11},{14,17},{16,15},{18,21},{2... | collective-permute-start | bytes 110600 | tf_op jit(solution)/shard_map/ppermute | solution.py:814
  10.8 1.5 %shard_map.76 = (f32[12,48,384]{2,1,0:T(8,128)S(1)}, f32[12,56,384]{2,1,0:T(8,128)S(1)}) custom-call(f32[12,48,384]{2,1,0:T(8,128)} %design.1, s32[12,48,384]{2,1,0:T(8,128)} %passive.1), custom_call_target="tpu_custom_call" | custom-call | flops 200000 | bytes 1000000 | tf_op jit(solution)/shard_map/pallas_call | solution.py:765
  12.3 0.0 collective-permute-done.4.far_b.far_a
  12.3 0.0 collective-permute-done.1.far
  12.3 0.0 collective-permute-done.near
  12.3 0.0 collective-permute-done.3.near_b.near_a
  12.3 0.0 copy-start
  12.4 0.0 copy-start.1
  12.4 2.3 %shard_map.78 = (f32[12,56,384]{2,1,0:T(8,128)S(1)}, f32[3,3,4,24,128]{4,3,2,1,0:T(8,128)S(1)}, f32[240,384]{1,0:T(8,128)S(1)}, f32[240,384]{1,0:T(8,128)S(1)}) custom-call(f32[12,48,384]{2,1,0:T(8,128)S(1)} %get-tuple-element.26.design, f32[12,56,384]{2,1,0:T(8,128)S(1)} %get-tuple-element.27.mask_in, f32[3,3,4,24,128]{4,3,2,1,0:T(8,128)S(1)} %get-tuple-element.28.nodes_in, ...), custom_call_target="tpu_custom_call" | custom-call | flops 10000000 | bytes 1000000 | tf_op jit(solution)/shard_map/pallas_call | solution.py:765
  14.7 4.6 %collective-permute-start.12 = (f32[240,384]{1,0:T(8,128)S(1)}, f32[240,384]{1,0:T(8,128)S(1)}, u32[]{:S(2)}, u32[]{:S(2)}) collective-permute-start(f32[240,384]{1,0:T(8,128)S(1)} %get-tuple-element.40), channel_id=1, source_target_pairs={{0,2},{1,3},{2,0},{3,1},{4,6},{5,7},{6,4},{7,5},{8,10},{9,11},{10,... | collective-permute-start | bytes 1105928 | tf_op jit(solution)/shard_map/ppermute | solution.py:814
  19.3 0.7 %collective-permute-start.13 = (f32[240,384]{1,0:T(8,128)S(1)}, f32[240,384]{1,0:T(8,128)S(1)}, u32[]{:S(2)}, u32[]{:S(2)}) collective-permute-start(f32[240,384]{1,0:T(8,128)S(1)} %get-tuple-element.41), channel_id=1, source_target_pairs={{2,4},{3,5},{4,2},{5,3},{6,8},{7,9},{8,6},{9,7},{10,12},{11,13},{1... | collective-permute-start | bytes 1105928 | tf_op jit(solution)/shard_map/ppermute | solution.py:814
  19.9 0.7 %collective-permute-start.5 = (f32[48,384]{1,0:T(8,128)S(1)}, f32[48,384]{1,0:T(8,128)S(1)}, u32[]{:S(2)}, u32[]{:S(2)}) collective-permute-start(f32[48,384]{1,0:T(8,128)S(1)} %get-tuple-element.35), channel_id=1, source_target_pairs={{4,2},{5,3},{8,6},{9,7},{12,10},{13,11},{16,14},{17,15},{20,18},{2... | collective-permute-start | bytes 221192 | tf_op jit(solution)/shard_map/ppermute | solution.py:814
  20.6 0.0 collective-permute-done.5.row
  20.6 2.5 %shard_map.79 = (f32[3,12,56,384]{3,2,1,0:T(8,128)S(1)}, f32[12,24,128]{2,1,0:T(8,128)S(1)}, f32[8,128]{1,0:T(8,128)S(1)}, f32[3,3,5,24,128]{4,3,2,1,0:T(8,128)S(1)}, f32[12,24,128]{2,1,0:T(8,128)S(1)}) custom-call(f32[12,56,384]{2,1,0:T(8,128)S(1)} %get-tuple-element.33.v_ref, f32[3,3,4,24,128]{4,3,2,1,0:T(8,128)S(1)} %get-tuple-element.34.nodes_in, ...), custom_call_target="tpu_custom_call" | custom-call | flops 10000000 | bytes 1000000 | tf_op jit(solution)/shard_map/pallas_call | solution.py:765
  23.1 1.7 %collective-permute-start.6 = (f32[8,128]{1,0:T(8,128)S(1)}, f32[8,128]{1,0:T(8,128)S(1)}, u32[]{:S(2)}, u32[]{:S(2)}) collective-permute-start(f32[8,128]{1,0:T(8,128)S(1)} %get-tuple-element.36), channel_id=1, source_target_pairs={{0,1},{1,0},{2,3},{3,2},{4,5},{5,4},{6,7},{7,6},{8,9},{9,8},{10,11... | collective-permute-start | bytes 12296 | tf_op jit(solution)/shard_map/ppermute | solution.py:783
  24.9 1.9 %collective-permute-done.6 = f32[8,128]{1,0:T(8,128)S(1)} collective-permute-done((f32[8,128]{1,0:T(8,128)S(1)}, f32[8,128]{1,0:T(8,128)S(1)}, u32[]{:S(2)}, u32[]{:S(2)}) %collective-permute-start.6) | collective-permute-done | bytes 4128 | tf_op jit(solution)/shard_map/ppermute | solution.py:783
  26.8 8.1 %collective-permute-start.7 = (f32[8,128]{1,0:T(8,128)S(1)}, f32[8,128]{1,0:T(8,128)S(1)}, u32[]{:S(2)}, u32[]{:S(2)}) collective-permute-start(f32[8,128]{1,0:T(8,128)S(1)} %add.18), channel_id=1, source_target_pairs={{0,2},{1,3},{2,0},{3,1},{4,6},{5,7},{6,4},{7,5},{8,10},{9,11},{10,... | collective-permute-start | bytes 12296 | tf_op jit(solution)/shard_map/ppermute | solution.py:783
  34.8 0.8 %collective-permute-done.7 = f32[8,128]{1,0:T(8,128)S(1)} collective-permute-done((f32[8,128]{1,0:T(8,128)S(1)}, f32[8,128]{1,0:T(8,128)S(1)}, u32[]{:S(2)}, u32[]{:S(2)}) %collective-permute-start.7) | collective-permute-done | bytes 4128 | tf_op jit(solution)/shard_map/ppermute | solution.py:783
  35.7 2.6 %collective-permute-start.8 = (f32[8,128]{1,0:T(8,128)S(1)}, f32[8,128]{1,0:T(8,128)S(1)}, u32[]{:S(2)}, u32[]{:S(2)}) collective-permute-start(f32[8,128]{1,0:T(8,128)S(1)} %add.19), channel_id=1, source_target_pairs={{0,4},{1,5},{2,6},{3,7},{4,0},{5,1},{6,2},{7,3},{8,12},{9,13},{10,... | collective-permute-start | bytes 12296 | tf_op jit(solution)/shard_map/ppermute | solution.py:783
  38.3 1.6 %collective-permute-done.8 = f32[8,128]{1,0:T(8,128)S(1)} collective-permute-done((f32[8,128]{1,0:T(8,128)S(1)}, f32[8,128]{1,0:T(8,128)S(1)}, u32[]{:S(2)}, u32[]{:S(2)}) %collective-permute-start.8) | collective-permute-done | bytes 4128 | tf_op jit(solution)/shard_map/ppermute | solution.py:783
  39.9 7.2 %collective-permute-start.11 = (f32[8,128]{1,0:T(8,128)S(1)}, f32[8,128]{1,0:T(8,128)S(1)}, u32[]{:S(2)}, u32[]{:S(2)}) collective-permute-start(f32[8,128]{1,0:T(8,128)S(1)} %add.20), channel_id=1, source_target_pairs={{0,24},{1,25},{2,26},{3,27},{4,28},{5,29},{6,30},{7,31},{8,16},{9,... | collective-permute-start | bytes 12296 | tf_op jit(solution)/shard_map/ppermute | solution.py:783
  47.1 0.0 collective-permute-start.10
  47.1 0.6 collective-permute-start.9
  47.6 0.0 copy-done
  47.6 0.0 copy-done.1
  47.6 1.5 %shard_map.82.residual = f32[3,3,4,16,128]{4,3,2,1,0:T(8,128)S(1)} custom-call(f32[3,3,5,24,128]{4,3,2,1,0:T(8,128)S(1)} %get-tuple-element.39.nodes_ref, f32[12,24,128]{2,1,0:T(8,128)S(1)} %get-tuple-element.44.moduli, s32[4,16,128]{2,1,0:T(8,128)S(1)} %copy-done, s32[4,16,128]{2,1,0:T(8,128)S(1)} %copy-done.1), custom_call_target="tpu_custom_call" | custom-call | flops 10000000 | bytes 1000000 | tf_op jit(solution)/shard_map/pallas_call | solution.py:765
  49.1 0.0 collective-permute-done.11
  49.1 2.4 %collective-permute-done.10 = f32[8,128]{1,0:T(8,128)S(1)} collective-permute-done((f32[8,128]{1,0:T(8,128)S(1)}, f32[8,128]{1,0:T(8,128)S(1)}, u32[]{:S(2)}, u32[]{:S(2)}) %collective-permute-start.10) | collective-permute-done | bytes 4128 | tf_op jit(solution)/shard_map/ppermute | solution.py:783
  51.6 0.0 collective-permute-done.9
  51.6 0.0 collective-permute-done.12.near
  51.6 0.0 collective-permute-done.13.far
  51.6 2.1 %shard_map.80 = (f32[3,6,56,384]{3,2,1,0:T(8,128)S(1)}, f32[18,3,56,128]{3,2,1,0:T(8,128)S(1)}, f32[3,3,16,128]{3,2,1,0:T(8,128)S(1)}) custom-call(f32[12,24,128]{2,1,0:T(8,128)S(1)} %get-tuple-element.38.energy, f32[3,3,5,24,128]{4,3,2,1,0:T(8,128)S(1)} %get-tuple-element.39.nodes_ref, f32[240,384]{1,0:T(8,128)S(1)} %collective-permute-done.12.near, ...), custom_call_target="tpu_custom_call" | custom-call | flops 10000000 | bytes 1000000 | tf_op jit(solution)/shard_map/pallas_call | solution.py:765
  53.7 2.0 %shard_map.81.summed = f32[3,12,48,384]{3,2,1,0:T(8,128)S(1)} custom-call(f32[3,12,56,384]{3,2,1,0:T(8,128)S(1)} %get-tuple-element.37.gg, f32[3,6,56,384]{3,2,1,0:T(8,128)S(1)} %get-tuple-element.42.outer, f32[18,3,56,128]{3,2,1,0:T(8,128)S(1)} %get-tuple-element.43.spread_ref), custom_call_target="tpu_custom_call" | custom-call | flops 10000000 | bytes 1000000 | tf_op jit(solution)/shard_map/pallas_call | solution.py:765
  55.8 2.7 %shard_map.83 = (f32[12,48,384]{2,1,0:T(8,128)}, f32[3,3,4,16,128]{4,3,2,1,0:T(8,128)}, f32[3]{0:T(128)}) custom-call(f32[8,128]{1,0:T(8,128)S(1)} %add_add_fusion.part, f32[3,12,48,384]{3,2,1,0:T(8,128)S(1)} %shard_map.81.summed, f32[3,3,4,16,128]{4,3,2,1,0:T(8,128)S(1)} %shard_map.82.residual, f32[3,3,16,128]{3,2,1,0:T(8,128)S(1)} %get-tuple-element.45.force, ...), custom_call_target="tpu_custom_call" | custom-call | flops 10000000 | bytes 1000000 | tf_op jit(solution)/shard_map/pallas_call | solution.py:765
  (4 shorter events, 0.0 us)
Async XLA Ops:
  2.0 8.2 %collective-permute-start.2 = (f32[136,384]{1,0:T(8,128)S(1)}, f32[136,384]{1,0:T(8,128)S(1)}, u32[]{:S(2)}, u32[]{:S(2)}) collective-permute-start(f32[136,384]{1,0:T(8,128)S(1)} %get-tuple-element.31), channel_id=1, source_target_pairs={{0,1},{2,3},{4,5},{6,7},{8,9},{10,11},{12,13},{14,15},{16,17},{18,... | collective-permute-start | bytes 626696 | tf_op jit(solution)/shard_map/ppermute | solution.py:814
  5.0 7.3 %collective-permute-start = (f32[4,48,384]{2,1,0:T(8,128)S(1)}, f32[4,48,384]{2,1,0:T(8,128)S(1)}, u32[]{:S(2)}, u32[]{:S(2)}) collective-permute-start(f32[4,48,384]{2,1,0:T(8,128)S(1)} %get-tuple-element.29), channel_id=1, source_target_pairs={{0,2},{1,3},{2,0},{3,1},{4,6},{5,7},{6,4},{7,5},{8,10},{9,11},{10,... | collective-permute-start | bytes 884744 | tf_op jit(solution)/shard_map/ppermute | solution.py:814
  5.0 7.3 %collective-permute-start.1 = (f32[3,48,384]{2,1,0:T(8,128)S(1)}, f32[3,48,384]{2,1,0:T(8,128)S(1)}, u32[]{:S(2)}, u32[]{:S(2)}) collective-permute-start(f32[3,48,384]{2,1,0:T(8,128)S(1)} %get-tuple-element.30), channel_id=1, source_target_pairs={{2,4},{3,5},{4,2},{5,3},{6,8},{7,9},{8,6},{9,7},{10,12},{11,13},{1... | collective-permute-start | bytes 663560 | tf_op jit(solution)/shard_map/ppermute | solution.py:814
  10.2 2.2 %collective-permute-start.3 = (f32[136,384]{1,0:T(8,128)S(1)}, f32[136,384]{1,0:T(8,128)S(1)}, u32[]{:S(2)}, u32[]{:S(2)}) collective-permute-start(f32[136,384]{1,0:T(8,128)S(1)} %collective-permute-done.2.side_b.side_a), channel_id=1, source_target_pairs={{0,2},{1,3},{2,0},{3,1},{4,6},{5,7},{6,4},{7,5},{8,10},{9,11},{10,... | collective-permute-start | bytes 626696 | tf_op jit(solution)/shard_map/ppermute | solution.py:814
  10.2 2.1 %collective-permute-start.4 = (f32[24,384]{1,0:T(8,128)S(1)}, f32[24,384]{1,0:T(8,128)S(1)}, u32[]{:S(2)}, u32[]{:S(2)}) collective-permute-start(f32[24,384]{1,0:T(8,128)S(1)} %get-tuple-element.32), channel_id=1, source_target_pairs={{2,5},{4,3},{6,9},{8,7},{10,13},{12,11},{14,17},{16,15},{18,21},{2... | collective-permute-start | bytes 110600 | tf_op jit(solution)/shard_map/ppermute | solution.py:814
  12.3 35.3 %copy-start = (s32[4,16,128]{2,1,0:T(8,128)S(1)}, s32[4,16,128]{2,1,0:T(8,128)}, u32[]{:S(2)}) copy-start(s32[4,16,128]{2,1,0:T(8,128)} %support.5) | copy-start | bytes 98308
  12.4 35.3 %copy-start.1 = (s32[4,16,128]{2,1,0:T(8,128)S(1)}, s32[4,16,128]{2,1,0:T(8,128)}, u32[]{:S(2)}) copy-start(s32[4,16,128]{2,1,0:T(8,128)} %loading.1) | copy-start | bytes 98308
  14.7 36.9 %collective-permute-start.12 = (f32[240,384]{1,0:T(8,128)S(1)}, f32[240,384]{1,0:T(8,128)S(1)}, u32[]{:S(2)}, u32[]{:S(2)}) collective-permute-start(f32[240,384]{1,0:T(8,128)S(1)} %get-tuple-element.40), channel_id=1, source_target_pairs={{0,2},{1,3},{2,0},{3,1},{4,6},{5,7},{6,4},{7,5},{8,10},{9,11},{10,... | collective-permute-start | bytes 1105928 | tf_op jit(solution)/shard_map/ppermute | solution.py:814
  19.3 32.3 %collective-permute-start.13 = (f32[240,384]{1,0:T(8,128)S(1)}, f32[240,384]{1,0:T(8,128)S(1)}, u32[]{:S(2)}, u32[]{:S(2)}) collective-permute-start(f32[240,384]{1,0:T(8,128)S(1)} %get-tuple-element.41), channel_id=1, source_target_pairs={{2,4},{3,5},{4,2},{5,3},{6,8},{7,9},{8,6},{9,7},{10,12},{11,13},{1... | collective-permute-start | bytes 1105928 | tf_op jit(solution)/shard_map/ppermute | solution.py:814
  19.9 0.7 %collective-permute-start.5 = (f32[48,384]{1,0:T(8,128)S(1)}, f32[48,384]{1,0:T(8,128)S(1)}, u32[]{:S(2)}, u32[]{:S(2)}) collective-permute-start(f32[48,384]{1,0:T(8,128)S(1)} %get-tuple-element.35), channel_id=1, source_target_pairs={{4,2},{5,3},{8,6},{9,7},{12,10},{13,11},{16,14},{17,15},{20,18},{2... | collective-permute-start | bytes 221192 | tf_op jit(solution)/shard_map/ppermute | solution.py:814
  23.1 3.6 %collective-permute-start.6 = (f32[8,128]{1,0:T(8,128)S(1)}, f32[8,128]{1,0:T(8,128)S(1)}, u32[]{:S(2)}, u32[]{:S(2)}) collective-permute-start(f32[8,128]{1,0:T(8,128)S(1)} %get-tuple-element.36), channel_id=1, source_target_pairs={{0,1},{1,0},{2,3},{3,2},{4,5},{5,4},{6,7},{7,6},{8,9},{9,8},{10,11... | collective-permute-start | bytes 12296 | tf_op jit(solution)/shard_map/ppermute | solution.py:783
  26.8 8.9 %collective-permute-start.7 = (f32[8,128]{1,0:T(8,128)S(1)}, f32[8,128]{1,0:T(8,128)S(1)}, u32[]{:S(2)}, u32[]{:S(2)}) collective-permute-start(f32[8,128]{1,0:T(8,128)S(1)} %add.18), channel_id=1, source_target_pairs={{0,2},{1,3},{2,0},{3,1},{4,6},{5,7},{6,4},{7,5},{8,10},{9,11},{10,... | collective-permute-start | bytes 12296 | tf_op jit(solution)/shard_map/ppermute | solution.py:783
  35.7 4.2 %collective-permute-start.8 = (f32[8,128]{1,0:T(8,128)S(1)}, f32[8,128]{1,0:T(8,128)S(1)}, u32[]{:S(2)}, u32[]{:S(2)}) collective-permute-start(f32[8,128]{1,0:T(8,128)S(1)} %add.19), channel_id=1, source_target_pairs={{0,4},{1,5},{2,6},{3,7},{4,0},{5,1},{6,2},{7,3},{8,12},{9,13},{10,... | collective-permute-start | bytes 12296 | tf_op jit(solution)/shard_map/ppermute | solution.py:783
  39.9 9.2 %collective-permute-start.11 = (f32[8,128]{1,0:T(8,128)S(1)}, f32[8,128]{1,0:T(8,128)S(1)}, u32[]{:S(2)}, u32[]{:S(2)}) collective-permute-start(f32[8,128]{1,0:T(8,128)S(1)} %add.20), channel_id=1, source_target_pairs={{0,24},{1,25},{2,26},{3,27},{4,28},{5,29},{6,30},{7,31},{8,16},{9,... | collective-permute-start | bytes 12296 | tf_op jit(solution)/shard_map/ppermute | solution.py:783
  47.1 4.5 %collective-permute-start.10 = (f32[8,128]{1,0:T(8,128)S(1)}, f32[8,128]{1,0:T(8,128)S(1)}, u32[]{:S(2)}, u32[]{:S(2)}) collective-permute-start(f32[8,128]{1,0:T(8,128)S(1)} %add.20), channel_id=1, source_target_pairs={{0,16},{1,17},{2,18},{3,19},{4,20},{5,21},{6,22},{7,23},{8,24},{9,... | collective-permute-start | bytes 12296 | tf_op jit(solution)/shard_map/ppermute | solution.py:783
  47.1 4.5 %collective-permute-start.9 = (f32[8,128]{1,0:T(8,128)S(1)}, f32[8,128]{1,0:T(8,128)S(1)}, u32[]{:S(2)}, u32[]{:S(2)}) collective-permute-start(f32[8,128]{1,0:T(8,128)S(1)} %add.20), channel_id=1, source_target_pairs={{0,8},{1,9},{2,10},{3,11},{4,12},{5,13},{6,14},{7,15},{8,0},{9,1},... | collective-permute-start | bytes 12296 | tf_op jit(solution)/shard_map/ppermute | solution.py:783
